TPU v7x, 128 devices: a whole 4x4x4 slice. The times are simulated.
128 devices in a mesh: gx: 16 (over z, x), gy: 8 (over y, core).
Axes of the slice: x: 4, y: 4, z: 4, core: 2. Of those that a mesh axis runs over, the one named last changes fastest.
Arguments:
- displacement_old: float32 [3, 128, 128, 256], P(None, 'gx', 'gy'), may hold values from -6 to 6
- pressure_old: float32 [128, 128, 256], P('gx', 'gy'), may hold values from -6 to 6
- body_force: float32 [3, 128, 128, 256], P(None, 'gx', 'gy'), may hold values from -400 to 400
- fluid_source: float32 [128, 128, 256], P('gx', 'gy'), may hold values from -400 to 400
- material_ids: int32 [128, 128, 256], P('gx', 'gy'), may hold values from 0 to 7
- materials: float32 [5, 8], replicated, may hold values from 0.5 to 4
Outputs:
- displacement: float32 [3, 128, 128, 256], P(None, 'gx', 'gy')
- pressure: float32 [128, 128, 256], P('gx', 'gy')
All inputs are finite; a program needn't handle non-finite values.
Results may differ from a plain program's by a relative error of at most 0.00017.
Values sent between devices are 32-bit elements; how exact they have to be, the bound alone decides.
No kernel may reach another device: no remote copies, remote signals or barrier semaphores. Data moves between devices by JAX's collectives and lax.ppermute only.
A program may use at most 64 MiB of HBM per device.

v0:
```python
import functools

import jax
import jax.numpy as jnp
from jax import lax
from jax.sharding import Mesh
from jax.sharding import PartitionSpec as P

OUTER = 2
INNER = 3
GX_GY = ("gx_0", "gx_1", "gy_0", "gy_1")
GX = ("gx_0", "gx_1")
GY = ("gy_0", "gy_1")


step_time = 4.0


def by_axis(shard, axes):
    return functools.reduce(lax.psum, axes, shard)


def extended(shard, sides, width):
    for axis, dim in sides:
        size, length = (lax.axis_size(axis), shard.shape[dim])
        up = [(i, (i + 1) % size) for i in range(size - 1)]
        down = [(j, i) for i, j in up]
        last = lax.slice_in_dim(shard, length - width, length, axis=dim)
        first = lax.slice_in_dim(shard, 0, width, axis=dim)
        before = lax.ppermute(last, axis, up)
        after = lax.ppermute(first, axis, down)
        shard = jnp.concatenate([before, shard, after], axis=dim)
    return shard


def with_halo(shard, sides, width):
    edges = {}
    for axis, dim in sides:
        size, length = (lax.axis_size(axis), shard.shape[dim])
        up = [(i, (i + 1) % size) for i in range(size - 1)]
        last = lax.slice_in_dim(shard, length - width, length, axis=dim)
        first = lax.slice_in_dim(shard, 0, width, axis=dim)
        edges[dim] = (
            lax.ppermute(last, axis, up),
            lax.ppermute(first, axis, [(b, a) for a, b in up]),
        )
    done = []
    for _, dim in sides:
        low, high = edges[dim]
        around = [(width, width) if d in done else (0, 0) for d in range(shard.ndim)]
        shard = jnp.concatenate([jnp.pad(low, around), shard, jnp.pad(high, around)], axis=dim)
        done.append(dim)
    return shard


def from_behind(shard, axis, by):
    length = lax.axis_size(axis)
    pairs = [(i, i + by) for i in range(length) if 0 <= i + by < length]
    return lax.ppermute(shard, axis, pairs)


def above_depth(values):
    return jnp.concatenate([values[..., 1:], jnp.zeros_like(values[..., :1])], axis=-1)


def below_depth(values):
    return jnp.concatenate([jnp.zeros_like(values[..., :1]), values[..., :-1]], axis=-1)


def harmonic(first_value, second_value):
    return 2.0 * first_value * second_value / (first_value + second_value)


def lookup(code_plus, materials, table_rows):
    collected = [jnp.zeros(code_plus.shape, jnp.float32) for table_row in table_rows]
    for material in range(materials.shape[1]):
        matched = code_plus == material + 1
        collected = [
            jnp.where(matched, materials[table_row, material], current)
            for table_row, current in zip(table_rows, collected)
        ]
    return collected


def run_solver(operate, precond, rhs_vec, initial):
    solution = initial
    residual = rhs_vec - operate(initial)
    direction = initial
    image_dir = initial
    gamma_last = None
    length_last = None
    for inner_step in range(INNER):
        smoothed = precond(residual)
        image_vec = operate(smoothed)
        gamma_now, delta_now = (
            by_axis(jnp.sum(residual * smoothed), GX_GY),
            by_axis(jnp.sum(smoothed * image_vec), GX_GY),
        )
        if inner_step == 0:
            step_length = gamma_now / delta_now
            direction = smoothed
            image_dir = image_vec
        else:
            ratio_now = gamma_now / gamma_last
            step_length = gamma_now / (delta_now - ratio_now * gamma_now / length_last)
            direction = smoothed + ratio_now * direction
            image_dir = image_vec + ratio_now * image_dir
        solution = solution + step_length * direction
        if inner_step + 1 < INNER:
            residual = residual - step_length * image_dir
        gamma_last = gamma_now
        length_last = step_length
    return solution


def on_device(displacement_old, pressure_old, body_force, fluid_source, material_ids, materials):
    code_plus = material_ids + 1
    widened_codes = extended(code_plus, ((GX, 0), (GY, 1)), 1)
    lame_wide, shear_wide, perm_wide = lookup(widened_codes, materials, (0, 1, 2))
    storage, biot_raw = lookup(code_plus, materials, (3, 4))
    biot_coef = 0.25 * biot_raw
    lame_first = lame_wide[1:-1, 1:-1]
    shear_mod = shear_wide[1:-1, 1:-1]
    permeability = perm_wide[1:-1, 1:-1]
    stiff_up = [
        0.5 * (shear_mod + shear_wide[2:, 1:-1]),
        0.5 * (shear_mod + shear_wide[1:-1, 2:]),
        0.5 * (shear_mod + above_depth(shear_mod)),
    ]
    stiff_down = [
        0.5 * (shear_mod + shear_wide[:-2, 1:-1]),
        0.5 * (shear_mod + shear_wide[1:-1, :-2]),
        0.5 * (shear_mod + below_depth(shear_mod)),
    ]
    flow_up = [
        harmonic(permeability, perm_wide[2:, 1:-1]),
        harmonic(permeability, perm_wide[1:-1, 2:]),
        harmonic(permeability, above_depth(permeability)),
    ]
    flow_down = [
        harmonic(permeability, perm_wide[:-2, 1:-1]),
        harmonic(permeability, perm_wide[1:-1, :-2]),
        harmonic(permeability, below_depth(permeability)),
    ]
    stab = biot_coef * biot_coef / (lame_first + 2.0 / 3.0 * shear_mod)
    storage_total = storage + stab
    flow_sum = flow_up[0] + flow_down[0] + flow_up[1] + flow_down[1] + flow_up[2] + flow_down[2]
    inv_pressure = 1.0 / (storage_total + step_time * flow_sum)
    stiff_sum = (
        stiff_up[0] + stiff_down[0] + stiff_up[1] + stiff_down[1] + stiff_up[2] + stiff_down[2]
    )
    lame_below = [lame_wide[:-2, 1:-1], lame_wide[1:-1, :-2], below_depth(lame_first)]
    inv_blocks = 1.0 / jnp.stack([stiff_sum + lame_below[spatial] for spatial in range(3)])
    factor = lame_first / (1.0 + lame_first * (inv_blocks[0] + inv_blocks[1] + inv_blocks[2]))

    def apply_pressure(field):
        widened = with_halo(field, ((GX, 0), (GY, 1)), 1)
        centre = widened[1:-1, 1:-1]
        upward = [widened[2:, 1:-1], widened[1:-1, 2:], above_depth(centre)]
        downward = [widened[:-2, 1:-1], widened[1:-1, :-2], below_depth(centre)]
        flux = jnp.zeros_like(centre)
        for spatial in range(3):
            flux = (
                flux
                + flow_up[spatial] * (centre - upward[spatial])
                + flow_down[spatial] * (centre - downward[spatial])
            )
        return storage_total * centre + step_time * flux

    def shear_part(widened):
        centre = widened[:, 1:-1, 1:-1]
        upward = [widened[:, 2:, 1:-1], widened[:, 1:-1, 2:], above_depth(centre)]
        downward = [widened[:, :-2, 1:-1], widened[:, 1:-1, :-2], below_depth(centre)]
        summed = jnp.zeros_like(centre)
        for spatial in range(3):
            summed = (
                summed
                + stiff_up[spatial] * (centre - upward[spatial])
                + stiff_down[spatial] * (centre - downward[spatial])
            )
        return (centre, summed)

    def apply_mech(field):
        widened = extended(field, ((GX, 1), (GY, 2)), 1)
        centre, summed = shear_part(widened)
        spread = (
            widened[0, 1:, :-1]
            - widened[0, :-1, :-1]
            + widened[1, :-1, 1:]
            - widened[1, :-1, :-1]
            + above_depth(widened[2, :-1, :-1])
            - widened[2, :-1, :-1]
        )
        weighted_wide = lame_wide[:-1, :-1] * spread
        weighted = weighted_wide[1:, 1:]
        below_x = weighted_wide[:-1, 1:]
        below_y = weighted_wide[1:, :-1]
        lame_pull = jnp.stack(
            [below_x - weighted, below_y - weighted, below_depth(weighted) - weighted]
        )
        return summed + lame_pull

    def solve_pressure(residual):
        return residual * inv_pressure

    def solve_blocks(residual):
        scaled = residual * inv_blocks
        summed = scaled[0] + scaled[1] + scaled[2]
        return scaled - inv_blocks * (factor * summed)

    pressure = pressure_old
    displacement = displacement_old
    for repeat in range(OUTER):
        change = displacement - displacement_old
        after_x = from_behind(change[0, :1], GX, -1)
        after_y = from_behind(change[1, :, :1], GY, -1)
        spread = (
            jnp.concatenate([change[0, 1:], after_x], axis=0)
            - change[0]
            + jnp.concatenate([change[1][:, 1:], after_y], axis=1)
            - change[1]
            + above_depth(change[2])
            - change[2]
        )
        rhs_pressure = (
            storage * pressure_old + step_time * fluid_source - biot_coef * spread + stab * pressure
        )
        pressure = run_solver(apply_pressure, solve_pressure, rhs_pressure, pressure)
        loaded = biot_coef * pressure
        before_x = from_behind(loaded[-1:], GX, 1)
        before_y = from_behind(loaded[:, -1:], GY, 1)
        pressure_push = jnp.stack(
            [
                jnp.concatenate([before_x, loaded[:-1]], axis=0) - loaded,
                jnp.concatenate([before_y, loaded[:, :-1]], axis=1) - loaded,
                below_depth(loaded) - loaded,
            ]
        )
        rhs_mech = body_force + pressure_push
        displacement = run_solver(apply_mech, solve_blocks, rhs_mech, displacement)
    return (displacement, pressure)


def solution(mesh):
    finer = Mesh(mesh.devices.reshape(4, 4, 4, 2), ("gx_0", "gx_1", "gy_0", "gy_1"))
    return jax.shard_map(
        on_device,
        mesh=finer,
        in_specs=(
            P(None, GX, GY, None),
            P(GX, GY, None),
            P(None, GX, GY, None),
            P(GX, GY, None),
            P(GX, GY, None),
            P(),
        ),
        out_specs=(P(None, GX, GY, None), P(GX, GY, None)),
        check_vma=False,
    )
```

profile of v0, /device:TPU:1, one launch (start us, length us, event | category | flops | bytes accessed | tf_op | source)
XLA Modules:
  0.0 776.3 jit_solution(9839679696418723052)
XLA Ops:
  62.2 11.5 %fusion.368 = (f32[8,16,256]{2,1,0:T(8,128)S(1)}, f32[8,16,256]{2,1,0:T(8,128)S(1)}, f32[8,16,256]{2,1,0:T(8,128)S(1)}, f32[8,16,256]{2,1,0:T(8,128)S(1)}, f32[8...) fusion(f32[8,16,256]{2,1,0:T(8,128)S(1)} %copy-done.6, ...), kind=kLoop, calls=%fused_computation.673 | loop fusion | flops 3112960 | bytes 4535872 | tf_op jit(solution)/shard_map/mul | solution.py:204
  88.9 15.3 %all-reduce.108 = (f32[]{:T(128)}, f32[]{:T(128)}) all-reduce(f32[]{:T(128)} %get-tuple-element.21, f32[]{:T(128)} %get-tuple-element.20), channel_id=1, replica_groups=mesh['gx_0'=4,'gx_1'=4,'gy_0'=4,'gy_1'=2] {'gx_0'}, use_global_device_ids=true, to_apply=%region_1.2 | all-reduce | flops 2 | bytes 16 | tf_op jit(solution)/shard_map/psum | solution.py:20
  104.2 7.6 all-reduce.96
  111.7 8.0 %all-reduce.84 = (f32[]{:T(128)}, f32[]{:T(128)}) all-reduce(f32[]{:T(128)} %get-tuple-element.68, f32[]{:T(128)} %get-tuple-element.69), channel_id=1, replica_groups=mesh['gx_0'=4,'gx_1'=4,'gy_0'=4,'gy_1'=2] {'gy_0'}, use_global_device_ids=true, to_apply=%region_3.4 | all-reduce | flops 2 | bytes 16 | tf_op jit(solution)/shard_map/psum | solution.py:20
  119.7 10.6 %all-reduce.120 = (f32[]{:T(128)}, f32[]{:T(128)}) all-reduce(f32[]{:T(128)} %get-tuple-element.44, f32[]{:T(128)} %get-tuple-element.45), channel_id=1, replica_groups=mesh['gx_0'=4,'gx_1'=4,'gy_0'=4,'gy_1'=2] {'gy_1'}, use_global_device_ids=true, to_apply=%region_4.5 | all-reduce | flops 2 | bytes 16 | tf_op jit(solution)/shard_map/psum | solution.py:20
  151.8 9.2 %all-reduce.95 = (f32[]{:T(128)}, f32[]{:T(128)}) all-reduce(f32[]{:T(128)} %get-tuple-element.90, f32[]{:T(128)} %get-tuple-element.91), channel_id=1, replica_groups=mesh['gx_0'=4,'gx_1'=4,'gy_0'=4,'gy_1'=2] {'gx_1'}, use_global_device_ids=true, to_apply=%region_12.13 | all-reduce | flops 2 | bytes 16 | tf_op jit(solution)/shard_map/psum | solution.py:20
  167.7 10.7 %all-reduce.119 = (f32[]{:T(128)}, f32[]{:T(128)}) all-reduce(f32[]{:T(128)} %get-tuple-element.42, f32[]{:T(128)} %get-tuple-element.43), channel_id=1, replica_groups=mesh['gx_0'=4,'gx_1'=4,'gy_0'=4,'gy_1'=2] {'gy_1'}, use_global_device_ids=true, to_apply=%region_14.15 | all-reduce | flops 2 | bytes 16 | tf_op jit(solution)/shard_map/psum | solution.py:20
  196.7 8.4 %all-reduce.106 = (f32[]{:T(128)}, f32[]{:T(128)}) all-reduce(f32[]{:T(128)} %get-tuple-element.144, f32[]{:T(128)} %fusion.341), channel_id=1, replica_groups=mesh['gx_0'=4,'gx_1'=4,'gy_0'=4,'gy_1'=2] {'gx_0'}, use_global_device_ids=true, to_apply=%region_21.22 | all-reduce | flops 2 | bytes 16 | tf_op jit(solution)/shard_map/psum | solution.py:20
  205.2 8.2 %all-reduce.94 = (f32[]{:T(128)}, f32[]{:T(128)}) all-reduce(f32[]{:T(128)} %get-tuple-element.88, f32[]{:T(128)} %get-tuple-element.89), channel_id=1, replica_groups=mesh['gx_0'=4,'gx_1'=4,'gy_0'=4,'gy_1'=2] {'gx_1'}, use_global_device_ids=true, to_apply=%region_22.23 | all-reduce | flops 2 | bytes 16 | tf_op jit(solution)/shard_map/psum | solution.py:20
  220.0 11.2 %all-reduce.118 = (f32[]{:T(128)}, f32[]{:T(128)}) all-reduce(f32[]{:T(128)} %get-tuple-element.40, f32[]{:T(128)} %get-tuple-element.41), channel_id=1, replica_groups=mesh['gx_0'=4,'gx_1'=4,'gy_0'=4,'gy_1'=2] {'gy_1'}, use_global_device_ids=true, to_apply=%region_24.25 | all-reduce | flops 2 | bytes 16 | tf_op jit(solution)/shard_map/psum | solution.py:20
  260.0 14.2 %all-reduce.105 = (f32[]{:T(128)}, f32[]{:T(128)}) all-reduce(f32[]{:T(128)} %get-tuple-element.13, f32[]{:T(128)} %get-tuple-element.12), channel_id=1, replica_groups=mesh['gx_0'=4,'gx_1'=4,'gy_0'=4,'gy_1'=2] {'gx_0'}, use_global_device_ids=true, to_apply=%region_31.32 | all-reduce | flops 2 | bytes 16 | tf_op jit(solution)/shard_map/psum | solution.py:20
  287.9 10.3 %all-reduce.117 = (f32[]{:T(128)}, f32[]{:T(128)}) all-reduce(f32[]{:T(128)} %get-tuple-element.38, f32[]{:T(128)} %get-tuple-element.39), channel_id=1, replica_groups=mesh['gx_0'=4,'gx_1'=4,'gy_0'=4,'gy_1'=2] {'gy_1'}, use_global_device_ids=true, to_apply=%region_34.35 | all-reduce | flops 2 | bytes 16 | tf_op jit(solution)/shard_map/psum | solution.py:20
  318.6 11.6 %all-reduce.104 = (f32[]{:T(128)}, f32[]{:T(128)}) all-reduce(f32[]{:T(128)} %get-tuple-element.11, f32[]{:T(128)} %get-tuple-element.10), channel_id=1, replica_groups=mesh['gx_0'=4,'gx_1'=4,'gy_0'=4,'gy_1'=2] {'gx_0'}, use_global_device_ids=true, to_apply=%region_41.42 | all-reduce | flops 2 | bytes 16 | tf_op jit(solution)/shard_map/psum | solution.py:20
  343.7 10.7 %all-reduce.116 = (f32[]{:T(128)}, f32[]{:T(128)}) all-reduce(f32[]{:T(128)} %get-tuple-element.36, f32[]{:T(128)} %get-tuple-element.37), channel_id=1, replica_groups=mesh['gx_0'=4,'gx_1'=4,'gy_0'=4,'gy_1'=2] {'gy_1'}, use_global_device_ids=true, to_apply=%region_44.45 | all-reduce | flops 2 | bytes 16 | tf_op jit(solution)/shard_map/psum | solution.py:20
  386.1 10.0 %all-reduce.103 = (f32[]{:T(128)}, f32[]{:T(128)}) all-reduce(f32[]{:T(128)} %get-tuple-element.9, f32[]{:T(128)} %get-tuple-element.8), channel_id=1, replica_groups=mesh['gx_0'=4,'gx_1'=4,'gy_0'=4,'gy_1'=2] {'gx_0'}, use_global_device_ids=true, to_apply=%region_51.52 | all-reduce | flops 2 | bytes 16 | tf_op jit(solution)/shard_map/psum | solution.py:20
  396.0 9.5 %all-reduce.91 = (f32[]{:T(128)}, f32[]{:T(128)}) all-reduce(f32[]{:T(128)} %get-tuple-element.82, f32[]{:T(128)} %get-tuple-element.83), channel_id=1, replica_groups=mesh['gx_0'=4,'gx_1'=4,'gy_0'=4,'gy_1'=2] {'gx_1'}, use_global_device_ids=true, to_apply=%region_52.53 | all-reduce | flops 2 | bytes 16 | tf_op jit(solution)/shard_map/psum | solution.py:20
  412.3 9.7 %all-reduce.115 = (f32[]{:T(128)}, f32[]{:T(128)}) all-reduce(f32[]{:T(128)} %get-tuple-element.34, f32[]{:T(128)} %get-tuple-element.35), channel_id=1, replica_groups=mesh['gx_0'=4,'gx_1'=4,'gy_0'=4,'gy_1'=2] {'gy_1'}, use_global_device_ids=true, to_apply=%region_54.55 | all-reduce | flops 2 | bytes 16 | tf_op jit(solution)/shard_map/psum | solution.py:20
  449.7 8.9 %all-reduce.102 = (f32[]{:T(128)}, f32[]{:T(128)}) all-reduce(f32[]{:T(128)} %get-tuple-element.17, f32[]{:T(128)} %get-tuple-element.16), channel_id=1, replica_groups=mesh['gx_0'=4,'gx_1'=4,'gy_0'=4,'gy_1'=2] {'gx_0'}, use_global_device_ids=true, to_apply=%region_61.62 | all-reduce | flops 2 | bytes 16 | tf_op jit(solution)/shard_map/psum | solution.py:20
  458.5 9.5 %all-reduce.90 = (f32[]{:T(128)}, f32[]{:T(128)}) all-reduce(f32[]{:T(128)} %get-tuple-element.80, f32[]{:T(128)} %get-tuple-element.81), channel_id=1, replica_groups=mesh['gx_0'=4,'gx_1'=4,'gy_0'=4,'gy_1'=2] {'gx_1'}, use_global_device_ids=true, to_apply=%region_62.63 | all-reduce | flops 2 | bytes 16 | tf_op jit(solution)/shard_map/psum | solution.py:20
  468.0 7.6 all-reduce.78
  475.7 10.5 %all-reduce.114 = (f32[]{:T(128)}, f32[]{:T(128)}) all-reduce(f32[]{:T(128)} %get-tuple-element.32, f32[]{:T(128)} %get-tuple-element.33), channel_id=1, replica_groups=mesh['gx_0'=4,'gx_1'=4,'gy_0'=4,'gy_1'=2] {'gy_1'}, use_global_device_ids=true, to_apply=%region_64.65 | all-reduce | flops 2 | bytes 16 | tf_op jit(solution)/shard_map/psum | solution.py:20
  509.3 8.6 %all-reduce.89 = (f32[]{:T(128)}, f32[]{:T(128)}) all-reduce(f32[]{:T(128)} %get-tuple-element.78, f32[]{:T(128)} %get-tuple-element.79), channel_id=1, replica_groups=mesh['gx_0'=4,'gx_1'=4,'gy_0'=4,'gy_1'=2] {'gx_1'}, use_global_device_ids=true, to_apply=%region_72.73 | all-reduce | flops 2 | bytes 16 | tf_op jit(solution)/shard_map/psum | solution.py:20
  524.9 9.0 %all-reduce.113 = (f32[]{:T(128)}, f32[]{:T(128)}) all-reduce(f32[]{:T(128)} %get-tuple-element.30, f32[]{:T(128)} %get-tuple-element.31), channel_id=1, replica_groups=mesh['gx_0'=4,'gx_1'=4,'gy_0'=4,'gy_1'=2] {'gy_1'}, use_global_device_ids=true, to_apply=%region_74.75 | all-reduce | flops 2 | bytes 16 | tf_op jit(solution)/shard_map/psum | solution.py:20
  558.9 7.9 %all-reduce.100 = (f32[]{:T(128)}, f32[]{:T(128)}) all-reduce(f32[]{:T(128)} %get-tuple-element.126, f32[]{:T(128)} %fusion.342), channel_id=1, replica_groups=mesh['gx_0'=4,'gx_1'=4,'gy_0'=4,'gy_1'=2] {'gx_0'}, use_global_device_ids=true, to_apply=%region_81.82 | all-reduce | flops 2 | bytes 16 | tf_op jit(solution)/shard_map/psum | solution.py:20
  566.8 8.5 %all-reduce.88 = (f32[]{:T(128)}, f32[]{:T(128)}) all-reduce(f32[]{:T(128)} %get-tuple-element.76, f32[]{:T(128)} %get-tuple-element.77), channel_id=1, replica_groups=mesh['gx_0'=4,'gx_1'=4,'gy_0'=4,'gy_1'=2] {'gx_1'}, use_global_device_ids=true, to_apply=%region_82.83 | all-reduce | flops 2 | bytes 16 | tf_op jit(solution)/shard_map/psum | solution.py:20
  582.6 8.1 %all-reduce.112 = (f32[]{:T(128)}, f32[]{:T(128)}) all-reduce(f32[]{:T(128)} %get-tuple-element.28, f32[]{:T(128)} %get-tuple-element.29), channel_id=1, replica_groups=mesh['gx_0'=4,'gx_1'=4,'gy_0'=4,'gy_1'=2] {'gy_1'}, use_global_device_ids=true, to_apply=%region_84.85 | all-reduce | flops 2 | bytes 16 | tf_op jit(solution)/shard_map/psum | solution.py:20
  620.5 13.9 %all-reduce.99 = (f32[]{:T(128)}, f32[]{:T(128)}) all-reduce(f32[]{:T(128)} %get-tuple-element.7, f32[]{:T(128)} %get-tuple-element.6), channel_id=1, replica_groups=mesh['gx_0'=4,'gx_1'=4,'gy_0'=4,'gy_1'=2] {'gx_0'}, use_global_device_ids=true, to_apply=%region_91.92 | all-reduce | flops 2 | bytes 16 | tf_op jit(solution)/shard_map/psum | solution.py:20
  647.8 10.9 %all-reduce.111 = (f32[]{:T(128)}, f32[]{:T(128)}) all-reduce(f32[]{:T(128)} %get-tuple-element.26, f32[]{:T(128)} %get-tuple-element.27), channel_id=1, replica_groups=mesh['gx_0'=4,'gx_1'=4,'gy_0'=4,'gy_1'=2] {'gy_1'}, use_global_device_ids=true, to_apply=%region_94.95 | all-reduce | flops 2 | bytes 16 | tf_op jit(solution)/shard_map/psum | solution.py:20
  676.9 11.7 %all-reduce.98 = (f32[]{:T(128)}, f32[]{:T(128)}) all-reduce(f32[]{:T(128)} %get-tuple-element.5, f32[]{:T(128)} %get-tuple-element.4), channel_id=1, replica_groups=mesh['gx_0'=4,'gx_1'=4,'gy_0'=4,'gy_1'=2] {'gx_0'}, use_global_device_ids=true, to_apply=%region_101.102 | all-reduce | flops 2 | bytes 16 | tf_op jit(solution)/shard_map/psum | solution.py:20
  701.9 10.8 %all-reduce.110 = (f32[]{:T(128)}, f32[]{:T(128)}) all-reduce(f32[]{:T(128)} %get-tuple-element.24, f32[]{:T(128)} %get-tuple-element.25), channel_id=1, replica_groups=mesh['gx_0'=4,'gx_1'=4,'gy_0'=4,'gy_1'=2] {'gy_1'}, use_global_device_ids=true, to_apply=%region_104.105 | all-reduce | flops 2 | bytes 16 | tf_op jit(solution)/shard_map/psum | solution.py:20
  734.3 11.9 %all-reduce.97 = (f32[]{:T(128)}, f32[]{:T(128)}) all-reduce(f32[]{:T(128)} %get-tuple-element.3, f32[]{:T(128)} %get-tuple-element.2), channel_id=1, replica_groups=mesh['gx_0'=4,'gx_1'=4,'gy_0'=4,'gy_1'=2] {'gx_0'}, use_global_device_ids=true, to_apply=%region_111.112 | all-reduce | flops 2 | bytes 16 | tf_op jit(solution)/shard_map/psum | solution.py:20
  759.5 10.8 %all-reduce.109 = (f32[]{:T(128)}, f32[]{:T(128)}) all-reduce(f32[]{:T(128)} %get-tuple-element.22, f32[]{:T(128)} %get-tuple-element.23), channel_id=1, replica_groups=mesh['gx_0'=4,'gx_1'=4,'gy_0'=4,'gy_1'=2] {'gy_1'}, use_global_device_ids=true, to_apply=%region_114.115 | all-reduce | flops 2 | bytes 16 | tf_op jit(solution)/shard_map/psum | solution.py:20
  (451 shorter events, 409.4 us)
Async XLA Ops:
  1.6 18.8 %collective-permute-start.2 = (s32[1,16,256]{2,1,0:T(8,128)S(1)}, s32[1,16,256]{2,1,0:T(8,128)S(1)}, u32[]{:S(2)}, u32[]{:S(2)}) collective-permute-start(s32[1,16,256]{2,1,0:T(8,128)S(1)} %get-tuple-element.339), channel_id=1, source_target_pairs={{0,8},{8,16},{16,24},{24,32},{32,40},{40,48},{48,56},{56,64},{64,7... | collective-permute-start | bytes 49160 | tf_op jit(solution)/shard_map/ppermute | solution.py:30
  5.7 18.5 %collective-permute-start.3 = (s32[1,16,256]{2,1,0:T(8,128)S(1)}, s32[1,16,256]{2,1,0:T(8,128)S(1)}, u32[]{:S(2)}, u32[]{:S(2)}) collective-permute-start(s32[1,16,256]{2,1,0:T(8,128)S(1)} %get-tuple-element.340), channel_id=1, source_target_pairs={{8,0},{16,8},{24,16},{32,24},{40,32},{48,40},{56,48},{64,56},{72,6... | collective-permute-start | bytes 49160 | tf_op jit(solution)/shard_map/ppermute | solution.py:31
  7.9 43.7 %collective-permute-start.25 = (f32[3,1,16,256]{3,2,1,0:T(8,128)S(1)}, f32[3,1,16,256]{3,2,1,0:T(8,128)S(1)}, u32[]{:S(2)}, u32[]{:S(2)}) collective-permute-start(f32[3,1,16,256]{3,2,1,0:T(8,128)S(1)} %get-tuple-element.244), channel_id=1, source_target_pairs={{0,8},{8,16},{16,24},{24,32},{32,40},{40,48},{48,56},{56,64},{64,7... | collective-permute-start | bytes 147464 | tf_op jit(solution)/shard_map/ppermute | solution.py:30
  11.9 15.3 %collective-permute-start.7 = (f32[1,16,256]{2,1,0:T(8,128)S(1)}, f32[1,16,256]{2,1,0:T(8,128)S(1)}, u32[]{:S(2)}, u32[]{:S(2)}) collective-permute-start(f32[1,16,256]{2,1,0:T(8,128)S(1)} %get-tuple-element.334), channel_id=1, source_target_pairs={{0,8},{8,16},{16,24},{24,32},{32,40},{40,48},{48,56},{56,64},{64,7... | collective-permute-start | bytes 49160 | tf_op jit(solution)/shard_map/ppermute | solution.py:44
  15.1 14.6 %collective-permute-start.6 = (f32[1,16,256]{2,1,0:T(8,128)S(1)}, f32[1,16,256]{2,1,0:T(8,128)S(1)}, u32[]{:S(2)}, u32[]{:S(2)}) collective-permute-start(f32[1,16,256]{2,1,0:T(8,128)S(1)} %get-tuple-element.333), channel_id=1, source_target_pairs={{8,0},{16,8},{24,16},{32,24},{40,32},{48,40},{56,48},{64,56},{72,6... | collective-permute-start | bytes 49160 | tf_op jit(solution)/shard_map/ppermute | solution.py:45
  20.4 39.8 %collective-permute-start.8 = (f32[8,1,256]{2,1,0:T(1,128)S(1)}, f32[8,1,256]{2,1,0:T(1,128)S(1)}, u32[]{:S(2)}, u32[]{:S(2)}) collective-permute-start(f32[8,1,256]{2,1,0:T(1,128)S(1)} %get-tuple-element.331), channel_id=1, source_target_pairs={{1,0},{2,1},{3,2},{4,3},{5,4},{6,5},{7,6},{9,8},{10,9},{11,10},{12... | collective-permute-start | bytes 24584 | tf_op jit(solution)/shard_map/ppermute | solution.py:45
  24.1 38.0 %collective-permute-start.9 = (f32[8,1,256]{2,1,0:T(1,128)S(1)}, f32[8,1,256]{2,1,0:T(1,128)S(1)}, u32[]{:S(2)}, u32[]{:S(2)}) collective-permute-start(f32[8,1,256]{2,1,0:T(1,128)S(1)} %get-tuple-element.332), channel_id=1, source_target_pairs={{0,1},{1,2},{2,3},{3,4},{4,5},{5,6},{6,7},{8,9},{9,10},{10,11},{11... | collective-permute-start | bytes 24584 | tf_op jit(solution)/shard_map/ppermute | solution.py:44
  31.7 23.9 %collective-permute-start.24 = (f32[3,1,16,256]{3,2,1,0:T(8,128)S(1)}, f32[3,1,16,256]{3,2,1,0:T(8,128)S(1)}, u32[]{:S(2)}, u32[]{:S(2)}) collective-permute-start(f32[3,1,16,256]{3,2,1,0:T(8,128)S(1)} %get-tuple-element.243), channel_id=1, source_target_pairs={{8,0},{16,8},{24,16},{32,24},{40,32},{48,40},{56,48},{64,56},{72,6... | collective-permute-start | bytes 147464 | tf_op jit(solution)/shard_map/ppermute | solution.py:31
  56.4 26.2 %collective-permute-start.27 = (f32[3,10,1,256]{3,2,1,0:T(1,128)S(1)}, f32[3,10,1,256]{3,2,1,0:T(1,128)S(1)}, u32[]{:S(2)}, u32[]{:S(2)}) collective-permute-start(f32[3,10,1,256]{3,2,1,0:T(1,128)S(1)} %get-tuple-element.208), channel_id=1, source_target_pairs={{0,1},{1,2},{2,3},{3,4},{4,5},{5,6},{6,7},{8,9},{9,10},{10,11},{11... | collective-permute-start | bytes 92168 | tf_op jit(solution)/shard_map/ppermute | solution.py:30
  60.2 26.5 %collective-permute-start.26 = (f32[3,10,1,256]{3,2,1,0:T(1,128)S(1)}, f32[3,10,1,256]{3,2,1,0:T(1,128)S(1)}, u32[]{:S(2)}, u32[]{:S(2)}) collective-permute-start(f32[3,10,1,256]{3,2,1,0:T(1,128)S(1)} %get-tuple-element.207), channel_id=1, source_target_pairs={{1,0},{2,1},{3,2},{4,3},{5,4},{6,5},{7,6},{9,8},{10,9},{11,10},{12... | collective-permute-start | bytes 92168 | tf_op jit(solution)/shard_map/ppermute | solution.py:31
  73.8 14.2 %collective-permute-start.10 = (f32[1,16,256]{2,1,0:T(8,128)S(1)}, f32[1,16,256]{2,1,0:T(8,128)S(1)}, u32[]{:S(2)}, u32[]{:S(2)}) collective-permute-start(f32[1,16,256]{2,1,0:T(8,128)S(1)} %get-tuple-element.320), channel_id=1, source_target_pairs={{8,0},{16,8},{24,16},{32,24},{40,32},{48,40},{56,48},{64,56},{72,6... | collective-permute-start | bytes 49160 | tf_op jit(solution)/shard_map/ppermute | solution.py:45
  75.1 12.9 %collective-permute-start.11 = (f32[1,16,256]{2,1,0:T(8,128)S(1)}, f32[1,16,256]{2,1,0:T(8,128)S(1)}, u32[]{:S(2)}, u32[]{:S(2)}) collective-permute-start(f32[1,16,256]{2,1,0:T(8,128)S(1)} %get-tuple-element.319), channel_id=1, source_target_pairs={{0,8},{8,16},{16,24},{24,32},{32,40},{40,48},{48,56},{56,64},{64,7... | collective-permute-start | bytes 49160 | tf_op jit(solution)/shard_map/ppermute | solution.py:44
  131.7 11.6 %collective-permute-start.14 = (f32[1,16,256]{2,1,0:T(8,128)S(1)}, f32[1,16,256]{2,1,0:T(8,128)S(1)}, u32[]{:S(2)}, u32[]{:S(2)}) collective-permute-start(f32[1,16,256]{2,1,0:T(8,128)S(1)} %get-tuple-element.314), channel_id=1, source_target_pairs={{8,0},{16,8},{24,16},{32,24},{40,32},{48,40},{56,48},{64,56},{72,6... | collective-permute-start | bytes 49160 | tf_op jit(solution)/shard_map/ppermute | solution.py:45
  133.0 10.4 %collective-permute-start.15 = (f32[1,16,256]{2,1,0:T(8,128)S(1)}, f32[1,16,256]{2,1,0:T(8,128)S(1)}, u32[]{:S(2)}, u32[]{:S(2)}) collective-permute-start(f32[1,16,256]{2,1,0:T(8,128)S(1)} %get-tuple-element.313), channel_id=1, source_target_pairs={{0,8},{8,16},{16,24},{24,32},{32,40},{40,48},{48,56},{56,64},{64,7... | collective-permute-start | bytes 49160 | tf_op jit(solution)/shard_map/ppermute | solution.py:44
  184.3 11.6 %collective-permute-start.18 = (f32[1,16,256]{2,1,0:T(8,128)S(1)}, f32[1,16,256]{2,1,0:T(8,128)S(1)}, u32[]{:S(2)}, u32[]{:S(2)}) collective-permute-start(f32[1,16,256]{2,1,0:T(8,128)S(1)} %get-tuple-element.308), channel_id=1, source_target_pairs={{8,0},{16,8},{24,16},{32,24},{40,32},{48,40},{56,48},{64,56},{72,6... | collective-permute-start | bytes 49160 | tf_op jit(solution)/shard_map/ppermute | solution.py:45
  185.6 10.4 %collective-permute-start.19 = (f32[1,16,256]{2,1,0:T(8,128)S(1)}, f32[1,16,256]{2,1,0:T(8,128)S(1)}, u32[]{:S(2)}, u32[]{:S(2)}) collective-permute-start(f32[1,16,256]{2,1,0:T(8,128)S(1)} %get-tuple-element.307), channel_id=1, source_target_pairs={{0,8},{8,16},{16,24},{24,32},{32,40},{40,48},{48,56},{56,64},{64,7... | collective-permute-start | bytes 49160 | tf_op jit(solution)/shard_map/ppermute | solution.py:44
  361.3 15.3 %collective-permute-start.36 = (f32[3,1,16,256]{3,2,1,0:T(8,128)S(1)}, f32[3,1,16,256]{3,2,1,0:T(8,128)S(1)}, u32[]{:S(2)}, u32[]{:S(2)}) collective-permute-start(f32[3,1,16,256]{3,2,1,0:T(8,128)S(1)} %get-tuple-element.230), channel_id=1, source_target_pairs={{8,0},{16,8},{24,16},{32,24},{40,32},{48,40},{56,48},{64,56},{72,6... | collective-permute-start | bytes 147464 | tf_op jit(solution)/shard_map/ppermute | solution.py:31
  362.6 14.0 %collective-permute-start.37 = (f32[3,1,16,256]{3,2,1,0:T(8,128)S(1)}, f32[3,1,16,256]{3,2,1,0:T(8,128)S(1)}, u32[]{:S(2)}, u32[]{:S(2)}) collective-permute-start(f32[3,1,16,256]{3,2,1,0:T(8,128)S(1)} %get-tuple-element.229), channel_id=1, source_target_pairs={{0,8},{8,16},{16,24},{24,32},{32,40},{40,48},{48,56},{56,64},{64,7... | collective-permute-start | bytes 147464 | tf_op jit(solution)/shard_map/ppermute | solution.py:30
  368.2 66.2 %collective-permute-start.42 = (f32[1,16,256]{2,1,0:T(8,128)}, f32[1,16,256]{2,1,0:T(8,128)S(1)}, u32[]{:S(2)}, u32[]{:S(2)}) collective-permute-start(f32[1,16,256]{2,1,0:T(8,128)} %get-tuple-element.299), channel_id=1, source_target_pairs={{8,0},{16,8},{24,16},{32,24},{40,32},{48,40},{56,48},{64,56},{72,6... | collective-permute-start | bytes 49160 | tf_op jit(solution)/shard_map/ppermute | solution.py:45
  369.5 64.9 %collective-permute-start.43 = (f32[1,16,256]{2,1,0:T(8,128)}, f32[1,16,256]{2,1,0:T(8,128)S(1)}, u32[]{:S(2)}, u32[]{:S(2)}) collective-permute-start(f32[1,16,256]{2,1,0:T(8,128)} %get-tuple-element.298), channel_id=1, source_target_pairs={{0,8},{8,16},{16,24},{24,32},{32,40},{40,48},{48,56},{56,64},{64,7... | collective-permute-start | bytes 49160 | tf_op jit(solution)/shard_map/ppermute | solution.py:44
  373.5 56.4 %collective-permute-start.44 = (f32[8,1,256]{2,1,0:T(1,128)}, f32[8,1,256]{2,1,0:T(1,128)}, u32[]{:S(2)}, u32[]{:S(2)}) collective-permute-start(f32[8,1,256]{2,1,0:T(1,128)} %get-tuple-element.296), channel_id=1, source_target_pairs={{1,0},{2,1},{3,2},{4,3},{5,4},{6,5},{7,6},{9,8},{10,9},{11,10},{12... | collective-permute-start | bytes 24584 | tf_op jit(solution)/shard_map/ppermute | solution.py:45
  382.5 50.5 %collective-permute-start.45 = (f32[8,1,256]{2,1,0:T(1,128)}, f32[8,1,256]{2,1,0:T(1,128)}, u32[]{:S(2)}, u32[]{:S(2)}) collective-permute-start(f32[8,1,256]{2,1,0:T(1,128)} %get-tuple-element.297), channel_id=1, source_target_pairs={{0,1},{1,2},{2,3},{3,4},{4,5},{5,6},{6,7},{8,9},{9,10},{10,11},{11... | collective-permute-start | bytes 24584 | tf_op jit(solution)/shard_map/ppermute | solution.py:44
  433.0 115.3 %collective-permute-start.60 = (f32[3,1,16,256]{3,2,1,0:T(8,128)}, f32[3,1,16,256]{3,2,1,0:T(8,128)}, u32[]{:S(2)}, u32[]{:S(2)}) collective-permute-start(f32[3,1,16,256]{3,2,1,0:T(8,128)} %get-tuple-element.226), channel_id=1, source_target_pairs={{8,0},{16,8},{24,16},{32,24},{40,32},{48,40},{56,48},{64,56},{72,6... | collective-permute-start | bytes 147464 | tf_op jit(solution)/shard_map/ppermute | solution.py:31
  436.1 12.8 %collective-permute-start.46 = (f32[1,16,256]{2,1,0:T(8,128)S(1)}, f32[1,16,256]{2,1,0:T(8,128)S(1)}, u32[]{:S(2)}, u32[]{:S(2)}) collective-permute-start(f32[1,16,256]{2,1,0:T(8,128)S(1)} %get-tuple-element.293), channel_id=1, source_target_pairs={{8,0},{16,8},{24,16},{32,24},{40,32},{48,40},{56,48},{64,56},{72,6... | collective-permute-start | bytes 49160 | tf_op jit(solution)/shard_map/ppermute | solution.py:45
  437.4 11.5 %collective-permute-start.47 = (f32[1,16,256]{2,1,0:T(8,128)S(1)}, f32[1,16,256]{2,1,0:T(8,128)S(1)}, u32[]{:S(2)}, u32[]{:S(2)}) collective-permute-start(f32[1,16,256]{2,1,0:T(8,128)S(1)} %get-tuple-element.292), channel_id=1, source_target_pairs={{0,8},{8,16},{16,24},{24,32},{32,40},{40,48},{48,56},{56,64},{64,7... | collective-permute-start | bytes 49160 | tf_op jit(solution)/shard_map/ppermute | solution.py:44
  487.4 13.5 %collective-permute-start.50 = (f32[1,16,256]{2,1,0:T(8,128)S(1)}, f32[1,16,256]{2,1,0:T(8,128)S(1)}, u32[]{:S(2)}, u32[]{:S(2)}) collective-permute-start(f32[1,16,256]{2,1,0:T(8,128)S(1)} %get-tuple-element.287), channel_id=1, source_target_pairs={{8,0},{16,8},{24,16},{32,24},{40,32},{48,40},{56,48},{64,56},{72,6... | collective-permute-start | bytes 49160 | tf_op jit(solution)/shard_map/ppermute | solution.py:45
  488.7 12.2 %collective-permute-start.51 = (f32[1,16,256]{2,1,0:T(8,128)S(1)}, f32[1,16,256]{2,1,0:T(8,128)S(1)}, u32[]{:S(2)}, u32[]{:S(2)}) collective-permute-start(f32[1,16,256]{2,1,0:T(8,128)S(1)} %get-tuple-element.286), channel_id=1, source_target_pairs={{0,8},{8,16},{16,24},{24,32},{32,40},{40,48},{48,56},{56,64},{64,7... | collective-permute-start | bytes 49160 | tf_op jit(solution)/shard_map/ppermute | solution.py:44
  498.4 52.6 %collective-permute-start.61 = (f32[3,1,16,256]{3,2,1,0:T(8,128)}, f32[3,1,16,256]{3,2,1,0:T(8,128)}, u32[]{:S(2)}, u32[]{:S(2)}) collective-permute-start(f32[3,1,16,256]{3,2,1,0:T(8,128)} %get-tuple-element.225), channel_id=1, source_target_pairs={{0,8},{8,16},{16,24},{24,32},{32,40},{40,48},{48,56},{56,64},{64,7... | collective-permute-start | bytes 147464 | tf_op jit(solution)/shard_map/ppermute | solution.py:30
  540.1 17.9 %collective-permute-start.54 = (f32[1,16,256]{2,1,0:T(8,128)S(1)}, f32[1,16,256]{2,1,0:T(8,128)S(1)}, u32[]{:S(2)}, u32[]{:S(2)}) collective-permute-start(f32[1,16,256]{2,1,0:T(8,128)S(1)} %get-tuple-element.281), channel_id=1, source_target_pairs={{8,0},{16,8},{24,16},{32,24},{40,32},{48,40},{56,48},{64,56},{72,6... | collective-permute-start | bytes 49160 | tf_op jit(solution)/shard_map/ppermute | solution.py:45
  541.4 16.7 %collective-permute-start.55 = (f32[1,16,256]{2,1,0:T(8,128)S(1)}, f32[1,16,256]{2,1,0:T(8,128)S(1)}, u32[]{:S(2)}, u32[]{:S(2)}) collective-permute-start(f32[1,16,256]{2,1,0:T(8,128)S(1)} %get-tuple-element.280), channel_id=1, source_target_pairs={{0,8},{8,16},{16,24},{24,32},{32,40},{40,48},{48,56},{56,64},{64,7... | collective-permute-start | bytes 49160 | tf_op jit(solution)/shard_map/ppermute | solution.py:44
  552.5 47.5 %collective-permute-start.62 = (f32[3,10,1,256]{3,2,1,0:T(1,128)}, f32[3,10,1,256]{3,2,1,0:T(1,128)S(1)}, u32[]{:S(2)}, u32[]{:S(2)}) collective-permute-start(f32[3,10,1,256]{3,2,1,0:T(1,128)} %get-tuple-element.193), channel_id=1, source_target_pairs={{1,0},{2,1},{3,2},{4,3},{5,4},{6,5},{7,6},{9,8},{10,9},{11,10},{12... | collective-permute-start | bytes 92168 | tf_op jit(solution)/shard_map/ppermute | solution.py:31
  554.4 45.6 %collective-permute-start.63 = (f32[3,10,1,256]{3,2,1,0:T(1,128)}, f32[3,10,1,256]{3,2,1,0:T(1,128)}, u32[]{:S(2)}, u32[]{:S(2)}) collective-permute-start(f32[3,10,1,256]{3,2,1,0:T(1,128)} %get-tuple-element.194), channel_id=1, source_target_pairs={{0,1},{1,2},{2,3},{3,4},{4,5},{5,6},{6,7},{8,9},{9,10},{10,11},{11... | collective-permute-start | bytes 92168 | tf_op jit(solution)/shard_map/ppermute | solution.py:30
  (97 other events, 823.6 us)
where the time goes:
time: 781 us; the launch traced here: 776 us
  blocking collectives  429 us (55%)
  starting transfers between devices  203 us (26%)
  other arithmetic  66.7 us (9%)
  between operations  41.7 us (5%)
  local copies, waits for them, and re-layouts  22.6 us (3%)
  waiting for transfers between devices  13.3 us (2%)
    psum x48, blocking collectives, by_axis(): return functools.reduce(lax.psum, axes, shard)  429 us
    ppermute x18, starting transfers between devices, extended(): before = lax.ppermute(last, axis, up)  63.7 us
    ppermute x16, starting transfers between devices, with_halo(): lax.ppermute(last, axis, up)  57.3 us
    ppermute x18, starting transfers between devices, extended(): after = lax.ppermute(first, axis, down)  34.4 us
    ppermute x16, starting transfers between devices, with_halo(): lax.ppermute(first, axis, [(b, a) for a, b in up])  32.2 us
  transfers between devices with their start and end apart: 76, of which 15 were waited for; matrix products, arithmetic and copies ran while one was open for 7% of the time, Pallas kernels for 0%

commit v1 on v0

v1 whole, which is shorter than its diff:
```python
import functools

import jax
import jax.numpy as jnp
from jax import lax
from jax.experimental import pallas as pl
from jax.experimental.pallas import tpu as pltpu
from jax.sharding import PartitionSpec as P

F32 = jnp.float32
DT = 4.0
TAU_U = -0.45
TAU_P = 0.0
NX, NY, NZ = 8, 16, 256
YE = 32
LOW, HIGH = 7, 6
XE = LOW + NX + HIGH
ML = 4
ME = NX + 2 * ML
MO = LOW - ML
PIVOT = 2e-7
VMEM_LIMIT = 48 * 1024 * 1024

VM = pl.BlockSpec(memory_space=pltpu.VMEM)
SM = pl.BlockSpec(memory_space=pltpu.SMEM)


def up_y(v):
    return pltpu.roll(v, v.shape[0] - 1, 0)


def dn_y(v):
    return pltpu.roll(v, 1, 0)


def up_z(v):
    return pltpu.roll(v, v.shape[1] - 1, 1)


def dn_z(v):
    return pltpu.roll(v, 1, 1)


def lane():
    return lax.broadcasted_iota(jnp.int32, (YE, NZ), 1)


def loop(low, high, body, unroll=1):
    def step(x, carry):
        body(x)
        return carry

    lax.fori_loop(low, high, step, 0, unroll=unroll)


def lookup(code, mats, rows):
    found = [jnp.zeros(code.shape, F32) for _ in rows]
    for m in range(8):
        hit = code == float(m + 1)
        found = [jnp.where(hit, mats[r, m], v) for r, v in zip(rows, found)]
    return found


def pack_x_kernel(ids, p, f, u, b, up, dn):
    k = 0
    for x in range(1, 8):
        up[k] = (ids[x] + 1).astype(F32)
        up[7 + k] = p[x]
        k += 1
    up[14:20] = f[2:8]
    for a in range(3):
        up[20 + 4 * a : 24 + 4 * a] = u[a, 4:8]
        up[32 + 3 * a : 35 + 3 * a] = b[a, 5:8]
    for x in range(6):
        dn[x] = (ids[x] + 1).astype(F32)
    dn[6:12] = p[0:6]
    dn[12:17] = f[0:5]
    for a in range(3):
        dn[17 + 4 * a : 21 + 4 * a] = u[a, 0:4]
        dn[29 + 3 * a : 32 + 3 * a] = b[a, 0:3]


def pick(x, low, own, high, first, n_low):
    if x < n_low:
        return low, first[0] + x
    if x < n_low + NX:
        return own, x - n_low
    return high, first[1] + x - n_low - NX


def pack_y_kernel(ids, p, f, u, b, low, high, up, dn):
    for x in range(21):
        ref, i = pick(x, low, ids, high, (0, 0), 7)
        for out, rows in ((up, slice(8, 16)), (dn, slice(0, 8))):
            v = ref[i, rows]
            out[x] = (v + 1).astype(F32) if ref is ids else v
        ref, i = pick(x, low, p, high, (7, 6), 7)
        up[21 + x] = ref[i, 8:16]
        dn[21 + x] = ref[i, 0:8]
    for x in range(19):
        ref, i = pick(x, low, f, high, (14, 12), 6)
        up[42 + x] = ref[i, 8:16]
        dn[42 + x] = ref[i, 0:8]
    for a in range(3):
        for m in range(16):
            ref, i = pick(m, low, u.at[a], high, (20 + 4 * a, 17 + 4 * a), 4)
            k, r = 61 + 8 * a + m // 2, 4 * (m % 2)
            up[k, r : r + 4] = ref[i, 12:16]
            dn[k, r : r + 4] = ref[i, 0:4]
        for m in range(14):
            ref, i = pick(m, low, b.at[a], high, (32 + 3 * a, 29 + 3 * a), 3)
            k, r = 85 + 7 * a + m // 2, 4 * (m % 2)
            up[k, r : r + 4] = ref[i, 12:16]
            dn[k, r : r + 4] = ref[i, 0:4]


def fill(out, n, n_low, own, low, high, first, yl, yh, k, flags, cast=None):
    for x in range(n):
        ref, i = pick(x, low, own, high, first, n_low)
        v = ref[i]
        if cast is not None and ref is own:
            v = cast(v)
        lo, hi = (yl[k + x], yh[k + x])
        if flags is not None:
            if x < n_low:
                edge = flags[0]
            elif x >= n_low + NX:
                edge = flags[1]
            else:
                edge = None
            lo, hi = (lo * flags[2], hi * flags[3])
            if edge is not None:
                v, lo, hi = (v * edge, lo * edge, hi * edge)
        out[x, 8:24] = v
        out[x, 0:8] = lo
        out[x, 24:32] = hi


def fill_half(out, n, n_low, own, low, high, first, yl, yh, k, flags, offset=0):
    for x in range(n):
        ref, i = pick(x, low, own, high, first, n_low)
        v = ref[i]
        r = 4 * (x % 2)
        lo, hi = (yl[k + x // 2, r : r + 4], yh[k + x // 2, r : r + 4])
        if flags is not None:
            if x < n_low:
                edge = flags[0]
            elif x >= n_low + NX:
                edge = flags[1]
            else:
                edge = None
            lo, hi = (lo * flags[2], hi * flags[3])
            if edge is not None:
                v, lo, hi = (v * edge, lo * edge, hi * edge)
        zero = jnp.zeros((4, NZ), F32)
        out[x + offset, 8:24] = v
        out[x + offset, 0:4] = zero
        out[x + offset, 4:8] = lo
        out[x + offset, 24:28] = hi
        out[x + offset, 28:32] = zero


def spread(parts, out):
    at = lax.broadcasted_iota(jnp.int32, (8, 128), 1)
    row = jnp.zeros((8, 128), F32)
    for k, part in enumerate(parts):
        row = jnp.where(at == k, jnp.sum(part), row)
    for i in range(0, 128, 8):
        out[i : i + 8] = row


def moments(left, right, last, out, comps, first):
    def body(x, acc):
        acc = list(acc)
        for a in range(comps):
            s = [v[a, first + x, 8:24] for v in left]
            q = [v[a, first + x, 8:24] for v in right]
            terms = (s[0] * q[0], s[0] * q[1], s[1] * q[1], s[1] * q[2], s[2] * q[2], s[2] * q[3])
            acc = [t + w for t, w in zip(acc, terms)]
        return tuple(acc)

    zero = jnp.zeros((NY, NZ), F32)
    spread(lax.fori_loop(0, NX, body, (zero,) * 6), out)


def coefficients(rows, tau):
    total = jnp.sum(rows[...], axis=0, keepdims=True)
    mu = [jnp.broadcast_to(total[:, k : k + 1], (1, 128)) for k in range(6)]
    g = lambda i: (1.0 - tau) * mu[i] - mu[i + 1]
    g00, g01, g02, g12, g22 = g(0), g(1), g(2), g(3), g(4)
    g11 = g02
    inverse = lambda d, scale: jnp.where(d > PIVOT * scale, 1.0 / d, 0.0)
    i0 = inverse(g00, 0.0 * g00)
    l10, l20 = g01 * i0, g02 * i0
    i1 = inverse(g11 - l10 * g01, g11)
    e = g12 - l10 * g02
    l21 = e * i1
    i2 = inverse(g22 - l20 * g02 - l21 * e, g22)
    c0 = mu[0]
    c1 = mu[1] - l10 * c0
    c2 = mu[2] - l20 * c0 - l21 * c1
    y2 = c2 * i2
    y1 = c1 * i1 - l21 * y2
    y0 = c0 * i0 - l10 * y1 - l20 * y2
    return y0[0, 0], y1[0, 0], y2[0, 0]


def pressure_around(v, x, cx, cy, cz):
    c = v[x]
    y, z = cy[x], cz[x]
    return (
        cx[x] * v[x + 1]
        + cx[x - 1] * v[x - 1]
        + y * up_y(c)
        + dn_y(y * c)
        + z * up_z(c)
        + dn_z(z * c)
    )


def pressure_chain(start, p, cx, cy, cz, inv, t, n, part):
    def first(x):
        r = start(x) + pressure_around(p, x, cx, cy, cz)
        n[0, x] = r
        t[0, x] = inv[x] * r

    loop(1, XE - 1, first)
    for i in (1, 2):

        def follow(x):
            r = pressure_around(t.at[i - 1], x, cx, cy, cz)
            n[i, x] = r
            t[i, x] = inv[x] * r

        loop(1 + i, XE - 1 - i, follow)

    def final(x):
        n[3, x] = pressure_around(t.at[2], x, cx, cy, cz)

    loop(LOW, LOW + NX, final)
    moments([t.at[i : i + 1] for i in range(3)], [n.at[i : i + 1] for i in range(4)], None, part, 1, LOW)


def pressure_first_kernel(
    flags, mats, ids, p, f, low, high, yl, yh,
    code, pe, coef, t, part,
    fe, perm, stor, stab, n,
):
    cx, cy, cz, inv, diag, base, biot = (coef.at[i] for i in range(7))
    fill(code, XE, LOW, ids, low, high, (0, 0), yl, yh, 0, flags, lambda v: (v + 1).astype(F32))
    fill(pe, XE, LOW, p, low, high, (7, 6), yl, yh, 21, flags)
    fill(fe.at[1:20], XE - 2, LOW - 1, f, low, high, (14, 12), yl, yh, 42, None)

    def tables(x):
        l, s, k, st, bi = lookup(code[x], mats, range(5))
        bi = 0.25 * bi
        perm[x] = k
        stor[x] = st
        biot[x] = bi
        stab[x] = bi * bi / jnp.maximum(l + (2.0 / 3.0) * s, 1e-30)

    loop(0, XE, tables)

    def faces(x):
        k = perm[x]

        def harmonic(other):
            return (2.0 * DT) * k * other / jnp.maximum(k + other, 1e-30)

        cx[x] = harmonic(perm[x + 1])
        cy[x] = harmonic(up_y(k))
        cz[x] = jnp.where(lane() < NZ - 1, harmonic(up_z(k)), 0.0)

    loop(0, XE - 1, faces)

    def diagonal(x):
        y, z = cy[x], cz[x]
        flow = cx[x] + cx[x - 1] + y + dn_y(y) + z + dn_z(z)
        inside = code[x] > 0.5
        d = stor[x] + stab[x] + flow
        inv[x] = jnp.where(inside, 1.0 / jnp.where(inside, d, 1.0), 0.0)
        diag[x] = stab[x] - d
        base[x] = stor[x] * pe[x] + DT * fe[x]

    loop(1, XE - 1, diagonal)
    pressure_chain(lambda x: base[x] + diag[x] * pe[x], pe, cx, cy, cz, inv, t, n, part)


def pressure_next_kernel(
    flags, coef, p, du, uo, low, high, yl, yh,
    pe, ue, t, part,
    de, n,
):
    cx, cy, cz, inv, diag, base, biot = (coef.at[i] for i in range(7))
    for a in range(3):
        fill(de.at[a, 1:21], XE - 1, LOW - 1, du.at[a], low, high, (6 * a, 6 * a), yl, yh, 20 * a, flags)
    fill(pe, XE, LOW, p, low, high, (18, 18), yl, yh, 60, flags)

    def start(x):
        c2 = de[2, x]
        div = (
            de[0, x + 1] - de[0, x]
            + up_y(de[1, x]) - de[1, x]
            + jnp.where(lane() < NZ - 1, up_z(c2), 0.0) - c2
        )
        return base[x] - biot[x] * div + diag[x] * pe[x]

    pressure_chain(start, pe, cx, cy, cz, inv, t, n, part)

    def shifted(m):
        for a in range(3):
            ue[a, m] = uo[a, m] + de[a, m + MO]

    loop(0, ME, shifted)


def shear_around(w, m, sx, sy, sz):
    c = w[m]
    y, z = sy[m], sz[m]
    return (
        sx[m] * w[m + 1]
        + sx[m - 1] * w[m - 1]
        + y * up_y(c)
        + dn_y(y * c)
        + z * up_z(c)
        + dn_z(z * c)
    )


def mech_chain(u, bf, load, mc, s, q, carry, part):
    sx, sy, sz, diag, lame, h0, h1, h2, kk = (mc.at[i] for i in range(9))
    h = (h0, h1, h2)

    def ups(w, m):
        return (
            w[0, m + 1],
            up_y(w[1, m]),
            jnp.where(lane() < NZ - 1, up_z(w[2, m]), 0.0),
        )

    def precondition(r, m):
        scaled = [r[a] * h[a][m] for a in range(3)]
        g = kk[m] * (scaled[0] + scaled[1] + scaled[2])
        return [scaled[a] - h[a][m] * g for a in range(3)]

    def pull(m):
        p = ups(u, m)
        t = p[0] + p[1] + p[2]
        return load[m] - lame[m] * (t - (u[0, m] + u[1, m] + u[2, m]))

    carry[0] = pull(0)

    def first(m):
        c = pull(m)
        low = (carry[0], dn_y(c), jnp.where(lane() > 0, dn_z(c), 0.0))
        r = []
        for a in range(3):
            r.append(
                bf[a, m] + low[a] - c - diag[m] * u[a, m] + shear_around(u.at[a], m, sx, sy, sz)
            )
        carry[0] = c
        z = precondition(r, m)
        for a in range(3):
            q[0, a, m] = r[a]
            s[0, a, m] = z[a]

    loop(1, ME - 1, first)

    def image(w, m):
        p = ups(w, m)
        t = p[0] + p[1] + p[2]
        e = (w[0, m] + w[1, m] + w[2, m]) - t
        l = lame[m]
        low = (
            carry[0],
            dn_y(l * (p[1] + e)),
            jnp.where(lane() > 0, dn_z(l * (p[2] + e)), 0.0),
        )
        carry[0] = l * (p[0] + e)
        push = l * t
        return [
            shear_around(w.at[a], m, sx, sy, sz) + push + low[a] for a in range(3)
        ]

    def carry_in(w, m):
        p = ups(w, m)
        t = p[0] + p[1] + p[2]
        carry[0] = lame[m] * (p[0] + (w[0, m] + w[1, m] + w[2, m]) - t)

    for i in (1, 2):
        w = s.at[i - 1]
        carry_in(w, i)

        def follow(m):
            r = image(w, m)
            r = [r[a] - TAU_U * q[i - 1, a, m] for a in range(3)]
            z = precondition(r, m)
            for a in range(3):
                q[i, a, m] = r[a]
                s[i, a, m] = z[a]

        loop(1 + i, ME - 1 - i, follow)

    carry_in(s.at[2], ML - 1)

    def final(m):
        r = image(s.at[2], m)
        for a in range(3):
            q[3, a, m] = r[a] - TAU_U * q[2, a, m]

    loop(ML, ML + NX, final)
    moments([s.at[i] for i in range(3)], [q.at[i] for i in range(4)], None, part, 3, ML)


def update_pressure(rows, t, pe, biot_of, pout, load):
    y = coefficients(rows, TAU_P)

    def body(m):
        x = m + MO
        v = pe[x] + (y[0] * t[0, x] + y[1] * t[1, x] + y[2] * t[2, x])
        load[m] = biot_of(x) * v
        pout[m] = v

    loop(0, ME - 1, body)


def mech_first_kernel(
    flags, mats, rows, code, pe, coef, t, u, b, low, high, yl, yh,
    pnew, ue, be, mc, s, part,
    q, load, pm, shear, sall, carry,
):
    sx, sy, sz, diag, lame, h0, h1, h2, kk = (mc.at[i] for i in range(9))
    biot = coef.at[6]
    for a in range(3):
        fill_half(ue.at[a], 16, 4, u.at[a], low, high, (20 + 4 * a, 17 + 4 * a), yl, yh, 61 + 8 * a, flags)
        fill_half(be.at[a], 14, 3, b.at[a], low, high, (32 + 3 * a, 29 + 3 * a), yl, yh, 85 + 7 * a, None, 1)

    def tables(m):
        l, g = lookup(code[m + MO], mats, (0, 1))
        lame[m] = l
        shear[m] = g

    loop(0, ME, tables)

    def faces(m):
        g = shear[m]
        sx[m] = 0.5 * (g + shear[m + 1])
        sy[m] = 0.5 * (g + up_y(g))
        sz[m] = jnp.where(lane() < NZ - 1, 0.5 * (g + up_z(g)), 0.0)

    loop(0, ME - 1, faces)

    def diagonal(m):
        g, l = shear[m], lame[m]
        around = (
            shear[m + 1] + shear[m - 1] + up_y(g) + dn_y(g)
            + jnp.where(lane() < NZ - 1, up_z(g), 0.0)
            + jnp.where(lane() > 0, dn_z(g), 0.0)
        )
        d = 3.0 * g + 0.5 * around
        diag[m] = d
        inside = code[m + MO] > 0.5
        lows = (lame[m - 1], dn_y(l), jnp.where(lane() > 0, dn_z(l), 0.0))
        hs = [jnp.where(inside, 1.0 / jnp.where(inside, d + v, 1.0), 0.0) for v in lows]
        h0[m], h1[m], h2[m] = hs
        kk[m] = l / (1.0 + l * (hs[0] + hs[1] + hs[2]))

    loop(1, ME - 1, diagonal)
    update_pressure(rows, t, pe, lambda x: biot[x], pm, load)
    for x in range(NX):
        pnew[x] = pm[x + ML, 8:24]
    mech_chain(ue, be, load, mc, sall, q, carry, part)
    for i in range(3):
        for a in range(3):
            for x in range(NX):
                s[i, a, x] = sall[i, a, x + ML, 8:24]


def mech_next_kernel(
    rows, pe, coef, t, ue, be, mc,
    pnew, s, part,
    q, load, pm, sall, carry,
):
    biot = coef.at[6]
    update_pressure(rows, t, pe, lambda x: biot[x], pm, load)
    for x in range(NX):
        pnew[x] = pm[x + ML, 8:24]
    mech_chain(ue, be, load, mc, sall, q, carry, part)
    for i in range(3):
        for a in range(3):
            for x in range(NX):
                s[i, a, x] = sall[i, a, x + ML, 8:24]


def change_kernel(rows, s, u, p, du, unew, up, dn):
    y = coefficients(rows, TAU_U)
    for a in range(3):
        for x in range(NX):
            d = y[0] * s[0, a, x] + y[1] * s[1, a, x] + y[2] * s[2, a, x]
            du[a, x] = d
            unew[a, x] = u[a, x] + d
            if x >= 2:
                up[6 * a + x - 2] = d
            if x < 6:
                dn[6 * a + x] = d
    up[18:25] = p[1:8]
    dn[18:24] = p[0:6]


def pack_change_kernel(du, p, low, high, up, dn):
    for a in range(3):
        for x in range(20):
            ref, i = pick(x, low, du.at[a], high, (6 * a, 6 * a), 6)
            up[20 * a + x] = ref[i, 8:16]
            dn[20 * a + x] = ref[i, 0:8]
    for x in range(21):
        ref, i = pick(x, low, p, high, (18, 18), 7)
        up[60 + x] = ref[i, 8:16]
        dn[60 + x] = ref[i, 0:8]


def finish_kernel(rows, s, u, out):
    y = coefficients(rows, TAU_U)
    for a in range(3):
        for x in range(NX):
            out[a, x] = u[a, x] + (y[0] * s[0, a, x] + y[1] * s[1, a, x] + y[2] * s[2, a, x])


def call(kernel, name, ins, outs, scratch=(), specs=None):
    return pl.pallas_call(
        kernel,
        name=name,
        out_shape=[jax.ShapeDtypeStruct(o, F32) for o in outs],
        in_specs=specs or [VM] * len(ins),
        out_specs=[VM] * len(outs),
        scratch_shapes=[pltpu.VMEM(s, F32) for s in scratch],
        compiler_params=pltpu.CompilerParams(vmem_limit_bytes=VMEM_LIMIT),
    )(*ins)


def neighbours(axis, size, up, dn):
    ring = [(i, (i + 1) % size) for i in range(size)]
    return lax.ppermute(up, axis, ring), lax.ppermute(dn, axis, [(b, a) for a, b in ring])


def gather_rows(part):
    return lax.all_to_all(part, ("gx", "gy"), 0, 0, tiled=True)


def on_device(gx_size, gy_size, u, p, b, f, ids, mats):
    gx, gy = lax.axis_index("gx"), lax.axis_index("gy")
    flags = jnp.stack([gx > 0, gx < gx_size - 1, gy > 0, gy < gy_size - 1]).astype(F32)
    wide = (YE, NZ)
    up, dn = call(pack_x_kernel, "pack_x", (ids, p, f, u, b), [(41, NY, NZ), (38, NY, NZ)])
    low, high = neighbours("gx", gx_size, up, dn)
    up, dn = call(
        pack_y_kernel, "pack_y", (ids, p, f, u, b, low, high), [(106, 8, NZ), (106, 8, NZ)]
    )
    yl, yh = neighbours("gy", gy_size, up, dn)
    code, pe, coef, t, part = call(
        pressure_first_kernel,
        "pressure_first",
        (flags, mats, ids, p, f, low, high, yl, yh),
        [(XE, *wide), (XE, *wide), (7, XE, *wide), (3, XE, *wide), (128, 128)],
        [(XE, *wide)] * 4 + [(4, XE, *wide)],
        [SM, SM] + [VM] * 7,
    )
    rows = gather_rows(part)
    p1, ue, be, mc, s, part = call(
        mech_first_kernel,
        "mech_first",
        (flags, mats, rows, code, pe, coef, t, u, b, low, high, yl, yh),
        [(NX, NY, NZ), (3, ME, *wide), (3, ME, *wide), (9, ME, *wide), (3, 3, NX, NY, NZ), (128, 128)],
        [(4, 3, ME, *wide), (ME, *wide), (ME, *wide), (ME, *wide), (3, 3, ME, *wide), (1, *wide)],
        [SM, SM] + [VM] * 11,
    )
    rows = gather_rows(part)
    du, u1, up, dn = call(
        change_kernel,
        "change",
        (rows, s, u, p1),
        [(3, NX, NY, NZ), (3, NX, NY, NZ), (25, NY, NZ), (24, NY, NZ)],
    )
    low, high = neighbours("gx", gx_size, up, dn)
    up, dn = call(pack_change_kernel, "pack_change", (du, p1, low, high), [(81, 8, NZ), (81, 8, NZ)])
    yl, yh = neighbours("gy", gy_size, up, dn)
    pe, ue, t, part = call(
        pressure_next_kernel,
        "pressure_next",
        (flags, coef, p1, du, ue, low, high, yl, yh),
        [(XE, *wide), (3, ME, *wide), (3, XE, *wide), (128, 128)],
        [(3, XE, *wide), (4, XE, *wide)],
        [SM] + [VM] * 8,
    )
    rows = gather_rows(part)
    p2, s, part = call(
        mech_next_kernel,
        "mech_next",
        (rows, pe, coef, t, ue, be, mc),
        [(NX, NY, NZ), (3, 3, NX, NY, NZ), (128, 128)],
        [(4, 3, ME, *wide), (ME, *wide), (ME, *wide), (3, 3, ME, *wide), (1, *wide)],
    )
    rows = gather_rows(part)
    (u2,) = call(finish_kernel, "finish", (rows, s, u1), [(3, NX, NY, NZ)])
    return u2, p2


def solution(mesh):
    body = functools.partial(on_device, mesh.shape["gx"], mesh.shape["gy"])
    field, vector = P("gx", "gy", None), P(None, "gx", "gy", None)
    return jax.shard_map(
        body,
        mesh=mesh,
        in_specs=(vector, field, vector, field, field, P()),
        out_specs=(vector, field),
        check_vma=False,
    )
```

time: 781 us -> 192 us (0.25)
  blocking collectives: 429 us -> 62.6 us
  starting transfers between devices: 203 us -> 16.1 us
  other arithmetic: 66.7 us -> 0.08 us
  Pallas kernels: 0 us -> 59.8 us
  between operations: 41.7 us -> 0.69 us
  waiting for transfers between devices: 13.3 us -> 46.3 us
  local copies, waits for them, and re-layouts: 22.6 us -> 5.99 us
    psum x48 -> x0, blocking collectives: 429 us -> none  [by_axis(): return functools.reduce(lax.psum, axes, shard)]
    ppermute x76 -> x8, starting transfers between devices: 203 us -> 16.1 us  [the longest x4 9.31 us: neighbours(): lax.ppermute(dn, axis, [(b, a) for a, b in ring])]
    all_to_all x0 -> x4, blocking collectives: none -> 62.6 us  [gather_rows(): return lax.all_to_all(part, ('gx', 'gy'), 0, 0, tiled=True)]
    pallas_call x0 -> x9, Pallas kernels: none -> 59.8 us  [call(): pl.pallas_call(kernel, name=name, out_shape=[jax.ShapeDtypeStruct(o, F32)...]
    ppermute x76 -> x8, waiting for transfers between devices: 13.3 us -> 46.3 us  [the longest x4 25.3 us: neighbours(): lax.ppermute(dn, axis, [(b, a) for a, b in ring])]
    mul x26 -> x0, other arithmetic: 21.7 us -> none  [the longest x4 12.7 us: solve_pressure(): return residual * inv_pressure]
    reduce_sum x14 -> x0, other arithmetic: 18.7 us -> none  [the longest x12 15.4 us: run_solver(): jnp.sum(smoothed * image_vec)]
    select_n x3 -> x0, other arithmetic: 15.5 us -> none  [lookup(): jnp.where(matched, materials[table_row, material], current)]
  transfers between devices with their start and end apart: 76 -> 8, of which waited for: 15 -> 8; matrix products, arithmetic and copies ran while one was open for 7% -> 0% of each run, Pallas kernels for 0% -> 0%
where the time goes in v1:
time: 192 us; the launch traced here: 191 us
  blocking collectives  62.6 us (33%)
  Pallas kernels  59.8 us (31%)
  waiting for transfers between devices  46.3 us (24%)
  starting transfers between devices  16.1 us (8%)
  local copies, waits for them, and re-layouts  5.99 us (3%)
    all_to_all x4, blocking collectives, gather_rows(): return lax.all_to_all(part, ('gx', 'gy'), 0, 0, tiled=True)  62.6 us
    pallas_call x9, Pallas kernels, call(): pl.pallas_call(kernel, name=name, out_shape=[jax.ShapeDtypeStruct(o, F32)...  59.8 us
    ppermute x4, waiting for transfers between devices, neighbours(): lax.ppermute(dn, axis, [(b, a) for a, b in ring])  25.3 us
    ppermute x4, waiting for transfers between devices, neighbours(): lax.ppermute(up, axis, ring)  21 us
    ppermute x4, starting transfers between devices, neighbours(): lax.ppermute(dn, axis, [(b, a) for a, b in ring])  9.31 us
    ppermute x4, starting transfers between devices, neighbours(): lax.ppermute(up, axis, ring)  6.78 us
    unnamed x26, local copies, waits for them, and re-layouts  5.99 us
  transfers between devices with their start and end apart: 8, of which 8 were waited for; matrix products, arithmetic and copies ran while one was open for 0% of the time, Pallas kernels for 0%

profile of v1, /device:TPU:1, one launch (start us, length us, event | category | flops | bytes accessed | tf_op | source)
XLA Modules:
  0.0 191.5 jit_solution(9275839627686083490)
XLA Ops:
  0.6 1.0 copy-done
  1.6 1.0 copy-done.2
  2.6 0.9 copy-done.5
  3.5 0.9 copy-done.7
  4.4 0.9 copy-done.9
  5.4 2.1 %collective-permute-start = (f32[41,16,256]{2,1,0:T(8,128)S(1)}, f32[41,16,256]{2,1,0:T(8,128)S(1)}, u32[]{:S(2)}, u32[]{:S(2)}) collective-permute-start(f32[41,16,256]{2,1,0:T(8,128)S(1)} %get-tuple-element.30), channel_id=1, source_target_pairs={{0,8},{8,16},{16,24},{24,32},{32,40},{40,48},{48,56},{56,64},{64,7... | collective-permute-start | bytes 2015240 | tf_op jit(solution)/shard_map/ppermute | solution.py:543
  7.5 4.8 %collective-permute-start.1 = (f32[38,16,256]{2,1,0:T(8,128)S(1)}, f32[38,16,256]{2,1,0:T(8,128)S(1)}, u32[]{:S(2)}, u32[]{:S(2)}) collective-permute-start(f32[38,16,256]{2,1,0:T(8,128)S(1)} %get-tuple-element.31), channel_id=1, source_target_pairs={{8,0},{16,8},{24,16},{32,24},{40,32},{48,40},{56,48},{64,56},{72,6... | collective-permute-start | bytes 1867784 | tf_op jit(solution)/shard_map/ppermute | solution.py:543
  12.4 12.7 %collective-permute-done.1.high = f32[38,16,256]{2,1,0:T(8,128)S(1)} collective-permute-done((f32[38,16,256]{2,1,0:T(8,128)S(1)}, f32[38,16,256]{2,1,0:T(8,128)S(1)}, u32[]{:S(2)}, u32[]{:S(2)}) %collective-permute-start.1) | collective-permute-done | bytes 622624 | tf_op jit(solution)/shard_map/ppermute | solution.py:543
  25.1 2.0 %collective-permute-done.low = f32[41,16,256]{2,1,0:T(8,128)S(1)} collective-permute-done((f32[41,16,256]{2,1,0:T(8,128)S(1)}, f32[41,16,256]{2,1,0:T(8,128)S(1)}, u32[]{:S(2)}, u32[]{:S(2)}) %collective-permute-start) | collective-permute-done | bytes 671776 | tf_op jit(solution)/shard_map/ppermute | solution.py:543
  27.1 1.5 pack_y.1
  28.5 2.4 %collective-permute-start.2 = (f32[106,8,256]{2,1,0:T(8,128)}, f32[106,8,256]{2,1,0:T(8,128)S(1)}, u32[]{:S(2)}, u32[]{:S(2)}) collective-permute-start(f32[106,8,256]{2,1,0:T(8,128)} %get-tuple-element.32), channel_id=1, source_target_pairs={{0,1},{1,2},{2,3},{3,4},{4,5},{5,6},{6,7},{7,0},{8,9},{9,10},{10,1... | collective-permute-start | bytes 2605064 | tf_op jit(solution)/shard_map/ppermute | solution.py:543
  31.1 10.0 %collective-permute-done.2.yl = f32[106,8,256]{2,1,0:T(8,128)S(1)} collective-permute-done((f32[106,8,256]{2,1,0:T(8,128)}, f32[106,8,256]{2,1,0:T(8,128)S(1)}, u32[]{:S(2)}, u32[]{:S(2)}) %collective-permute-start.2) | collective-permute-done | bytes 868384 | tf_op jit(solution)/shard_map/ppermute | solution.py:543
  41.1 2.4 %collective-permute-done.3.yh = f32[106,8,256]{2,1,0:T(8,128)S(1)} collective-permute-done((f32[106,8,256]{2,1,0:T(8,128)}, f32[106,8,256]{2,1,0:T(8,128)S(1)}, u32[]{:S(2)}, u32[]{:S(2)}) %collective-permute-start.3) | collective-permute-done | bytes 868384 | tf_op jit(solution)/shard_map/ppermute | solution.py:543
  43.5 14.2 %pressure_first.1 = (f32[21,32,256]{2,1,0:T(8,128)S(1)}, f32[21,32,256]{2,1,0:T(8,128)S(1)}, f32[7,21,32,256]{3,2,1,0:T(8,128)}, f32[3,21,32,256]{3,2,1,0:T(8,128)}, f32[128,128]{1,0:T(8,128)S(1)}) custom-call(f32[4]{0:T(128)S(1)} %add_convert_fusion.flags, f32[5,8]{1,0:T(8,128)S(1)} %copy-done.12, s32[8,16,256]{2,1,0:T(8,128)S(1)} %copy-done.6, ...), custom_call_target="tpu_custom_call" | custom-call | tf_op jit(solution)/shard_map/pressure_first/pallas_call | solution.py:530
  57.7 16.8 %all_to_all.44 = f32[128,1,128]{2,1,0:T(1,128)S(1)} all-to-all(f32[128,1,128]{2,1,0:T(1,128)S(1)} %bitcast.27), channel_id=1, replica_groups=mesh['gx'=16,'gy'=8] {'gx','gy'}, dimensions={0} | all-to-all | bytes 131072 | tf_op jit(solution)/shard_map/all_to_all | solution.py:547
  74.5 18.8 %mech_first.1 = (f32[8,16,256]{2,1,0:T(8,128)S(1)}, f32[3,16,32,256]{3,2,1,0:T(8,128)}, f32[3,16,32,256]{3,2,1,0:T(8,128)}, f32[9,16,32,256]{3,2,1,0:T(8,128)}, ...) custom-call(f32[4]{0:T(128)S(1)} %add_convert_fusion.flags, f32[5,8]{1,0:T(8,128)S(1)} %copy-done.12, ...), custom_call_target="tpu_custom_call" | custom-call | tf_op jit(solution)/shard_map/mech_first/pallas_call | solution.py:530
  93.3 13.8 %all_to_all.45 = f32[128,1,128]{2,1,0:T(1,128)S(1)} all-to-all(f32[128,1,128]{2,1,0:T(1,128)S(1)} %bitcast.24), channel_id=1, replica_groups=mesh['gx'=16,'gy'=8] {'gx','gy'}, dimensions={0} | all-to-all | bytes 131072 | tf_op jit(solution)/shard_map/all_to_all | solution.py:547
  107.2 1.3 copy-done.11
  108.4 0.3 change.1
  108.8 0.4 collective-permute-start.4
  109.1 4.5 %collective-permute-start.5 = (f32[24,16,256]{2,1,0:T(8,128)S(1)}, f32[24,16,256]{2,1,0:T(8,128)S(1)}, u32[]{:S(2)}, u32[]{:S(2)}) collective-permute-start(f32[24,16,256]{2,1,0:T(8,128)S(1)} %get-tuple-element.45), channel_id=1, source_target_pairs={{8,0},{16,8},{24,16},{32,24},{40,32},{48,40},{56,48},{64,56},{72,6... | collective-permute-start | bytes 1179656 | tf_op jit(solution)/shard_map/ppermute | solution.py:543
  113.6 7.4 %collective-permute-done.5.high = f32[24,16,256]{2,1,0:T(8,128)S(1)} collective-permute-done((f32[24,16,256]{2,1,0:T(8,128)S(1)}, f32[24,16,256]{2,1,0:T(8,128)S(1)}, u32[]{:S(2)}, u32[]{:S(2)}) %collective-permute-start.5) | collective-permute-done | bytes 393248 | tf_op jit(solution)/shard_map/ppermute | solution.py:543
  121.1 1.4 collective-permute-done.4.low
  122.4 0.1 pack_change.1
  122.5 1.9 collective-permute-start.6
  124.4 7.6 %collective-permute-done.6.yl = f32[81,8,256]{2,1,0:T(8,128)S(1)} collective-permute-done((f32[81,8,256]{2,1,0:T(8,128)S(1)}, f32[81,8,256]{2,1,0:T(8,128)S(1)}, u32[]{:S(2)}, u32[]{:S(2)}) %collective-permute-start.6) | collective-permute-done | bytes 663584 | tf_op jit(solution)/shard_map/ppermute | solution.py:543
  132.0 2.8 %collective-permute-done.7.yh = f32[81,8,256]{2,1,0:T(8,128)S(1)} collective-permute-done((f32[81,8,256]{2,1,0:T(8,128)S(1)}, f32[81,8,256]{2,1,0:T(8,128)S(1)}, u32[]{:S(2)}, u32[]{:S(2)}) %collective-permute-start.7) | collective-permute-done | bytes 663584 | tf_op jit(solution)/shard_map/ppermute | solution.py:543
  134.8 10.3 %pressure_next.1 = (f32[21,32,256]{2,1,0:T(8,128)S(1)}, f32[3,16,32,256]{3,2,1,0:T(8,128)S(1)}, f32[3,21,32,256]{3,2,1,0:T(8,128)}, f32[128,128]{1,0:T(8,128)S(1)}) custom-call(f32[4]{0:T(128)S(1)} %add_convert_fusion.flags, f32[7,21,32,256]{3,2,1,0:T(8,128)} %get-tuple-element.34.coef, f32[8,16,256]{2,1,0:T(8,128)S(1)} %get-tuple-element.39.p, ...), custom_call_target="tpu_custom_call" | custom-call | tf_op jit(solution)/shard_map/pressure_next/pallas_call | solution.py:530
  145.1 18.1 %all_to_all.46 = f32[128,1,128]{2,1,0:T(1,128)S(1)} all-to-all(f32[128,1,128]{2,1,0:T(1,128)S(1)} %bitcast.25), channel_id=1, replica_groups=mesh['gx'=16,'gy'=8] {'gx','gy'}, dimensions={0} | all-to-all | bytes 131072 | tf_op jit(solution)/shard_map/all_to_all | solution.py:547
  163.2 13.5 %mech_next.1 = (f32[8,16,256]{2,1,0:T(8,128)}, f32[3,3,8,16,256]{4,3,2,1,0:T(8,128)S(1)}, f32[128,128]{1,0:T(8,128)S(1)}) custom-call(f32[128,128]{1,0:T(8,128)S(1)} %bitcast.21, f32[21,32,256]{2,1,0:T(8,128)S(1)} %get-tuple-element.49.pe, f32[7,21,32,256]{3,2,1,0:T(8,128)} %get-tuple-element.34.coef, f32[3,21,32,256]{3,2,1,0:T(8,128)} %get-tuple-element.50.t, ...), custom_call_target="tpu_custom_call" | custom-call | tf_op jit(solution)/shard_map/mech_next/pallas_call | solution.py:530
  176.7 13.8 %all_to_all.47 = f32[128,1,128]{2,1,0:T(1,128)S(1)} all-to-all(f32[128,1,128]{2,1,0:T(1,128)S(1)} %bitcast.26), channel_id=1, replica_groups=mesh['gx'=16,'gy'=8] {'gx','gy'}, dimensions={0} | all-to-all | bytes 131072 | tf_op jit(solution)/shard_map/all_to_all | solution.py:547
  190.5 1.0 finish.1
  (24 shorter events, 0.2 us)
Async XLA Ops:
  0.6 1.0 copy-start
  1.6 1.0 copy-start.2
  2.6 0.9 copy-start.5
  3.5 0.9 copy-start.7
  4.4 0.9 copy-start.9
  5.3 38.1 %copy-start.6 = (s32[8,16,256]{2,1,0:T(8,128)S(1)}, s32[8,16,256]{2,1,0:T(8,128)}, u32[]{:S(2)}) copy-start(s32[8,16,256]{2,1,0:T(8,128)} %ids.5) | copy-start | bytes 393220
  5.3 38.1 %copy-start.8 = (f32[8,16,256]{2,1,0:T(8,128)S(1)}, f32[8,16,256]{2,1,0:T(8,128)}, u32[]{:S(2)}) copy-start(f32[8,16,256]{2,1,0:T(8,128)} %p.5) | copy-start | bytes 393220
  5.3 38.1 %copy-start.10 = (f32[8,16,256]{2,1,0:T(8,128)S(1)}, f32[8,16,256]{2,1,0:T(8,128)}, u32[]{:S(2)}) copy-start(f32[8,16,256]{2,1,0:T(8,128)} %f.5) | copy-start | bytes 393220
  5.3 38.1 %copy-start.12 = (f32[5,8]{1,0:T(8,128)S(1)}, f32[5,8]{1,0:T(8,128)}, u32[]{:S(2)}) copy-start(f32[5,8]{1,0:T(8,128)} %mats.3) | copy-start | bytes 484
  5.4 21.6 %collective-permute-start = (f32[41,16,256]{2,1,0:T(8,128)S(1)}, f32[41,16,256]{2,1,0:T(8,128)S(1)}, u32[]{:S(2)}, u32[]{:S(2)}) collective-permute-start(f32[41,16,256]{2,1,0:T(8,128)S(1)} %get-tuple-element.30), channel_id=1, source_target_pairs={{0,8},{8,16},{16,24},{24,32},{32,40},{40,48},{48,56},{56,64},{64,7... | collective-permute-start | bytes 2015240 | tf_op jit(solution)/shard_map/ppermute | solution.py:543
  7.5 17.5 %collective-permute-start.1 = (f32[38,16,256]{2,1,0:T(8,128)S(1)}, f32[38,16,256]{2,1,0:T(8,128)S(1)}, u32[]{:S(2)}, u32[]{:S(2)}) collective-permute-start(f32[38,16,256]{2,1,0:T(8,128)S(1)} %get-tuple-element.31), channel_id=1, source_target_pairs={{8,0},{16,8},{24,16},{32,24},{40,32},{48,40},{56,48},{64,56},{72,6... | collective-permute-start | bytes 1867784 | tf_op jit(solution)/shard_map/ppermute | solution.py:543
  28.5 12.6 %collective-permute-start.2 = (f32[106,8,256]{2,1,0:T(8,128)}, f32[106,8,256]{2,1,0:T(8,128)S(1)}, u32[]{:S(2)}, u32[]{:S(2)}) collective-permute-start(f32[106,8,256]{2,1,0:T(8,128)} %get-tuple-element.32), channel_id=1, source_target_pairs={{0,1},{1,2},{2,3},{3,4},{4,5},{5,6},{6,7},{7,0},{8,9},{9,10},{10,1... | collective-permute-start | bytes 2605064 | tf_op jit(solution)/shard_map/ppermute | solution.py:543
  31.0 12.5 %collective-permute-start.3 = (f32[106,8,256]{2,1,0:T(8,128)}, f32[106,8,256]{2,1,0:T(8,128)S(1)}, u32[]{:S(2)}, u32[]{:S(2)}) collective-permute-start(f32[106,8,256]{2,1,0:T(8,128)} %get-tuple-element.33), channel_id=1, source_target_pairs={{1,0},{2,1},{3,2},{4,3},{5,4},{6,5},{7,6},{0,7},{9,8},{10,9},{11,1... | collective-permute-start | bytes 2605064 | tf_op jit(solution)/shard_map/ppermute | solution.py:543
  31.0 43.5 %copy-start.1 = (f32[3,8,16,256]{3,2,1,0:T(8,128)S(1)}, f32[3,8,16,256]{3,2,1,0:T(8,128)}, u32[]{:S(2)}) copy-start(f32[3,8,16,256]{3,2,1,0:T(8,128)} %u.7) | copy-start | bytes 1179652
  31.0 43.5 %copy-start.3 = (f32[3,8,16,256]{3,2,1,0:T(8,128)S(1)}, f32[3,8,16,256]{3,2,1,0:T(8,128)}, u32[]{:S(2)}) copy-start(f32[3,8,16,256]{3,2,1,0:T(8,128)} %b.5) | copy-start | bytes 1179652
  107.2 1.3 copy-start.11
  108.8 13.6 %collective-permute-start.4 = (f32[25,16,256]{2,1,0:T(8,128)S(1)}, f32[25,16,256]{2,1,0:T(8,128)S(1)}, u32[]{:S(2)}, u32[]{:S(2)}) collective-permute-start(f32[25,16,256]{2,1,0:T(8,128)S(1)} %get-tuple-element.44), channel_id=1, source_target_pairs={{0,8},{8,16},{16,24},{24,32},{32,40},{40,48},{48,56},{56,64},{64,7... | collective-permute-start | bytes 1228808 | tf_op jit(solution)/shard_map/ppermute | solution.py:543
  109.1 11.9 %collective-permute-start.5 = (f32[24,16,256]{2,1,0:T(8,128)S(1)}, f32[24,16,256]{2,1,0:T(8,128)S(1)}, u32[]{:S(2)}, u32[]{:S(2)}) collective-permute-start(f32[24,16,256]{2,1,0:T(8,128)S(1)} %get-tuple-element.45), channel_id=1, source_target_pairs={{8,0},{16,8},{24,16},{32,24},{40,32},{48,40},{56,48},{64,56},{72,6... | collective-permute-start | bytes 1179656 | tf_op jit(solution)/shard_map/ppermute | solution.py:543
  122.5 9.5 %collective-permute-start.6 = (f32[81,8,256]{2,1,0:T(8,128)S(1)}, f32[81,8,256]{2,1,0:T(8,128)S(1)}, u32[]{:S(2)}, u32[]{:S(2)}) collective-permute-start(f32[81,8,256]{2,1,0:T(8,128)S(1)} %get-tuple-element.46), channel_id=1, source_target_pairs={{0,1},{1,2},{2,3},{3,4},{4,5},{5,6},{6,7},{7,0},{8,9},{9,10},{10,1... | collective-permute-start | bytes 1990664 | tf_op jit(solution)/shard_map/ppermute | solution.py:543
  124.4 10.4 %collective-permute-start.7 = (f32[81,8,256]{2,1,0:T(8,128)S(1)}, f32[81,8,256]{2,1,0:T(8,128)S(1)}, u32[]{:S(2)}, u32[]{:S(2)}) collective-permute-start(f32[81,8,256]{2,1,0:T(8,128)S(1)} %get-tuple-element.47), channel_id=1, source_target_pairs={{1,0},{2,1},{3,2},{4,3},{5,4},{6,5},{7,6},{0,7},{9,8},{10,9},{11,1... | collective-permute-start | bytes 1990664 | tf_op jit(solution)/shard_map/ppermute | solution.py:543
  134.8 28.4 %copy-start.4 = (f32[3,16,32,256]{3,2,1,0:T(8,128)S(1)}, f32[3,16,32,256]{3,2,1,0:T(8,128)}, u32[]{:S(2)}) copy-start(f32[3,16,32,256]{3,2,1,0:T(8,128)} %get-tuple-element.52.be) | copy-start | bytes 4718596

commit v2 on v1

v2 whole, which is shorter than its diff:
```python
import functools

import jax
import jax.numpy as jnp
from jax import lax
from jax.experimental import pallas as pl
from jax.experimental.pallas import tpu as pltpu
from jax.sharding import PartitionSpec as P

F32 = jnp.float32
DT = 4.0
NX, NY, NZ = 8, 16, 256
YE = 32
YM = 24
GENS = 4
PAIRS = [(a, b) for a in range(GENS) for b in range(a, GENS)]
LEVELS = ((0, 0), (0, 1), (1, 1), (1, 2), (2, 2), (2, 3))
LOW, HIGH = 7, 6
XE = LOW + NX + HIGH
ML = 4
ME = NX + 2 * ML
MO = LOW - ML
PK = ML + NX + 3
PIVOT = 2e-7
PW = 4
COST = 200_000_000

VM = pl.BlockSpec(memory_space=pltpu.VMEM)
SM = pl.BlockSpec(memory_space=pltpu.SMEM)
HB = pl.BlockSpec(memory_space=pltpu.HBM)


def up_y(v):
    return pltpu.roll(v, v.shape[0] - 1, 0)


def dn_y(v):
    return pltpu.roll(v, 1, 0)


def up_z(v):
    low, high = pltpu.roll(v[:, :128], 127, 1), pltpu.roll(v[:, 128:], 127, 1)
    inner = lax.broadcasted_iota(jnp.int32, low.shape, 1) < 127
    return jnp.concatenate([jnp.where(inner, low, high), jnp.where(inner, high, 0.0)], axis=1)


def dn_z(v):
    low, high = pltpu.roll(v[:, :128], 1, 1), pltpu.roll(v[:, 128:], 1, 1)
    inner = lax.broadcasted_iota(jnp.int32, low.shape, 1) > 0
    return jnp.concatenate([jnp.where(inner, low, 0.0), jnp.where(inner, high, low)], axis=1)


def loop(low, high, compute, width=1):
    def group(x, count):
        for i in range(count):
            for ref, index, value in compute(x + i):
                ref[index] = value

    steps = (high - low) // width

    def step(k, carry):
        group(low + k * width, width)
        return carry

    lax.fori_loop(0, steps, step, 0)
    if (high - low) % width:
        group(low + steps * width, (high - low) % width)


def lookup(code, mats, rows):
    found = [jnp.zeros(code.shape, F32) for _ in rows]
    for m in range(8):
        hit = code == float(m + 1)
        found = [jnp.where(hit, mats[r, m], v) for r, v in zip(rows, found)]
    return found


def pack_x_kernel(ids, p, f, u, b, up_p, dn_p, up_m, dn_m, code, pv, fv, raw, sems):
    copies = []

    def take(src, dst):
        copies.append(pltpu.make_async_copy(src, dst, sems.at[len(copies)]))
        copies[-1].start()

    take(ids, raw)
    take(p, pv)
    take(f, fv)
    take(p.at[1:8], up_p.at[7:14])
    take(p.at[0:6], dn_p.at[6:12])
    take(f.at[2:8], up_p.at[14:20])
    take(f.at[0:5], dn_p.at[12:17])
    for a in range(3):
        take(u.at[a, 4:8], up_m.at[4 * a : 4 * a + 4])
        take(u.at[a, 0:4], dn_m.at[4 * a : 4 * a + 4])
        take(b.at[a, 5:8], up_m.at[12 + 3 * a : 15 + 3 * a])
        take(b.at[a, 0:3], dn_m.at[12 + 3 * a : 15 + 3 * a])
    copies[0].wait()
    for x in range(NX):
        c = (raw[x] + 1).astype(F32)
        code[x] = c
        if x >= 1:
            up_p[x - 1] = c
        if x < 6:
            dn_p[x] = c
    for copy in copies[1:]:
        copy.wait()


def pick(x, low, own, high, first, n_low):
    if x < n_low:
        return low, first[0] + x
    if x < n_low + NX:
        return own, x - n_low
    return high, first[1] + x - n_low - NX


def pack_y_pressure_kernel(ids, p, f, low, high, up, dn):
    for x in range(21):
        ref, i = pick(x, low, ids, high, (0, 0), 7)
        up[x] = ref[i, 8:16]
        dn[x] = ref[i, 0:8]
        ref, i = pick(x, low, p, high, (7, 6), 7)
        up[21 + x] = ref[i, 8:16]
        dn[21 + x] = ref[i, 0:8]
    for x in range(19):
        ref, i = pick(x, low, f, high, (14, 12), 6)
        up[42 + x] = ref[i, 8:16]
        dn[42 + x] = ref[i, 0:8]


def pack_y_mech_kernel(u, b, low, high, up, dn):
    for a in range(3):
        for m in range(16):
            ref, i = pick(m, low, u.at[a], high, (4 * a, 4 * a), 4)
            k, r = 8 * a + m // 2, 4 * (m % 2)
            up[k, r : r + 4] = ref[i, 12:16]
            dn[k, r : r + 4] = ref[i, 0:4]
        for m in range(14):
            ref, i = pick(m, low, b.at[a], high, (12 + 3 * a, 12 + 3 * a), 3)
            k, r = 24 + 7 * a + m // 2, 4 * (m % 2)
            up[k, r : r + 4] = ref[i, 12:16]
            dn[k, r : r + 4] = ref[i, 0:4]


def masked(x, n_low, flags, v, lo, hi):
    if flags is None:
        return v, lo, hi
    lo, hi = (lo * flags[2], hi * flags[3])
    if n_low <= x < n_low + NX:
        return v, lo, hi
    edge = flags[0] if x < n_low else flags[1]
    return v * edge, lo * edge, hi * edge


def fill(out, n, n_low, own, low, high, first, yl, yh, k, flags):
    for x in range(n):
        ref, i = pick(x, low, own, high, first, n_low)
        v, lo, hi = masked(x, n_low, flags, ref[i], yl[k + x], yh[k + x])
        out[x, 8:24] = v
        out[x, 0:8] = lo
        out[x, 24:32] = hi


def fill_mech(out, n, n_low, own, low, high, first, yl, yh, k, flags, offset):
    for x in range(n):
        ref, i = pick(x, low, own, high, first, n_low)
        r = 4 * (x % 2)
        lo, hi = yl[k + x // 2, r : r + 4], yh[k + x // 2, r : r + 4]
        v, lo, hi = masked(x, n_low, flags, ref[i], lo, hi)
        out[x + offset, 0:4] = lo
        out[x + offset, 4:20] = v
        out[x + offset, 20:24] = hi


def solve(mu):
    g = lambda i: mu[i] - mu[i + 1]
    g00, g01, g02, g12, g22 = g(0), g(1), g(2), g(3), g(4)
    g11 = g02
    inverse = lambda d, scale: jnp.where(d > PIVOT * scale, 1.0 / d, 0.0)
    i0 = inverse(g00, 0.0 * g00)
    l10, l20 = g01 * i0, g02 * i0
    i1 = inverse(g11 - l10 * g01, g11)
    e = g12 - l10 * g02
    l21 = e * i1
    i2 = inverse(g22 - l20 * g02 - l21 * e, g22)
    c0 = mu[0]
    c1 = mu[1] - l10 * c0
    c2 = mu[2] - l20 * c0 - l21 * c1
    y2 = c2 * i2
    y1 = c1 * i1 - l21 * y2
    y0 = c0 * i0 - l10 * y1 - l20 * y2
    return y0, y1, y2


def coefficients(rows):
    total = jnp.sum(rows[...], axis=0, keepdims=True)
    at = lambda k: jnp.broadcast_to(total[:, k : k + 1], (1, 128))
    y = solve([at(k) for k in range(6)])
    c = (1.0, *y)
    mu = []
    for k in range(6):
        m = 0.0
        for i, (a, b) in enumerate(PAIRS):
            w = c[a] * c[b] * (1.0 if a == b else 2.0)
            m = m + w * at(6 + 10 * k + i)
        mu.append(m)
    v = solve(mu)
    scalar = lambda x: x[0, 0]
    return [scalar(x) for x in y], [[scalar(x * c[g]) for g in range(GENS)] for x in v]


def around(v, x, cx, cy, cz):
    c = v[x]
    y, z = cy[x], cz[x]
    return (
        cx[x] * v[x + 1]
        + cx[x - 1] * v[x - 1]
        + y * up_y(c)
        + dn_y(y * c)
        + z * up_z(c)
        + dn_z(z * c)
    )


def pressure_chain(start, p, cx, cy, cz, inv, t, n, part):
    def first(x):
        r = start(x) + around(p, x, cx, cy, cz)
        return [(n, (0, x), r), (t, (0, x), inv[x] * r)]

    loop(1, XE - 1, first, PW)
    for i in (1, 2):

        def follow(x):
            r = around(t.at[i - 1], x, cx, cy, cz)
            return [(n, (i, x), r), (t, (i, x), inv[x] * r)]

        loop(1 + i, XE - 1 - i, follow, PW)

    def final(x):
        return [(n, (3, x), around(t.at[2], x, cx, cy, cz))]

    loop(LOW, LOW + NX, final, PW)

    def body(x, acc):
        s = [t[i, LOW + x, 8:24] for i in range(3)]
        q = [n[i, LOW + x, 8:24] for i in range(4)]
        return tuple(v + s[i] * q[j] for v, (i, j) in zip(acc, LEVELS))

    sums = lax.fori_loop(0, NX, body, (jnp.zeros((NY, NZ), F32),) * 6)
    at = lax.broadcasted_iota(jnp.int32, (8, 128), 1)
    row = jnp.zeros((8, 128), F32)
    for k, v in enumerate(sums):
        row = jnp.where(at == k, jnp.sum(v), row)
    part[...] = row


def pressure_first_kernel(
    flags, mats, ids, p, f, low, high, yl, yh,
    code, pe, coef, t, part,
    fe, perm, stor, stab, n,
):
    cx, cy, cz, inv, diag, base, biot = (coef.at[i] for i in range(7))
    fill(code, XE, LOW, ids, low, high, (0, 0), yl, yh, 0, flags)
    fill(pe, XE, LOW, p, low, high, (7, 6), yl, yh, 21, flags)
    fill(fe.at[1:20], XE - 2, LOW - 1, f, low, high, (14, 12), yl, yh, 42, None)

    def tables(x):
        l, s, k, st, bi = lookup(code[x], mats, range(5))
        bi = 0.25 * bi
        st2 = bi * bi / jnp.maximum(l + (2.0 / 3.0) * s, 1e-30)
        return [(perm, x, k), (stor, x, st), (biot, x, bi), (stab, x, st2)]

    loop(0, XE, tables)

    def faces(x):
        k = perm[x]

        def harmonic(other):
            return (2.0 * DT) * k * other / jnp.maximum(k + other, 1e-30)

        return [
            (cx, x, harmonic(perm[x + 1])),
            (cy, x, harmonic(up_y(k))),
            (cz, x, harmonic(up_z(k))),
        ]

    loop(0, XE - 1, faces, 2)

    def diagonal(x):
        y, z = cy[x], cz[x]
        flow = cx[x] + cx[x - 1] + y + dn_y(y) + z + dn_z(z)
        inside = code[x] > 0.5
        d = stor[x] + stab[x] + flow
        return [
            (inv, x, jnp.where(inside, 1.0 / jnp.where(inside, d, 1.0), 0.0)),
            (diag, x, stab[x] - d),
            (base, x, stor[x] * pe[x] + DT * fe[x]),
        ]

    loop(1, XE - 1, diagonal, 2)
    pressure_chain(lambda x: base[x] + diag[x] * pe[x], pe, cx, cy, cz, inv, t, n, part)


def pressure_next_kernel(
    flags, coef, p, du, uo, low, high, yl, yh,
    pe, ue, t, part,
    de, n,
):
    cx, cy, cz, inv, diag, base, biot = (coef.at[i] for i in range(7))
    edge = lambda x, n: flags[0] if x < n else flags[1]
    zero = jnp.zeros((2, NZ), F32)
    for a in range(3):
        for x in range(20):
            k = 6 * (20 * a + x)
            out = de.at[a, x + 1]
            lo, hi = yl[k : k + 6] * flags[2], yh[k : k + 6] * flags[3]
            if 5 <= x < 15:
                out[4:28] = du[a, x - 5]
            else:
                outer = edge(x, 5)
                lo, hi = lo * outer, hi * outer
                ref = low.at[5 * a + x] if x < 5 else high.at[5 * a + x - 15]
                out[8:24] = ref[...] * outer
            if not 6 <= x < 14:
                lo, hi = lo * edge(x, 6), hi * edge(x, 6)
            out[0:2] = zero
            out[2:8] = lo
            out[24:30] = hi
            out[30:32] = zero
    for x in range(XE):
        k = 360 + 8 * x
        lo, hi = yl[k : k + 8] * flags[2], yh[k : k + 8] * flags[3]
        if not LOW <= x < LOW + NX:
            lo, hi = lo * edge(x, LOW), hi * edge(x, LOW)
        if 3 <= x < 18:
            pe[x, 8:24] = p[x - 3, 8:24]
        else:
            ref = low.at[15 + x] if x < 3 else high.at[15 + x - 18]
            pe[x, 8:24] = ref[...] * edge(x, LOW)
        pe[x, 0:8] = lo
        pe[x, 24:32] = hi

    def start(x):
        c2 = de[2, x]
        div = (
            de[0, x + 1] - de[0, x]
            + up_y(de[1, x]) - de[1, x]
            + up_z(c2) - c2
        )
        return base[x] - biot[x] * div + diag[x] * pe[x]

    pressure_chain(start, pe, cx, cy, cz, inv, t, n, part)
    for a in range(3):
        for m in range(ME):
            ue[a, m] = uo[a, m] + de[a, m + MO, 4:28]


def mech_chain(u, bf, pe, t, biot, mc, kept, q, load, carry, acc, s, part_p, part):
    sx, sy, sz, diag, lame, h0, h1, h2, kk = (mc.at[i] for i in range(9))
    h = (h0, h1, h2)

    def loads(m):
        x = m + MO
        bi = biot[x, 4:28]
        fields = [pe[x, 4:28]] + [t[i, x, 4:28] for i in range(3)]
        return [(load, (g, m), bi * v) for g, v in enumerate(fields)]

    loop(0, ME - 1, loads, 2)

    def ups(w, m):
        return (w[0, m + 1], up_y(w[1, m]), up_z(w[2, m]))

    def precondition(r, m):
        hs = [h[a][m] for a in range(3)]
        scaled = [r[a] * hs[a] for a in range(3)]
        k = kk[m] * (scaled[0] + scaled[1] + scaled[2])
        return [scaled[a] - hs[a] * k for a in range(3)]

    def pull(m):
        p = ups(u, m)
        return lame[m] * (p[0] + p[1] + p[2] - (u[0, m] + u[1, m] + u[2, m]))

    carry[0] = load[0, 0] - pull(0)

    def own(m):
        return jnp.where((m >= ML) & (m < ML + NX), m - ML, NX)

    def near(m):
        return jnp.where((m >= ML - 1) & (m <= ML + NX), m - ML + 1, NX + 2)

    def residual(m):
        for g in range(GENS):
            if g == 0:
                c = load[0, m] - pull(m)
                below = carry[0]
                d = diag[m]
                r = [
                    bf[a, m] - d * u[a, m] + around(u.at[a], m, sx, sy, sz) for a in range(3)
                ]
            else:
                c = load[g, m]
                below = load[g, m - 1]
                r = [0.0, 0.0, 0.0]
            low = (below, dn_y(c), dn_z(c))
            r = [r[a] + (low[a] - c) for a in range(3)]
            if g == 0:
                yield carry, 0, c
            z = precondition(r, m)
            for a in range(3):
                yield q, (0, g, a, own(m)), r[a]
                yield s, (0, g, a, m), z[a]
                yield kept, (g * 3 + a, near(m)), z[a]

    loop(1, ME - 1, residual)

    def basis(i, g):
        if i < 2:
            return s.at[i, g], 0
        k = (i * GENS + g) * 3
        return kept.at[k : k + 3], ML - 1

    def parts(w, m, o):
        c = [w[a, m - o] for a in range(3)]
        p = (w[0, m + 1 - o], up_y(c[1]), up_z(c[2]))
        total = p[0] + p[1] + p[2]
        l = lame[m]
        e = (c[0] + c[1] + c[2]) - total
        x, y, z = sx[m], sy[m], sz[m]
        above = x * c[0] + l * (p[0] + e)
        r = [
            x * p[0],
            y * p[1] + dn_y(y * c[1] + l * (p[1] + e)),
            z * p[2] + dn_z(z * c[2] + l * (p[2] + e)),
        ]
        return c, r, l * total, above

    for i in (1, 2, 3):
        for g in range(GENS):
            w, o = basis(i - 1, g)
            carry[g] = parts(w, i, o)[3]

        def follow(m):
            for g in range(GENS):
                w, o = basis(i - 1, g)
                c, r, push, above = parts(w, m, o)
                below = carry[g]
                yield carry, g, above
                x, xb, y, z = sx[m], sx[m - 1], sy[m], sz[m]
                r[0] = r[0] + push + below + (y * up_y(c[0]) + dn_y(y * c[0])) + (
                    z * up_z(c[0]) + dn_z(z * c[0])
                )
                r[1] = r[1] + push + (x * w[1, m + 1 - o] + xb * w[1, m - 1 - o]) + (
                    z * up_z(c[1]) + dn_z(z * c[1])
                )
                r[2] = r[2] + push + (x * w[2, m + 1 - o] + xb * w[2, m - 1 - o]) + (
                    y * up_y(c[2]) + dn_y(y * c[2])
                )
                slot = own(m) if i < 3 else m - ML
                for a in range(3):
                    yield q, (i, g, a, slot), r[a]
                if i < 3:
                    v = precondition(r, m)
                    for a in range(3):
                        if i == 1:
                            yield s, (i, g, a, m), v[a]
                        yield kept, ((i * GENS + g) * 3 + a, near(m)), v[a]

        loop(1 + i, ME - 1 - i, follow)

    top = lax.broadcasted_iota(jnp.int32, (8, NZ), 0) >= 4
    for k, (i, j) in enumerate(LEVELS):

        def body(x, sums):
            sums = list(sums)
            for a in range(3):
                v = [kept[(i * GENS + g) * 3 + a, 1 + x] for g in range(GENS)]
                w = [q[j, g, a, x] for g in range(GENS)]
                for pick_rows in (
                    lambda f: f[8:16],
                    lambda f: jnp.where(top, f[0:8], f[16:24]),
                ):
                    vt, wt = [pick_rows(f) for f in v], [pick_rows(f) for f in w]
                    sums = [c + vt[g] * wt[o] for c, (g, o) in zip(sums, PAIRS)]
            return tuple(sums)

        sums = lax.fori_loop(0, NX, body, (jnp.zeros((8, NZ), F32),) * len(PAIRS))
        for n, v in enumerate(sums):
            acc[10 * k + n] = v
    at = lax.broadcasted_iota(jnp.int32, (8, 128), 1)
    row = part_p[...]
    for k in range(60):
        row = jnp.where(at == k + 6, jnp.sum(acc[k]), row)
    for i in range(0, 128, 8):
        part[i : i + 8] = row


def mech_first_kernel(
    flags, mats, part_p, code, pe, coef, t, u, b, low, high, yl, yh,
    ue, be, mc, kept, part,
    q, load, shear, carry, acc, s,
):
    sx, sy, sz, diag, lame, h0, h1, h2, kk = (mc.at[i] for i in range(9))
    for a in range(3):
        fill_mech(ue.at[a], 16, 4, u.at[a], low, high, (4 * a, 4 * a), yl, yh, 8 * a, flags, 0)
        fill_mech(be.at[a], 14, 3, b.at[a], low, high, (12 + 3 * a, 12 + 3 * a), yl, yh, 24 + 7 * a, None, 1)

    def tables(m):
        l, g = lookup(code[m + MO, 4:28], mats, (0, 1))
        return [(lame, m, l), (shear, m, g)]

    loop(0, ME, tables)

    def faces(m):
        g = shear[m]
        return [
            (sx, m, 0.5 * (g + shear[m + 1])),
            (sy, m, 0.5 * (g + up_y(g))),
            (sz, m, 0.5 * (g + up_z(g))),
        ]

    loop(0, ME - 1, faces, 2)

    def diagonal(m):
        g, l = shear[m], lame[m]
        near = (
            shear[m + 1] + shear[m - 1] + up_y(g) + dn_y(g)
            + up_z(g) + dn_z(g)
        )
        d = 3.0 * g + 0.5 * near
        inside = g > 0.0
        lows = (lame[m - 1], dn_y(l), dn_z(l))
        hs = [jnp.where(inside, 1.0 / jnp.where(inside, d + v, 1.0), 0.0) for v in lows]
        k = l / (1.0 + l * (hs[0] + hs[1] + hs[2]))
        return [(diag, m, d), (h0, m, hs[0]), (h1, m, hs[1]), (h2, m, hs[2]), (kk, m, k)]

    loop(1, ME - 1, diagonal, 2)
    mech_chain(ue, be, pe, t, coef.at[6], mc, kept, q, load, carry, acc, s, part_p, part)


def mech_next_kernel(
    part_p, pe, coef, t, ue, be, mc,
    kept, part,
    q, load, carry, acc, s,
):
    mech_chain(ue, be, pe, t, coef.at[6], mc, kept, q, load, carry, acc, s, part_p, part)


def combine(v, kept, a, x):
    total = 0.0
    for i in range(3):
        for g in range(GENS):
            total = total + v[i][g] * kept[(i * GENS + g) * 3 + a, x]
    return total


def change_kernel(rows, t, pe, kept, u, du, pnew, unew, up, dn):
    y, v = coefficients(rows)
    for k in range(PK):
        x = k + MO
        w = pe[x] + (y[0] * t[0, x] + y[1] * t[1, x] + y[2] * t[2, x])
        pnew[k] = w
        i = k - ML
        if 1 <= i <= 3:
            up[14 + i] = w[8:24]
        if 3 <= i <= 5:
            dn[12 + i] = w[8:24]
    for a in range(3):
        for k in range(NX + 2):
            d = combine(v, kept, a, k)
            du[a, k] = d
            i = k - 1
            if 0 <= i < NX:
                unew[a, i] = u[a, i] + d[4:20]
            if 2 <= i <= 6:
                up[5 * a + i - 2] = d[4:20]
            if 1 <= i <= 5:
                dn[5 * a + i - 1] = d[4:20]


def pack_change_kernel(du, p, low, high, up, dn):
    for a in range(3):
        for x in range(20):
            if x < 5:
                ref, r = low.at[5 * a + x], 0
            elif x < 15:
                ref, r = du.at[a, x - 5], 4
            else:
                ref, r = high.at[5 * a + x - 15], 0
            k = 6 * (20 * a + x)
            up[k : k + 6] = ref[r + 10 : r + 16]
            dn[k : k + 6] = ref[r : r + 6]
    for x in range(XE):
        if x < 3:
            ref, r = low.at[15 + x], 0
        elif x < 18:
            ref, r = p.at[x - 3], 8
        else:
            ref, r = high.at[15 + x - 18], 0
        k = 360 + 8 * x
        up[k : k + 8] = ref[r + 8 : r + 16]
        dn[k : k + 8] = ref[r : r + 8]


def finish_kernel(rows, t, p, kept, u, unew, pnew):
    y, v = coefficients(rows)
    for x in range(NX):
        k = x + LOW
        w = p[k, 8:24] + (y[0] * t[0, k, 8:24] + y[1] * t[1, k, 8:24] + y[2] * t[2, k, 8:24])
        pnew[x] = w
        for a in range(3):
            unew[a, x] = u[a, x] + combine(v, kept, a, x + 1)[4:20]


def call(kernel, name, ins, outs, scratch=(), specs=None, cost=0, limit=12):
    return pl.pallas_call(
        kernel,
        name=name,
        out_shape=[jax.ShapeDtypeStruct(o, F32) for o in outs],
        in_specs=specs or [VM] * len(ins),
        out_specs=[VM] * len(outs),
        scratch_shapes=[pltpu.VMEM(s, F32) if isinstance(s, tuple) else s for s in scratch],
        compiler_params=pltpu.CompilerParams(vmem_limit_bytes=limit * 2**20),
        cost_estimate=pl.CostEstimate(flops=cost, bytes_accessed=0, transcendentals=0) if cost else None,
    )(*ins)


def neighbours(axis, size, up, dn):
    ring = [(i, (i + 1) % size) for i in range(size)]
    return lax.ppermute(up, axis, ring), lax.ppermute(dn, axis, [(b, a) for a, b in ring])


def gather_rows(part):
    return lax.all_to_all(part, ("gx", "gy"), 0, 0, tiled=True)


def on_device(gx_size, gy_size, u, p, b, f, ids, mats):
    gx, gy = lax.axis_index("gx"), lax.axis_index("gy")
    flags = jnp.stack([gx > 0, gx < gx_size - 1, gy > 0, gy < gy_size - 1]).astype(F32)
    wide, mech = (YE, NZ), (YM, NZ)
    up_p, dn_p, up_m, dn_m, own_code, own_p, own_f = call(
        pack_x_kernel,
        "pack_x",
        [pltpu.with_memory_space_constraint(v, pltpu.HBM) for v in (ids, p, f, u, b)],
        [(20, NY, NZ), (17, NY, NZ), (21, NY, NZ), (21, NY, NZ)] + [(NX, NY, NZ)] * 3,
        [pltpu.VMEM((NX, NY, NZ), jnp.int32), pltpu.SemaphoreType.DMA((19,))],
        [HB] * 5,
    )
    low_p, high_p = neighbours("gx", gx_size, up_p, dn_p)
    low_m, high_m = neighbours("gx", gx_size, up_m, dn_m)
    up, dn = call(
        pack_y_pressure_kernel, "pack_yp", (own_code, own_p, own_f, low_p, high_p), [(61, 8, NZ), (61, 8, NZ)], limit=4
    )
    yl_p, yh_p = neighbours("gy", gy_size, up, dn)
    up, dn = call(pack_y_mech_kernel, "pack_ym", (u, b, low_m, high_m), [(45, 8, NZ), (45, 8, NZ)], limit=4)
    yl_m, yh_m = neighbours("gy", gy_size, up, dn)
    code, pe, coef, t, part_p = call(
        pressure_first_kernel,
        "pressure_first",
        (flags, mats, own_code, own_p, own_f, low_p, high_p, yl_p, yh_p),
        [(XE, *wide), (XE, *wide), (7, XE, *wide), (3, XE, *wide), (8, 128)],
        [(XE, *wide)] * 4 + [(4, XE, *wide)],
        [SM, SM] + [VM] * 7,
        COST,
    )
    mech_scratch = [
        (4, GENS, 3, NX + 1, *mech),
        (GENS, ME, *mech),
        (GENS, *mech),
        (60, 8, NZ),
        (2, GENS, 3, ME, *mech),
    ]
    basis = (9 * GENS, NX + 3, *mech)
    ue, be, mc, s, part = call(
        mech_first_kernel,
        "mech_first",
        (flags, mats, part_p, code, pe, coef, t, u, b, low_m, high_m, yl_m, yh_m),
        [(3, ME, *mech), (3, ME, *mech), (9, ME, *mech), basis, (128, 128)],
        mech_scratch[:2] + [(ME, *mech)] + mech_scratch[2:],
        [SM, SM] + [VM] * 11,
        COST,
        24,
    )
    rows = gather_rows(part)
    du, p1, u1, up, dn = call(
        change_kernel,
        "change",
        (rows, t, pe, s, u),
        [(3, NX + 2, *mech), (PK, *wide), (3, NX, NY, NZ), (18, NY, NZ), (18, NY, NZ)],
    )
    low, high = neighbours("gx", gx_size, up, dn)
    up, dn = call(pack_change_kernel, "pack_change", (du, p1, low, high), [(528, NZ), (528, NZ)])
    yl, yh = neighbours("gy", gy_size, up, dn)
    pe, ue, t, part_p = call(
        pressure_next_kernel,
        "pressure_next",
        (flags, coef, p1, du, ue, low, high, yl, yh),
        [(XE, *wide), (3, ME, *mech), (3, XE, *wide), (8, 128)],
        [(3, XE, *wide), (4, XE, *wide)],
        [SM] + [VM] * 8,
        COST,
    )
    s, part = call(
        mech_next_kernel,
        "mech_next",
        (part_p, pe, coef, t, ue, be, mc),
        [basis, (128, 128)],
        mech_scratch,
        None,
        COST,
        24,
    )
    rows = gather_rows(part)
    u2, p2 = call(
        finish_kernel,
        "finish",
        (rows, t, pe, s, u1),
        [(3, NX, NY, NZ), (NX, NY, NZ)],
    )
    return u2, p2


def solution(mesh):
    body = functools.partial(on_device, mesh.shape["gx"], mesh.shape["gy"])
    field, vector = P("gx", "gy", None), P(None, "gx", "gy", None)
    return jax.shard_map(
        body,
        mesh=mesh,
        in_specs=(vector, field, vector, field, field, P()),
        out_specs=(vector, field),
        check_vma=False,
    )
```

time: 192 us -> 141 us (0.73)
  blocking collectives: 62.6 us -> 36.1 us
  waiting for transfers between devices: 46.3 us -> 23 us
  starting transfers between devices: 16.1 us -> 24.2 us
  local copies, waits for them, and re-layouts: 5.99 us -> 0.01 us
  Pallas kernels: 59.8 us -> 56.7 us
    all_to_all x4 -> x2, blocking collectives: 62.6 us -> 36.1 us  [gather_rows(): return lax.all_to_all(part, ('gx', 'gy'), 0, 0, tiled=True)]
    ppermute x4 -> x6, waiting for transfers between devices: 25.3 us -> 5.3 us  [neighbours(): lax.ppermute(dn, axis, [(b, a) for a, b in ring])]
    unnamed x26 -> x6, local copies, waits for them, and re-layouts: 5.99 us -> 0.01 us
    ppermute x4 -> x6, starting transfers between devices: 9.31 us -> 14.1 us  [neighbours(): lax.ppermute(dn, axis, [(b, a) for a, b in ring])]
    ppermute x4 -> x6, waiting for transfers between devices: 21 us -> 17.7 us  [neighbours(): lax.ppermute(up, axis, ring)]
    ppermute x4 -> x6, starting transfers between devices: 6.78 us -> 10.1 us  [neighbours(): lax.ppermute(up, axis, ring)]
    pallas_call x9 -> x10, Pallas kernels: 59.8 us -> 56.7 us  [call(): pl.pallas_call(kernel, name=name, out_shape=[jax.ShapeDtypeStruct(o, F32)...]
  transfers between devices with their start and end apart: 8 -> 12, of which waited for: 8 -> 7; matrix products, arithmetic and copies ran while one was open for 0% -> 0% of each run, Pallas kernels for 0% -> 6%
where the time goes in v2:
time: 141 us
  Pallas kernels  56.7 us (40%)
  blocking collectives  36.1 us (26%)
  starting transfers between devices  24.2 us (17%)
  waiting for transfers between devices  23 us (16%)
    pallas_call x10, Pallas kernels, call(): pl.pallas_call(kernel, name=name, out_shape=[jax.ShapeDtypeStruct(o, F32)...  56.7 us
    all_to_all x2, blocking collectives, gather_rows(): return lax.all_to_all(part, ('gx', 'gy'), 0, 0, tiled=True)  36.1 us
    ppermute x6, waiting for transfers between devices, neighbours(): lax.ppermute(up, axis, ring)  17.7 us
    ppermute x6, starting transfers between devices, neighbours(): lax.ppermute(dn, axis, [(b, a) for a, b in ring])  14.1 us
    ppermute x6, starting transfers between devices, neighbours(): lax.ppermute(up, axis, ring)  10.1 us
    ppermute x6, waiting for transfers between devices, neighbours(): lax.ppermute(dn, axis, [(b, a) for a, b in ring])  5.3 us
  transfers between devices with their start and end apart: 12, of which 7 were waited for; matrix products, arithmetic and copies ran while one was open for 0% of the time, Pallas kernels for 6%

profile of v2, /device:TPU:1, one launch (start us, length us, event | category | flops | bytes accessed | tf_op | source)
XLA Modules:
  0.0 140.7 jit_solution(10071603430709966294)
XLA Ops:
  0.7 1.6 %pack_x.1 = (f32[20,16,256]{2,1,0:T(8,128)S(1)}, f32[17,16,256]{2,1,0:T(8,128)S(1)}, f32[21,16,256]{2,1,0:T(8,128)S(1)}, f32[21,16,256]{2,1,0:T(8,128)S(1)}, f32...) custom-call(s32[8,16,256]{2,1,0:T(8,128)} %ids.1, f32[8,16,256]{2,1,0:T(8,128)} %p.1, ...), custom_call_target="tpu_custom_call" | custom-call | tf_op jit(solution)/shard_map/pack_x/pallas_call | solution.py:615
  2.3 2.1 %collective-permute-start = (f32[20,16,256]{2,1,0:T(8,128)S(1)}, f32[20,16,256]{2,1,0:T(8,128)S(1)}, u32[]{:S(2)}, u32[]{:S(2)}) collective-permute-start(f32[20,16,256]{2,1,0:T(8,128)S(1)} %get-tuple-element.39), channel_id=1, source_target_pairs={{0,8},{8,16},{16,24},{24,32},{32,40},{40,48},{48,56},{56,64},{64,7... | collective-permute-start | bytes 983048 | tf_op jit(solution)/shard_map/ppermute | solution.py:629
  4.4 4.8 %collective-permute-start.1 = (f32[17,16,256]{2,1,0:T(8,128)S(1)}, f32[17,16,256]{2,1,0:T(8,128)S(1)}, u32[]{:S(2)}, u32[]{:S(2)}) collective-permute-start(f32[17,16,256]{2,1,0:T(8,128)S(1)} %get-tuple-element.40), channel_id=1, source_target_pairs={{8,0},{16,8},{24,16},{32,24},{40,32},{48,40},{56,48},{64,56},{72,6... | collective-permute-start | bytes 835592 | tf_op jit(solution)/shard_map/ppermute | solution.py:629
  9.2 4.8 %collective-permute-start.5 = (f32[21,16,256]{2,1,0:T(8,128)S(1)}, f32[21,16,256]{2,1,0:T(8,128)S(1)}, u32[]{:S(2)}, u32[]{:S(2)}) collective-permute-start(f32[21,16,256]{2,1,0:T(8,128)S(1)} %get-tuple-element.49), channel_id=1, source_target_pairs={{8,0},{16,8},{24,16},{32,24},{40,32},{48,40},{56,48},{64,56},{72,6... | collective-permute-start | bytes 1032200 | tf_op jit(solution)/shard_map/ppermute | solution.py:629
  14.0 0.6 collective-permute-done.1.high
  14.5 2.0 %collective-permute-done.low = f32[20,16,256]{2,1,0:T(8,128)S(1)} collective-permute-done((f32[20,16,256]{2,1,0:T(8,128)S(1)}, f32[20,16,256]{2,1,0:T(8,128)S(1)}, u32[]{:S(2)}, u32[]{:S(2)}) %collective-permute-start) | collective-permute-done | bytes 327712 | tf_op jit(solution)/shard_map/ppermute | solution.py:629
  16.5 1.0 pack_yp.1
  17.6 3.3 %collective-permute-start.2 = (f32[61,8,256]{2,1,0:T(8,128)}, f32[61,8,256]{2,1,0:T(8,128)S(1)}, u32[]{:S(2)}, u32[]{:S(2)}) collective-permute-start(f32[61,8,256]{2,1,0:T(8,128)} %get-tuple-element.41), channel_id=1, source_target_pairs={{0,1},{1,2},{2,3},{3,4},{4,5},{5,6},{6,7},{7,0},{8,9},{9,10},{10,1... | collective-permute-start | bytes 1499144 | tf_op jit(solution)/shard_map/ppermute | solution.py:629
  20.9 3.0 %collective-permute-done.4.low = f32[21,16,256]{2,1,0:T(8,128)S(1)} collective-permute-done((f32[21,16,256]{2,1,0:T(8,128)S(1)}, f32[21,16,256]{2,1,0:T(8,128)S(1)}, u32[]{:S(2)}, u32[]{:S(2)}) %collective-permute-start.4) | collective-permute-done | bytes 344096 | tf_op jit(solution)/shard_map/ppermute | solution.py:629
  23.9 1.0 pack_ym.1
  24.9 2.4 %collective-permute-start.6 = (f32[45,8,256]{2,1,0:T(8,128)}, f32[45,8,256]{2,1,0:T(8,128)}, u32[]{:S(2)}, u32[]{:S(2)}) collective-permute-start(f32[45,8,256]{2,1,0:T(8,128)} %get-tuple-element.50), channel_id=1, source_target_pairs={{0,1},{1,2},{2,3},{3,4},{4,5},{5,6},{6,7},{7,0},{8,9},{9,10},{10,1... | collective-permute-start | bytes 1105928 | tf_op jit(solution)/shard_map/ppermute | solution.py:629
  27.4 0.0 collective-permute-start.7
  27.4 0.1 add_convert_fusion.flags
  27.5 2.0 %collective-permute-done.3.yh = f32[61,8,256]{2,1,0:T(8,128)S(1)} collective-permute-done((f32[61,8,256]{2,1,0:T(8,128)}, f32[61,8,256]{2,1,0:T(8,128)S(1)}, u32[]{:S(2)}, u32[]{:S(2)}) %collective-permute-start.3) | collective-permute-done | bytes 499744 | tf_op jit(solution)/shard_map/ppermute | solution.py:629
  29.4 7.0 %pressure_first.1 = (f32[21,32,256]{2,1,0:T(8,128)S(1)}, f32[21,32,256]{2,1,0:T(8,128)S(1)}, f32[7,21,32,256]{3,2,1,0:T(8,128)S(1)}, f32[3,21,32,256]{3,2,1,0:T(8,128)S(1)}, f32[8,128]{1,0:T(8,128)S(1)}) custom-call(f32[4]{0:T(128)S(1)} %add_convert_fusion.flags, f32[5,8]{1,0:T(8,128)S(1)} %copy-done.2, f32[8,16,256]{2,1,0:T(8,128)S(1)} %get-tuple-element.36.ids, ...), custom_call_target="tpu_custom_call" | custom-call | flops 200000000 | tf_op jit(solution)/shard_map/pressure_first/pallas_call | solution.py:615
  36.4 0.0 collective-permute-done.6.yl
  36.4 0.0 collective-permute-done.7.yh
  36.5 21.2 %mech_first.1 = (f32[3,16,24,256]{3,2,1,0:T(8,128)S(1)}, f32[3,16,24,256]{3,2,1,0:T(8,128)S(1)}, f32[9,16,24,256]{3,2,1,0:T(8,128)S(1)}, f32[36,11,24,256]{3,2,1,0:T(8,128)S(1)}, f32[128,128]{1,0:T(8,128)S(1)}) custom-call(f32[4]{0:T(128)S(1)} %add_convert_fusion.flags, f32[5,8]{1,0:T(8,128)S(1)} %copy-done.2, f32[8,128]{1,0:T(8,128)S(1)} %get-tuple-element.44.part_p, ...), custom_call_target="tpu_custom_call" | custom-call | flops 200000000 | tf_op jit(solution)/shard_map/mech_first/pallas_call | solution.py:615
  57.7 17.6 %all_to_all.22 = f32[128,1,128]{2,1,0:T(1,128)S(1)} all-to-all(f32[128,1,128]{2,1,0:T(1,128)S(1)} %bitcast.14), channel_id=1, replica_groups=mesh['gx'=16,'gy'=8] {'gx','gy'}, dimensions={0} | all-to-all | bytes 131072 | tf_op jit(solution)/shard_map/all_to_all | solution.py:633
  75.3 1.4 change.1
  76.7 0.4 collective-permute-start.8
  77.1 4.5 %collective-permute-start.9 = (f32[18,16,256]{2,1,0:T(8,128)S(1)}, f32[18,16,256]{2,1,0:T(8,128)S(1)}, u32[]{:S(2)}, u32[]{:S(2)}) collective-permute-start(f32[18,16,256]{2,1,0:T(8,128)S(1)} %get-tuple-element.58), channel_id=1, source_target_pairs={{8,0},{16,8},{24,16},{32,24},{40,32},{48,40},{56,48},{64,56},{72,6... | collective-permute-start | bytes 884744 | tf_op jit(solution)/shard_map/ppermute | solution.py:629
  81.5 6.3 %collective-permute-done.8.low = f32[18,16,256]{2,1,0:T(8,128)S(1)} collective-permute-done((f32[18,16,256]{2,1,0:T(8,128)S(1)}, f32[18,16,256]{2,1,0:T(8,128)S(1)}, u32[]{:S(2)}, u32[]{:S(2)}) %collective-permute-start.8) | collective-permute-done | bytes 294944 | tf_op jit(solution)/shard_map/ppermute | solution.py:629
  87.9 0.0 collective-permute-done.9.high
  87.9 0.2 pack_change.1
  88.1 1.9 %collective-permute-start.10 = (f32[528,256]{1,0:T(8,128)S(1)}, f32[528,256]{1,0:T(8,128)S(1)}, u32[]{:S(2)}, u32[]{:S(2)}) collective-permute-start(f32[528,256]{1,0:T(8,128)S(1)} %get-tuple-element.59), channel_id=1, source_target_pairs={{0,1},{1,2},{2,3},{3,4},{4,5},{5,6},{6,7},{7,0},{8,9},{9,10},{10,1... | collective-permute-start | bytes 1622024 | tf_op jit(solution)/shard_map/ppermute | solution.py:629
  89.9 6.3 %collective-permute-done.10.yl = f32[528,256]{1,0:T(8,128)S(1)} collective-permute-done((f32[528,256]{1,0:T(8,128)S(1)}, f32[528,256]{1,0:T(8,128)S(1)}, u32[]{:S(2)}, u32[]{:S(2)}) %collective-permute-start.10) | collective-permute-done | bytes 540704 | tf_op jit(solution)/shard_map/ppermute | solution.py:629
  96.2 2.8 %collective-permute-done.11.yh = f32[528,256]{1,0:T(8,128)S(1)} collective-permute-done((f32[528,256]{1,0:T(8,128)S(1)}, f32[528,256]{1,0:T(8,128)S(1)}, u32[]{:S(2)}, u32[]{:S(2)}) %collective-permute-start.11) | collective-permute-done | bytes 540704 | tf_op jit(solution)/shard_map/ppermute | solution.py:629
  99.0 4.0 %pressure_next.1 = (f32[21,32,256]{2,1,0:T(8,128)S(1)}, f32[3,16,24,256]{3,2,1,0:T(8,128)S(1)}, f32[3,21,32,256]{3,2,1,0:T(8,128)S(1)}, f32[8,128]{1,0:T(8,128)S(1)}) custom-call(f32[4]{0:T(128)S(1)} %add_convert_fusion.flags, f32[7,21,32,256]{3,2,1,0:T(8,128)S(1)} %get-tuple-element.43.coef, f32[15,32,256]{2,1,0:T(8,128)S(1)} %get-tuple-element.54.p, ...), custom_call_target="tpu_custom_call" | custom-call | flops 200000000 | tf_op jit(solution)/shard_map/pressure_next/pallas_call | solution.py:615
  103.0 17.7 %mech_next.1 = (f32[36,11,24,256]{3,2,1,0:T(8,128)S(1)}, f32[128,128]{1,0:T(8,128)S(1)}) custom-call(f32[8,128]{1,0:T(8,128)S(1)} %get-tuple-element.61.part_p, f32[21,32,256]{2,1,0:T(8,128)S(1)} %get-tuple-element.62.pe.p, f32[7,21,32,256]{3,2,1,0:T(8,128)S(1)} %get-tuple-element.43.coef, f32[3,21,32,256]{3,2,1,0:T(8,128)S(1)} %get-tuple-element.63.t, ...), custom_call_target="tpu_custom_call" | custom-call | flops 200000000 | tf_op jit(solution)/shard_map/mech_next/pallas_call | solution.py:615
  120.7 18.4 %all_to_all.23 = f32[128,1,128]{2,1,0:T(1,128)S(1)} all-to-all(f32[128,1,128]{2,1,0:T(1,128)S(1)} %bitcast.15), channel_id=1, replica_groups=mesh['gx'=16,'gy'=8] {'gx','gy'}, dimensions={0} | all-to-all | bytes 131072 | tf_op jit(solution)/shard_map/all_to_all | solution.py:633
  139.2 1.6 %finish.1 = (f32[3,8,16,256]{3,2,1,0:T(8,128)}, f32[8,16,256]{2,1,0:T(8,128)}) custom-call(f32[128,128]{1,0:T(8,128)S(1)} %bitcast.13, f32[3,21,32,256]{3,2,1,0:T(8,128)S(1)} %get-tuple-element.63.t, f32[21,32,256]{2,1,0:T(8,128)S(1)} %get-tuple-element.62.pe.p, f32[36,11,24,256]{3,2,1,0:T(8,128)S(1)} %get-tuple-element.68.kept, ...), custom_call_target="tpu_custom_call" | custom-call | tf_op jit(solution)/shard_map/finish/pallas_call | solution.py:615
  (11 shorter events, 0.0 us)
Async XLA Ops:
  0.6 23.3 %copy-start = (f32[3,8,16,256]{3,2,1,0:T(8,128)S(1)}, f32[3,8,16,256]{3,2,1,0:T(8,128)}, u32[]{:S(2)}) copy-start(f32[3,8,16,256]{3,2,1,0:T(8,128)} %u.7) | copy-start | bytes 1179652
  0.6 23.3 %copy-start.1 = (f32[3,8,16,256]{3,2,1,0:T(8,128)S(1)}, f32[3,8,16,256]{3,2,1,0:T(8,128)}, u32[]{:S(2)}) copy-start(f32[3,8,16,256]{3,2,1,0:T(8,128)} %b.5) | copy-start | bytes 1179652
  0.7 28.8 %copy-start.2 = (f32[5,8]{1,0:T(8,128)S(1)}, f32[5,8]{1,0:T(8,128)}, u32[]{:S(2)}) copy-start(f32[5,8]{1,0:T(8,128)} %mats.3) | copy-start | bytes 484
  2.3 14.3 %collective-permute-start = (f32[20,16,256]{2,1,0:T(8,128)S(1)}, f32[20,16,256]{2,1,0:T(8,128)S(1)}, u32[]{:S(2)}, u32[]{:S(2)}) collective-permute-start(f32[20,16,256]{2,1,0:T(8,128)S(1)} %get-tuple-element.39), channel_id=1, source_target_pairs={{0,8},{8,16},{16,24},{24,32},{32,40},{40,48},{48,56},{56,64},{64,7... | collective-permute-start | bytes 983048 | tf_op jit(solution)/shard_map/ppermute | solution.py:629
  4.4 10.2 %collective-permute-start.1 = (f32[17,16,256]{2,1,0:T(8,128)S(1)}, f32[17,16,256]{2,1,0:T(8,128)S(1)}, u32[]{:S(2)}, u32[]{:S(2)}) collective-permute-start(f32[17,16,256]{2,1,0:T(8,128)S(1)} %get-tuple-element.40), channel_id=1, source_target_pairs={{8,0},{16,8},{24,16},{32,24},{40,32},{48,40},{56,48},{64,56},{72,6... | collective-permute-start | bytes 835592 | tf_op jit(solution)/shard_map/ppermute | solution.py:629
  9.2 14.7 %collective-permute-start.4 = (f32[21,16,256]{2,1,0:T(8,128)S(1)}, f32[21,16,256]{2,1,0:T(8,128)S(1)}, u32[]{:S(2)}, u32[]{:S(2)}) collective-permute-start(f32[21,16,256]{2,1,0:T(8,128)S(1)} %get-tuple-element.48), channel_id=1, source_target_pairs={{0,8},{8,16},{16,24},{24,32},{32,40},{40,48},{48,56},{56,64},{64,7... | collective-permute-start | bytes 1032200 | tf_op jit(solution)/shard_map/ppermute | solution.py:629
  9.2 14.7 %collective-permute-start.5 = (f32[21,16,256]{2,1,0:T(8,128)S(1)}, f32[21,16,256]{2,1,0:T(8,128)S(1)}, u32[]{:S(2)}, u32[]{:S(2)}) collective-permute-start(f32[21,16,256]{2,1,0:T(8,128)S(1)} %get-tuple-element.49), channel_id=1, source_target_pairs={{8,0},{16,8},{24,16},{32,24},{40,32},{48,40},{56,48},{64,56},{72,6... | collective-permute-start | bytes 1032200 | tf_op jit(solution)/shard_map/ppermute | solution.py:629
  17.6 9.9 %collective-permute-start.2 = (f32[61,8,256]{2,1,0:T(8,128)}, f32[61,8,256]{2,1,0:T(8,128)S(1)}, u32[]{:S(2)}, u32[]{:S(2)}) collective-permute-start(f32[61,8,256]{2,1,0:T(8,128)} %get-tuple-element.41), channel_id=1, source_target_pairs={{0,1},{1,2},{2,3},{3,4},{4,5},{5,6},{6,7},{7,0},{8,9},{9,10},{10,1... | collective-permute-start | bytes 1499144 | tf_op jit(solution)/shard_map/ppermute | solution.py:629
  20.9 8.6 %collective-permute-start.3 = (f32[61,8,256]{2,1,0:T(8,128)}, f32[61,8,256]{2,1,0:T(8,128)S(1)}, u32[]{:S(2)}, u32[]{:S(2)}) collective-permute-start(f32[61,8,256]{2,1,0:T(8,128)} %get-tuple-element.42), channel_id=1, source_target_pairs={{1,0},{2,1},{3,2},{4,3},{5,4},{6,5},{7,6},{0,7},{9,8},{10,9},{11,1... | collective-permute-start | bytes 1499144 | tf_op jit(solution)/shard_map/ppermute | solution.py:629
  24.9 11.5 %collective-permute-start.6 = (f32[45,8,256]{2,1,0:T(8,128)}, f32[45,8,256]{2,1,0:T(8,128)}, u32[]{:S(2)}, u32[]{:S(2)}) collective-permute-start(f32[45,8,256]{2,1,0:T(8,128)} %get-tuple-element.50), channel_id=1, source_target_pairs={{0,1},{1,2},{2,3},{3,4},{4,5},{5,6},{6,7},{7,0},{8,9},{9,10},{10,1... | collective-permute-start | bytes 1105928 | tf_op jit(solution)/shard_map/ppermute | solution.py:629
  27.4 9.1 %collective-permute-start.7 = (f32[45,8,256]{2,1,0:T(8,128)}, f32[45,8,256]{2,1,0:T(8,128)}, u32[]{:S(2)}, u32[]{:S(2)}) collective-permute-start(f32[45,8,256]{2,1,0:T(8,128)} %get-tuple-element.51), channel_id=1, source_target_pairs={{1,0},{2,1},{3,2},{4,3},{5,4},{6,5},{7,6},{0,7},{9,8},{10,9},{11,1... | collective-permute-start | bytes 1105928 | tf_op jit(solution)/shard_map/ppermute | solution.py:629
  76.7 11.2 %collective-permute-start.8 = (f32[18,16,256]{2,1,0:T(8,128)S(1)}, f32[18,16,256]{2,1,0:T(8,128)S(1)}, u32[]{:S(2)}, u32[]{:S(2)}) collective-permute-start(f32[18,16,256]{2,1,0:T(8,128)S(1)} %get-tuple-element.57), channel_id=1, source_target_pairs={{0,8},{8,16},{16,24},{24,32},{32,40},{40,48},{48,56},{56,64},{64,7... | collective-permute-start | bytes 884744 | tf_op jit(solution)/shard_map/ppermute | solution.py:629
  77.1 10.8 %collective-permute-start.9 = (f32[18,16,256]{2,1,0:T(8,128)S(1)}, f32[18,16,256]{2,1,0:T(8,128)S(1)}, u32[]{:S(2)}, u32[]{:S(2)}) collective-permute-start(f32[18,16,256]{2,1,0:T(8,128)S(1)} %get-tuple-element.58), channel_id=1, source_target_pairs={{8,0},{16,8},{24,16},{32,24},{40,32},{48,40},{56,48},{64,56},{72,6... | collective-permute-start | bytes 884744 | tf_op jit(solution)/shard_map/ppermute | solution.py:629
  88.1 8.2 %collective-permute-start.10 = (f32[528,256]{1,0:T(8,128)S(1)}, f32[528,256]{1,0:T(8,128)S(1)}, u32[]{:S(2)}, u32[]{:S(2)}) collective-permute-start(f32[528,256]{1,0:T(8,128)S(1)} %get-tuple-element.59), channel_id=1, source_target_pairs={{0,1},{1,2},{2,3},{3,4},{4,5},{5,6},{6,7},{7,0},{8,9},{9,10},{10,1... | collective-permute-start | bytes 1622024 | tf_op jit(solution)/shard_map/ppermute | solution.py:629
  89.9 9.1 %collective-permute-start.11 = (f32[528,256]{1,0:T(8,128)S(1)}, f32[528,256]{1,0:T(8,128)S(1)}, u32[]{:S(2)}, u32[]{:S(2)}) collective-permute-start(f32[528,256]{1,0:T(8,128)S(1)} %get-tuple-element.60), channel_id=1, source_target_pairs={{1,0},{2,1},{3,2},{4,3},{5,4},{6,5},{7,6},{0,7},{9,8},{10,9},{11,1... | collective-permute-start | bytes 1622024 | tf_op jit(solution)/shard_map/ppermute | solution.py:629

commit v3 on v2

--- a/solution.py
+++ b/solution.py
@@ -15,12 +15,12 @@
 GENS = 4
 PAIRS = [(a, b) for a in range(GENS) for b in range(a, GENS)]
 LEVELS = ((0, 0), (0, 1), (1, 1), (1, 2), (2, 2), (2, 3))
-LOW, HIGH = 7, 6
+LOW, HIGH = 6, 6
 XE = LOW + NX + HIGH
-ML = 4
-ME = NX + 2 * ML
+ML, MH = 3, 4
+ME = ML + NX + MH
 MO = LOW - ML
-PK = ML + NX + 3
+PK = 3 + NX + 3
 PIVOT = 2e-7
 PW = 4
 COST = 200_000_000
@@ -31,11 +31,19 @@
 
 
 def up_y(v):
-    return pltpu.roll(v, v.shape[0] - 1, 0)
+    n = v.shape[0] // 8
+    turned = [pltpu.roll(v[8 * k : 8 * k + 8], 7, 0) for k in range(n)]
+    inner = lax.broadcasted_iota(jnp.int32, turned[0].shape, 0) < 7
+    joined = [jnp.where(inner, turned[k], turned[k + 1]) for k in range(n - 1)]
+    return jnp.concatenate([*joined, turned[n - 1]], axis=0)
 
 
 def dn_y(v):
-    return pltpu.roll(v, 1, 0)
+    n = v.shape[0] // 8
+    turned = [pltpu.roll(v[8 * k : 8 * k + 8], 1, 0) for k in range(n)]
+    inner = lax.broadcasted_iota(jnp.int32, turned[0].shape, 0) > 0
+    joined = [jnp.where(inner, turned[k], turned[k - 1]) for k in range(1, n)]
+    return jnp.concatenate([turned[0], *joined], axis=0)
 
 
 def up_z(v):
@@ -85,21 +93,21 @@
     take(ids, raw)
     take(p, pv)
     take(f, fv)
-    take(p.at[1:8], up_p.at[7:14])
+    take(p.at[2:8], up_p.at[6:12])
     take(p.at[0:6], dn_p.at[6:12])
-    take(f.at[2:8], up_p.at[14:20])
+    take(f.at[3:8], up_p.at[12:17])
     take(f.at[0:5], dn_p.at[12:17])
     for a in range(3):
-        take(u.at[a, 4:8], up_m.at[4 * a : 4 * a + 4])
+        take(u.at[a, 5:8], up_m.at[3 * a : 3 * a + 3])
         take(u.at[a, 0:4], dn_m.at[4 * a : 4 * a + 4])
-        take(b.at[a, 5:8], up_m.at[12 + 3 * a : 15 + 3 * a])
+        take(b.at[a, 6:8], up_m.at[9 + 2 * a : 11 + 2 * a])
         take(b.at[a, 0:3], dn_m.at[12 + 3 * a : 15 + 3 * a])
     copies[0].wait()
     for x in range(NX):
         c = (raw[x] + 1).astype(F32)
         code[x] = c
-        if x >= 1:
-            up_p[x - 1] = c
+        if x >= 2:
+            up_p[x - 2] = c
         if x < 6:
             dn_p[x] = c
     for copy in copies[1:]:
@@ -115,28 +123,28 @@
 
 
 def pack_y_pressure_kernel(ids, p, f, low, high, up, dn):
-    for x in range(21):
-        ref, i = pick(x, low, ids, high, (0, 0), 7)
+    for x in range(XE):
+        ref, i = pick(x, low, ids, high, (0, 0), LOW)
         up[x] = ref[i, 8:16]
         dn[x] = ref[i, 0:8]
-        ref, i = pick(x, low, p, high, (7, 6), 7)
-        up[21 + x] = ref[i, 8:16]
-        dn[21 + x] = ref[i, 0:8]
-    for x in range(19):
-        ref, i = pick(x, low, f, high, (14, 12), 6)
-        up[42 + x] = ref[i, 8:16]
-        dn[42 + x] = ref[i, 0:8]
+        ref, i = pick(x, low, p, high, (6, 6), LOW)
+        up[20 + x] = ref[i, 8:16]
+        dn[20 + x] = ref[i, 0:8]
+    for x in range(XE - 2):
+        ref, i = pick(x, low, f, high, (12, 12), LOW - 1)
+        up[40 + x] = ref[i, 8:16]
+        dn[40 + x] = ref[i, 0:8]
 
 
 def pack_y_mech_kernel(u, b, low, high, up, dn):
     for a in range(3):
-        for m in range(16):
-            ref, i = pick(m, low, u.at[a], high, (4 * a, 4 * a), 4)
+        for m in range(ME):
+            ref, i = pick(m, low, u.at[a], high, (3 * a, 4 * a), ML)
             k, r = 8 * a + m // 2, 4 * (m % 2)
             up[k, r : r + 4] = ref[i, 12:16]
             dn[k, r : r + 4] = ref[i, 0:4]
-        for m in range(14):
-            ref, i = pick(m, low, b.at[a], high, (12 + 3 * a, 12 + 3 * a), 3)
+        for m in range(ME - 2):
+            ref, i = pick(m, low, b.at[a], high, (9 + 2 * a, 12 + 3 * a), ML - 1)
             k, r = 24 + 7 * a + m // 2, 4 * (m % 2)
             up[k, r : r + 4] = ref[i, 12:16]
             dn[k, r : r + 4] = ref[i, 0:4]
@@ -237,7 +245,9 @@
         loop(1 + i, XE - 1 - i, follow, PW)
 
     def final(x):
-        return [(n, (3, x), around(t.at[2], x, cx, cy, cz))]
+        v = t[2, x]
+        e = cx[x] * t[2, x + 1] + cy[x] * up_y(v) + cz[x] * up_z(v)
+        return [(n, (3, x), 2.0 * e)]
 
     loop(LOW, LOW + NX, final, PW)
 
@@ -261,8 +271,8 @@
 ):
     cx, cy, cz, inv, diag, base, biot = (coef.at[i] for i in range(7))
     fill(code, XE, LOW, ids, low, high, (0, 0), yl, yh, 0, flags)
-    fill(pe, XE, LOW, p, low, high, (7, 6), yl, yh, 21, flags)
-    fill(fe.at[1:20], XE - 2, LOW - 1, f, low, high, (14, 12), yl, yh, 42, None)
+    fill(pe, XE, LOW, p, low, high, (6, 6), yl, yh, 20, flags)
+    fill(fe.at[1 : XE - 1], XE - 2, LOW - 1, f, low, high, (12, 12), yl, yh, 40, None)
 
     def tables(x):
         l, s, k, st, bi = lookup(code[x], mats, range(5))
@@ -310,32 +320,32 @@
     edge = lambda x, n: flags[0] if x < n else flags[1]
     zero = jnp.zeros((2, NZ), F32)
     for a in range(3):
-        for x in range(20):
-            k = 6 * (20 * a + x)
+        for x in range(19):
+            k = 6 * (19 * a + x)
             out = de.at[a, x + 1]
             lo, hi = yl[k : k + 6] * flags[2], yh[k : k + 6] * flags[3]
-            if 5 <= x < 15:
+            if 5 <= x < 14:
                 out[4:28] = du[a, x - 5]
             else:
                 outer = edge(x, 5)
                 lo, hi = lo * outer, hi * outer
-                ref = low.at[5 * a + x] if x < 5 else high.at[5 * a + x - 15]
+                ref = low.at[5 * a + x] if x < 5 else high.at[5 * a + x - 14]
                 out[8:24] = ref[...] * outer
-            if not 6 <= x < 14:
-                lo, hi = lo * edge(x, 6), hi * edge(x, 6)
+            if x == 13:
+                lo, hi = lo * flags[1], hi * flags[1]
             out[0:2] = zero
             out[2:8] = lo
             out[24:30] = hi
             out[30:32] = zero
     for x in range(XE):
-        k = 360 + 8 * x
+        k = 344 + 8 * x
         lo, hi = yl[k : k + 8] * flags[2], yh[k : k + 8] * flags[3]
         if not LOW <= x < LOW + NX:
             lo, hi = lo * edge(x, LOW), hi * edge(x, LOW)
-        if 3 <= x < 18:
+        if 3 <= x < 17:
             pe[x, 8:24] = p[x - 3, 8:24]
         else:
-            ref = low.at[15 + x] if x < 3 else high.at[15 + x - 18]
+            ref = low.at[15 + x] if x < 3 else high.at[15 + x - 17]
             pe[x, 8:24] = ref[...] * edge(x, LOW)
         pe[x, 0:8] = lo
         pe[x, 24:32] = hi
@@ -355,7 +365,7 @@
             ue[a, m] = uo[a, m] + de[a, m + MO, 4:28]
 
 
-def mech_chain(u, bf, pe, t, biot, mc, kept, q, load, carry, acc, s, part_p, part):
+def mech_chain(u, bf, pe, t, biot, mc, kept, q, load, carry, acc, s, tg, part_p, part):
     sx, sy, sz, diag, lame, h0, h1, h2, kk = (mc.at[i] for i in range(9))
     h = (h0, h1, h2)
 
@@ -386,7 +396,7 @@
         return jnp.where((m >= ML) & (m < ML + NX), m - ML, NX)
 
     def near(m):
-        return jnp.where((m >= ML - 1) & (m <= ML + NX), m - ML + 1, NX + 2)
+        return jnp.where((m >= ML) & (m <= ML + NX), m - ML, NX + 1)
 
     def residual(m):
         for g in range(GENS):
@@ -411,13 +421,13 @@
                 yield s, (0, g, a, m), z[a]
                 yield kept, (g * 3 + a, near(m)), z[a]
 
-    loop(1, ME - 1, residual)
+    loop(1, ME - 1, residual, 2)
 
     def basis(i, g):
         if i < 2:
             return s.at[i, g], 0
         k = (i * GENS + g) * 3
-        return kept.at[k : k + 3], ML - 1
+        return kept.at[k : k + 3], ML
 
     def parts(w, m, o):
         c = [w[a, m - o] for a in range(3)]
@@ -434,7 +444,7 @@
         ]
         return c, r, l * total, above
 
-    for i in (1, 2, 3):
+    for i in (1, 2):
         for g in range(GENS):
             w, o = basis(i - 1, g)
             carry[g] = parts(w, i, o)[3]
@@ -455,35 +465,56 @@
                 r[2] = r[2] + push + (x * w[2, m + 1 - o] + xb * w[2, m - 1 - o]) + (
                     y * up_y(c[2]) + dn_y(y * c[2])
                 )
-                slot = own(m) if i < 3 else m - ML
+                v = precondition(r, m)
                 for a in range(3):
-                    yield q, (i, g, a, slot), r[a]
-                if i < 3:
-                    v = precondition(r, m)
-                    for a in range(3):
-                        if i == 1:
-                            yield s, (i, g, a, m), v[a]
-                        yield kept, ((i * GENS + g) * 3 + a, near(m)), v[a]
+                    yield q, (i, g, a, own(m)), r[a]
+                    if i == 1:
+                        yield s, (i, g, a, m), v[a]
+                    yield kept, ((i * GENS + g) * 3 + a, near(m)), v[a]
 
         loop(1 + i, ME - 1 - i, follow)
+
+    def energy(m):
+        l, x, y, z = lame[m], sx[m], sy[m], sz[m]
+        half = (0.5 * lame[m - 1], 0.5 * dn_y(l), 0.5 * dn_z(l))
+        for g in range(GENS):
+            w, o = basis(2, g)
+            total = 0.0
+            for a in range(3):
+                c = w[a, m - o]
+                up = (w[a, m + 1 - o], up_y(c), up_z(c))
+                total = total + up[a]
+                yield q, (3, g, a, m - ML), x * up[0] + y * up[1] + z * up[2] + half[a] * c
+            near_sum = w[0, m - o] + w[1, m - o] + w[2, m - o]
+            yield tg, (0, g, m - ML), total
+            yield tg, (1, g, m - ML), l * (near_sum - 0.5 * total)
+
+    loop(ML, ML + NX, energy)
 
     top = lax.broadcasted_iota(jnp.int32, (8, NZ), 0) >= 4
     for k, (i, j) in enumerate(LEVELS):
 
-        def body(x, sums):
+        def body(step, sums):
             sums = list(sums)
-            for a in range(3):
-                v = [kept[(i * GENS + g) * 3 + a, 1 + x] for g in range(GENS)]
-                w = [q[j, g, a, x] for g in range(GENS)]
-                for pick_rows in (
-                    lambda f: f[8:16],
-                    lambda f: jnp.where(top, f[0:8], f[16:24]),
-                ):
-                    vt, wt = [pick_rows(f) for f in v], [pick_rows(f) for f in w]
-                    sums = [c + vt[g] * wt[o] for c, (g, o) in zip(sums, PAIRS)]
+            for x in (2 * step, 2 * step + 1):
+                for a in range(3 if j < 3 else 4):
+                    if a < 3:
+                        v = [kept[(i * GENS + g) * 3 + a, x] for g in range(GENS)]
+                        w = [q[j, g, a, x] for g in range(GENS)]
+                    else:
+                        v = [tg[0, g, x] for g in range(GENS)]
+                        w = [tg[1, g, x] for g in range(GENS)]
+                    for pick_rows in (
+                        lambda f: f[8:16],
+                        lambda f: jnp.where(top, f[0:8], f[16:24]),
+                    ):
+                        vt, wt = [pick_rows(f) for f in v], [pick_rows(f) for f in w]
+                        sums = [c + vt[g] * wt[o] for c, (g, o) in zip(sums, PAIRS)]
+                        if j == 3:
+                            sums = [c + vt[o] * wt[g] for c, (g, o) in zip(sums, PAIRS)]
             return tuple(sums)
 
-        sums = lax.fori_loop(0, NX, body, (jnp.zeros((8, NZ), F32),) * len(PAIRS))
+        sums = lax.fori_loop(0, NX // 2, body, (jnp.zeros((8, NZ), F32),) * len(PAIRS))
         for n, v in enumerate(sums):
             acc[10 * k + n] = v
     at = lax.broadcasted_iota(jnp.int32, (8, 128), 1)
@@ -497,12 +528,14 @@
 def mech_first_kernel(
     flags, mats, part_p, code, pe, coef, t, u, b, low, high, yl, yh,
     ue, be, mc, kept, part,
-    q, load, shear, carry, acc, s,
+    q, load, shear, carry, acc, s, tg,
 ):
     sx, sy, sz, diag, lame, h0, h1, h2, kk = (mc.at[i] for i in range(9))
     for a in range(3):
-        fill_mech(ue.at[a], 16, 4, u.at[a], low, high, (4 * a, 4 * a), yl, yh, 8 * a, flags, 0)
-        fill_mech(be.at[a], 14, 3, b.at[a], low, high, (12 + 3 * a, 12 + 3 * a), yl, yh, 24 + 7 * a, None, 1)
+        fill_mech(ue.at[a], ME, ML, u.at[a], low, high, (3 * a, 4 * a), yl, yh, 8 * a, flags, 0)
+        fill_mech(
+            be.at[a], ME - 2, ML - 1, b.at[a], low, high, (9 + 2 * a, 12 + 3 * a), yl, yh, 24 + 7 * a, None, 1
+        )
 
     def tables(m):
         l, g = lookup(code[m + MO, 4:28], mats, (0, 1))
@@ -534,15 +567,15 @@
         return [(diag, m, d), (h0, m, hs[0]), (h1, m, hs[1]), (h2, m, hs[2]), (kk, m, k)]
 
     loop(1, ME - 1, diagonal, 2)
-    mech_chain(ue, be, pe, t, coef.at[6], mc, kept, q, load, carry, acc, s, part_p, part)
+    mech_chain(ue, be, pe, t, coef.at[6], mc, kept, q, load, carry, acc, s, tg, part_p, part)
 
 
 def mech_next_kernel(
     part_p, pe, coef, t, ue, be, mc,
     kept, part,
-    q, load, carry, acc, s,
+    q, load, carry, acc, s, tg,
 ):
-    mech_chain(ue, be, pe, t, coef.at[6], mc, kept, q, load, carry, acc, s, part_p, part)
+    mech_chain(ue, be, pe, t, coef.at[6], mc, kept, q, load, carry, acc, s, tg, part_p, part)
 
 
 def combine(v, kept, a, x):
@@ -560,43 +593,42 @@
         w = pe[x] + (y[0] * t[0, x] + y[1] * t[1, x] + y[2] * t[2, x])
         pnew[k] = w
         i = k - ML
-        if 1 <= i <= 3:
-            up[14 + i] = w[8:24]
+        if 2 <= i <= 4:
+            up[13 + i] = w[8:24]
         if 3 <= i <= 5:
             dn[12 + i] = w[8:24]
     for a in range(3):
-        for k in range(NX + 2):
-            d = combine(v, kept, a, k)
-            du[a, k] = d
-            i = k - 1
-            if 0 <= i < NX:
+        for i in range(NX + 1):
+            d = combine(v, kept, a, i)
+            du[a, i] = d
+            if i < NX:
                 unew[a, i] = u[a, i] + d[4:20]
-            if 2 <= i <= 6:
-                up[5 * a + i - 2] = d[4:20]
+            if 3 <= i <= 7:
+                up[5 * a + i - 3] = d[4:20]
             if 1 <= i <= 5:
                 dn[5 * a + i - 1] = d[4:20]
 
 
 def pack_change_kernel(du, p, low, high, up, dn):
     for a in range(3):
-        for x in range(20):
+        for x in range(19):
             if x < 5:
                 ref, r = low.at[5 * a + x], 0
-            elif x < 15:
+            elif x < 14:
                 ref, r = du.at[a, x - 5], 4
             else:
-                ref, r = high.at[5 * a + x - 15], 0
-            k = 6 * (20 * a + x)
+                ref, r = high.at[5 * a + x - 14], 0
+            k = 6 * (19 * a + x)
             up[k : k + 6] = ref[r + 10 : r + 16]
             dn[k : k + 6] = ref[r : r + 6]
     for x in range(XE):
         if x < 3:
             ref, r = low.at[15 + x], 0
-        elif x < 18:
+        elif x < 17:
             ref, r = p.at[x - 3], 8
         else:
-            ref, r = high.at[15 + x - 18], 0
-        k = 360 + 8 * x
+            ref, r = high.at[15 + x - 17], 0
+        k = 344 + 8 * x
         up[k : k + 8] = ref[r + 8 : r + 16]
         dn[k : k + 8] = ref[r : r + 8]
 
@@ -608,7 +640,7 @@
         w = p[k, 8:24] + (y[0] * t[0, k, 8:24] + y[1] * t[1, k, 8:24] + y[2] * t[2, k, 8:24])
         pnew[x] = w
         for a in range(3):
-            unew[a, x] = u[a, x] + combine(v, kept, a, x + 1)[4:20]
+            unew[a, x] = u[a, x] + combine(v, kept, a, x)[4:20]
 
 
 def call(kernel, name, ins, outs, scratch=(), specs=None, cost=0, limit=12):
@@ -641,14 +673,14 @@
         pack_x_kernel,
         "pack_x",
         [pltpu.with_memory_space_constraint(v, pltpu.HBM) for v in (ids, p, f, u, b)],
-        [(20, NY, NZ), (17, NY, NZ), (21, NY, NZ), (21, NY, NZ)] + [(NX, NY, NZ)] * 3,
+        [(17, NY, NZ), (17, NY, NZ), (15, NY, NZ), (21, NY, NZ)] + [(NX, NY, NZ)] * 3,
         [pltpu.VMEM((NX, NY, NZ), jnp.int32), pltpu.SemaphoreType.DMA((19,))],
         [HB] * 5,
     )
     low_p, high_p = neighbours("gx", gx_size, up_p, dn_p)
     low_m, high_m = neighbours("gx", gx_size, up_m, dn_m)
     up, dn = call(
-        pack_y_pressure_kernel, "pack_yp", (own_code, own_p, own_f, low_p, high_p), [(61, 8, NZ), (61, 8, NZ)], limit=4
+        pack_y_pressure_kernel, "pack_yp", (own_code, own_p, own_f, low_p, high_p), [(58, 8, NZ), (58, 8, NZ)], limit=4
     )
     yl_p, yh_p = neighbours("gy", gy_size, up, dn)
     up, dn = call(pack_y_mech_kernel, "pack_ym", (u, b, low_m, high_m), [(45, 8, NZ), (45, 8, NZ)], limit=4)
@@ -668,8 +700,9 @@
         (GENS, *mech),
         (60, 8, NZ),
         (2, GENS, 3, ME, *mech),
+        (2, GENS, NX, *mech),
     ]
-    basis = (9 * GENS, NX + 3, *mech)
+    basis = (9 * GENS, NX + 2, *mech)
     ue, be, mc, s, part = call(
         mech_first_kernel,
         "mech_first",
@@ -678,17 +711,17 @@
         mech_scratch[:2] + [(ME, *mech)] + mech_scratch[2:],
         [SM, SM] + [VM] * 11,
         COST,
-        24,
+        26,
     )
     rows = gather_rows(part)
     du, p1, u1, up, dn = call(
         change_kernel,
         "change",
         (rows, t, pe, s, u),
-        [(3, NX + 2, *mech), (PK, *wide), (3, NX, NY, NZ), (18, NY, NZ), (18, NY, NZ)],
+        [(3, NX + 1, *mech), (PK, *wide), (3, NX, NY, NZ), (18, NY, NZ), (18, NY, NZ)],
     )
     low, high = neighbours("gx", gx_size, up, dn)
-    up, dn = call(pack_change_kernel, "pack_change", (du, p1, low, high), [(528, NZ), (528, NZ)])
+    up, dn = call(pack_change_kernel, "pack_change", (du, p1, low, high), [(504, NZ), (504, NZ)])
     yl, yh = neighbours("gy", gy_size, up, dn)
     pe, ue, t, part_p = call(
         pressure_next_kernel,
@@ -707,7 +740,7 @@
         mech_scratch,
         None,
         COST,
-        24,
+        26,
     )
     rows = gather_rows(part)
     u2, p2 = call(

time: 141 us -> 134 us (0.950)
  Pallas kernels: 56.7 us -> 50.8 us
  starting transfers between devices: 24.2 us -> 20.7 us
    pallas_call x10, Pallas kernels: 56.7 us -> 50.8 us  [call(): pl.pallas_call(kernel, name=name, out_shape=[jax.ShapeDtypeStruct(o, F32)...]
    ppermute x6, starting transfers between devices: 14.1 us -> 10.7 us  [neighbours(): lax.ppermute(dn, axis, [(b, a) for a, b in ring])]
    ppermute x6, waiting for transfers between devices: 5.3 us -> 6.77 us  [neighbours(): lax.ppermute(dn, axis, [(b, a) for a, b in ring])]
    all_to_all x2, blocking collectives: 36.1 us -> 37.5 us  [gather_rows(): return lax.all_to_all(part, ('gx', 'gy'), 0, 0, tiled=True)]
where the time goes in v3:
time: 134 us
  Pallas kernels  50.8 us (38%)
  blocking collectives  37.5 us (28%)
  waiting for transfers between devices  24.4 us (18%)
  starting transfers between devices  20.7 us (15%)
    pallas_call x10, Pallas kernels, call(): pl.pallas_call(kernel, name=name, out_shape=[jax.ShapeDtypeStruct(o, F32)...  50.8 us
    all_to_all x2, blocking collectives, gather_rows(): return lax.all_to_all(part, ('gx', 'gy'), 0, 0, tiled=True)  37.5 us
    ppermute x6, waiting for transfers between devices, neighbours(): lax.ppermute(up, axis, ring)  17.7 us
    ppermute x6, starting transfers between devices, neighbours(): lax.ppermute(dn, axis, [(b, a) for a, b in ring])  10.7 us
    ppermute x6, starting transfers between devices, neighbours(): lax.ppermute(up, axis, ring)  10 us
    ppermute x6, waiting for transfers between devices, neighbours(): lax.ppermute(dn, axis, [(b, a) for a, b in ring])  6.77 us
  transfers between devices with their start and end apart: 12, of which 7 were waited for; matrix products, arithmetic and copies ran while one was open for 0% of the time, Pallas kernels for 6%

profile of v3, /device:TPU:1, one launch (start us, length us, event | category | flops | bytes accessed | tf_op | source)
XLA Modules:
  0.0 134.3 jit_solution(13420517460288915281)
XLA Ops:
  0.7 1.5 %pack_x.1 = (f32[17,16,256]{2,1,0:T(8,128)S(1)}, f32[17,16,256]{2,1,0:T(8,128)S(1)}, f32[15,16,256]{2,1,0:T(8,128)S(1)}, f32[21,16,256]{2,1,0:T(8,128)S(1)}, f32...) custom-call(s32[8,16,256]{2,1,0:T(8,128)} %ids.1, f32[8,16,256]{2,1,0:T(8,128)} %p.1, ...), custom_call_target="tpu_custom_call" | custom-call | tf_op jit(solution)/shard_map/pack_x/pallas_call | solution.py:647
  2.2 2.1 %collective-permute-start = (f32[17,16,256]{2,1,0:T(8,128)S(1)}, f32[17,16,256]{2,1,0:T(8,128)S(1)}, u32[]{:S(2)}, u32[]{:S(2)}) collective-permute-start(f32[17,16,256]{2,1,0:T(8,128)S(1)} %get-tuple-element.39), channel_id=1, source_target_pairs={{0,8},{8,16},{16,24},{24,32},{32,40},{40,48},{48,56},{56,64},{64,7... | collective-permute-start | bytes 835592 | tf_op jit(solution)/shard_map/ppermute | solution.py:661
  4.3 4.8 %collective-permute-start.1 = (f32[17,16,256]{2,1,0:T(8,128)S(1)}, f32[17,16,256]{2,1,0:T(8,128)S(1)}, u32[]{:S(2)}, u32[]{:S(2)}) collective-permute-start(f32[17,16,256]{2,1,0:T(8,128)S(1)} %get-tuple-element.40), channel_id=1, source_target_pairs={{8,0},{16,8},{24,16},{32,24},{40,32},{48,40},{56,48},{64,56},{72,6... | collective-permute-start | bytes 835592 | tf_op jit(solution)/shard_map/ppermute | solution.py:661
  9.1 1.4 %collective-permute-start.5 = (f32[21,16,256]{2,1,0:T(8,128)S(1)}, f32[21,16,256]{2,1,0:T(8,128)S(1)}, u32[]{:S(2)}, u32[]{:S(2)}) collective-permute-start(f32[21,16,256]{2,1,0:T(8,128)S(1)} %get-tuple-element.49), channel_id=1, source_target_pairs={{8,0},{16,8},{24,16},{32,24},{40,32},{48,40},{56,48},{64,56},{72,6... | collective-permute-start | bytes 1032200 | tf_op jit(solution)/shard_map/ppermute | solution.py:661
  10.5 0.1 collective-permute-start.4
  10.6 4.8 %collective-permute-done.low = f32[17,16,256]{2,1,0:T(8,128)S(1)} collective-permute-done((f32[17,16,256]{2,1,0:T(8,128)S(1)}, f32[17,16,256]{2,1,0:T(8,128)S(1)}, u32[]{:S(2)}, u32[]{:S(2)}) %collective-permute-start) | collective-permute-done | bytes 278560 | tf_op jit(solution)/shard_map/ppermute | solution.py:661
  15.4 0.0 collective-permute-done.1.high
  15.4 1.0 pack_yp.1
  16.4 2.9 %collective-permute-start.2 = (f32[58,8,256]{2,1,0:T(8,128)}, f32[58,8,256]{2,1,0:T(8,128)S(1)}, u32[]{:S(2)}, u32[]{:S(2)}) collective-permute-start(f32[58,8,256]{2,1,0:T(8,128)} %get-tuple-element.41), channel_id=1, source_target_pairs={{0,1},{1,2},{2,3},{3,4},{4,5},{5,6},{6,7},{7,0},{8,9},{9,10},{10,1... | collective-permute-start | bytes 1425416 | tf_op jit(solution)/shard_map/ppermute | solution.py:661
  19.3 0.0 collective-permute-start.3
  19.3 0.5 collective-permute-done.4.low
  19.8 2.0 %collective-permute-done.5.high = f32[21,16,256]{2,1,0:T(8,128)S(1)} collective-permute-done((f32[21,16,256]{2,1,0:T(8,128)S(1)}, f32[21,16,256]{2,1,0:T(8,128)S(1)}, u32[]{:S(2)}, u32[]{:S(2)}) %collective-permute-start.5) | collective-permute-done | bytes 344096 | tf_op jit(solution)/shard_map/ppermute | solution.py:661
  21.9 1.0 pack_ym.1
  22.9 2.7 %collective-permute-start.6 = (f32[45,8,256]{2,1,0:T(8,128)}, f32[45,8,256]{2,1,0:T(8,128)}, u32[]{:S(2)}, u32[]{:S(2)}) collective-permute-start(f32[45,8,256]{2,1,0:T(8,128)} %get-tuple-element.50), channel_id=1, source_target_pairs={{0,1},{1,2},{2,3},{3,4},{4,5},{5,6},{6,7},{7,0},{8,9},{9,10},{10,1... | collective-permute-start | bytes 1105928 | tf_op jit(solution)/shard_map/ppermute | solution.py:661
  25.6 0.0 collective-permute-start.7
  25.6 0.1 add_convert_fusion.flags
  25.6 2.0 %collective-permute-done.3.yh = f32[58,8,256]{2,1,0:T(8,128)S(1)} collective-permute-done((f32[58,8,256]{2,1,0:T(8,128)}, f32[58,8,256]{2,1,0:T(8,128)S(1)}, u32[]{:S(2)}, u32[]{:S(2)}) %collective-permute-start.3) | collective-permute-done | bytes 475168 | tf_op jit(solution)/shard_map/ppermute | solution.py:661
  27.6 6.7 %pressure_first.1 = (f32[20,32,256]{2,1,0:T(8,128)S(1)}, f32[20,32,256]{2,1,0:T(8,128)S(1)}, f32[7,20,32,256]{3,2,1,0:T(8,128)S(1)}, f32[3,20,32,256]{3,2,1,0:T(8,128)S(1)}, f32[8,128]{1,0:T(8,128)S(1)}) custom-call(f32[4]{0:T(128)S(1)} %add_convert_fusion.flags, f32[5,8]{1,0:T(8,128)S(1)} %copy-done.2, f32[8,16,256]{2,1,0:T(8,128)S(1)} %get-tuple-element.36.ids, ...), custom_call_target="tpu_custom_call" | custom-call | flops 200000000 | tf_op jit(solution)/shard_map/pressure_first/pallas_call | solution.py:647
  34.3 18.7 %mech_first.1 = (f32[3,15,24,256]{3,2,1,0:T(8,128)S(1)}, f32[3,15,24,256]{3,2,1,0:T(8,128)S(1)}, f32[9,15,24,256]{3,2,1,0:T(8,128)S(1)}, f32[36,10,24,256]{3,2,1,0:T(8,128)S(1)}, f32[128,128]{1,0:T(8,128)S(1)}) custom-call(f32[4]{0:T(128)S(1)} %add_convert_fusion.flags, f32[5,8]{1,0:T(8,128)S(1)} %copy-done.2, f32[8,128]{1,0:T(8,128)S(1)} %get-tuple-element.44.part_p, ...), custom_call_target="tpu_custom_call" | custom-call | flops 200000000 | tf_op jit(solution)/shard_map/mech_first/pallas_call | solution.py:647
  53.0 19.0 %all_to_all.22 = f32[128,1,128]{2,1,0:T(1,128)S(1)} all-to-all(f32[128,1,128]{2,1,0:T(1,128)S(1)} %bitcast.14), channel_id=1, replica_groups=mesh['gx'=16,'gy'=8] {'gx','gy'}, dimensions={0} | all-to-all | bytes 131072 | tf_op jit(solution)/shard_map/all_to_all | solution.py:665
  72.1 1.3 change.1
  73.4 0.4 collective-permute-start.8
  73.7 4.5 %collective-permute-start.9 = (f32[18,16,256]{2,1,0:T(8,128)S(1)}, f32[18,16,256]{2,1,0:T(8,128)S(1)}, u32[]{:S(2)}, u32[]{:S(2)}) collective-permute-start(f32[18,16,256]{2,1,0:T(8,128)S(1)} %get-tuple-element.58), channel_id=1, source_target_pairs={{8,0},{16,8},{24,16},{32,24},{40,32},{48,40},{56,48},{64,56},{72,6... | collective-permute-start | bytes 884744 | tf_op jit(solution)/shard_map/ppermute | solution.py:661
  78.2 6.3 %collective-permute-done.8.low = f32[18,16,256]{2,1,0:T(8,128)S(1)} collective-permute-done((f32[18,16,256]{2,1,0:T(8,128)S(1)}, f32[18,16,256]{2,1,0:T(8,128)S(1)}, u32[]{:S(2)}, u32[]{:S(2)}) %collective-permute-start.8) | collective-permute-done | bytes 294944 | tf_op jit(solution)/shard_map/ppermute | solution.py:661
  84.6 0.2 pack_change.1
  84.7 1.9 %collective-permute-start.10 = (f32[504,256]{1,0:T(8,128)S(1)}, f32[504,256]{1,0:T(8,128)S(1)}, u32[]{:S(2)}, u32[]{:S(2)}) collective-permute-start(f32[504,256]{1,0:T(8,128)S(1)} %get-tuple-element.59), channel_id=1, source_target_pairs={{0,1},{1,2},{2,3},{3,4},{4,5},{5,6},{6,7},{7,0},{8,9},{9,10},{10,1... | collective-permute-start | bytes 1548296 | tf_op jit(solution)/shard_map/ppermute | solution.py:661
  86.6 6.0 %collective-permute-done.10.yl = f32[504,256]{1,0:T(8,128)S(1)} collective-permute-done((f32[504,256]{1,0:T(8,128)S(1)}, f32[504,256]{1,0:T(8,128)S(1)}, u32[]{:S(2)}, u32[]{:S(2)}) %collective-permute-start.10) | collective-permute-done | bytes 516128 | tf_op jit(solution)/shard_map/ppermute | solution.py:661
  92.6 2.8 %collective-permute-done.11.yh = f32[504,256]{1,0:T(8,128)S(1)} collective-permute-done((f32[504,256]{1,0:T(8,128)S(1)}, f32[504,256]{1,0:T(8,128)S(1)}, u32[]{:S(2)}, u32[]{:S(2)}) %collective-permute-start.11) | collective-permute-done | bytes 516128 | tf_op jit(solution)/shard_map/ppermute | solution.py:661
  95.4 3.7 %pressure_next.1 = (f32[20,32,256]{2,1,0:T(8,128)S(1)}, f32[3,15,24,256]{3,2,1,0:T(8,128)S(1)}, f32[3,20,32,256]{3,2,1,0:T(8,128)S(1)}, f32[8,128]{1,0:T(8,128)S(1)}) custom-call(f32[4]{0:T(128)S(1)} %add_convert_fusion.flags, f32[7,20,32,256]{3,2,1,0:T(8,128)S(1)} %get-tuple-element.43.coef, f32[14,32,256]{2,1,0:T(8,128)S(1)} %get-tuple-element.54.p, ...), custom_call_target="tpu_custom_call" | custom-call | flops 200000000 | tf_op jit(solution)/shard_map/pressure_next/pallas_call | solution.py:647
  99.2 15.1 %mech_next.1 = (f32[36,10,24,256]{3,2,1,0:T(8,128)S(1)}, f32[128,128]{1,0:T(8,128)S(1)}) custom-call(f32[8,128]{1,0:T(8,128)S(1)} %get-tuple-element.61.part_p, f32[20,32,256]{2,1,0:T(8,128)S(1)} %get-tuple-element.62.pe.p, f32[7,20,32,256]{3,2,1,0:T(8,128)S(1)} %get-tuple-element.43.coef, f32[3,20,32,256]{3,2,1,0:T(8,128)S(1)} %get-tuple-element.63.t, ...), custom_call_target="tpu_custom_call" | custom-call | flops 200000000 | tf_op jit(solution)/shard_map/mech_next/pallas_call | solution.py:647
  114.3 18.4 %all_to_all.23 = f32[128,1,128]{2,1,0:T(1,128)S(1)} all-to-all(f32[128,1,128]{2,1,0:T(1,128)S(1)} %bitcast.15), channel_id=1, replica_groups=mesh['gx'=16,'gy'=8] {'gx','gy'}, dimensions={0} | all-to-all | bytes 131072 | tf_op jit(solution)/shard_map/all_to_all | solution.py:665
  132.7 1.6 %finish.1 = (f32[3,8,16,256]{3,2,1,0:T(8,128)}, f32[8,16,256]{2,1,0:T(8,128)}) custom-call(f32[128,128]{1,0:T(8,128)S(1)} %bitcast.13, f32[3,20,32,256]{3,2,1,0:T(8,128)S(1)} %get-tuple-element.63.t, f32[20,32,256]{2,1,0:T(8,128)S(1)} %get-tuple-element.62.pe.p, f32[36,10,24,256]{3,2,1,0:T(8,128)S(1)} %get-tuple-element.68.kept, ...), custom_call_target="tpu_custom_call" | custom-call | tf_op jit(solution)/shard_map/finish/pallas_call | solution.py:647
  (11 shorter events, 0.0 us)
Async XLA Ops:
  0.6 21.2 %copy-start = (f32[3,8,16,256]{3,2,1,0:T(8,128)S(1)}, f32[3,8,16,256]{3,2,1,0:T(8,128)}, u32[]{:S(2)}) copy-start(f32[3,8,16,256]{3,2,1,0:T(8,128)} %u.7) | copy-start | bytes 1179652
  0.6 21.2 %copy-start.1 = (f32[3,8,16,256]{3,2,1,0:T(8,128)S(1)}, f32[3,8,16,256]{3,2,1,0:T(8,128)}, u32[]{:S(2)}) copy-start(f32[3,8,16,256]{3,2,1,0:T(8,128)} %b.5) | copy-start | bytes 1179652
  0.7 27.0 %copy-start.2 = (f32[5,8]{1,0:T(8,128)S(1)}, f32[5,8]{1,0:T(8,128)}, u32[]{:S(2)}) copy-start(f32[5,8]{1,0:T(8,128)} %mats.3) | copy-start | bytes 484
  2.2 13.2 %collective-permute-start = (f32[17,16,256]{2,1,0:T(8,128)S(1)}, f32[17,16,256]{2,1,0:T(8,128)S(1)}, u32[]{:S(2)}, u32[]{:S(2)}) collective-permute-start(f32[17,16,256]{2,1,0:T(8,128)S(1)} %get-tuple-element.39), channel_id=1, source_target_pairs={{0,8},{8,16},{16,24},{24,32},{32,40},{40,48},{48,56},{56,64},{64,7... | collective-permute-start | bytes 835592 | tf_op jit(solution)/shard_map/ppermute | solution.py:661
  4.3 11.1 %collective-permute-start.1 = (f32[17,16,256]{2,1,0:T(8,128)S(1)}, f32[17,16,256]{2,1,0:T(8,128)S(1)}, u32[]{:S(2)}, u32[]{:S(2)}) collective-permute-start(f32[17,16,256]{2,1,0:T(8,128)S(1)} %get-tuple-element.40), channel_id=1, source_target_pairs={{8,0},{16,8},{24,16},{32,24},{40,32},{48,40},{56,48},{64,56},{72,6... | collective-permute-start | bytes 835592 | tf_op jit(solution)/shard_map/ppermute | solution.py:661
  9.1 12.7 %collective-permute-start.5 = (f32[21,16,256]{2,1,0:T(8,128)S(1)}, f32[21,16,256]{2,1,0:T(8,128)S(1)}, u32[]{:S(2)}, u32[]{:S(2)}) collective-permute-start(f32[21,16,256]{2,1,0:T(8,128)S(1)} %get-tuple-element.49), channel_id=1, source_target_pairs={{8,0},{16,8},{24,16},{32,24},{40,32},{48,40},{56,48},{64,56},{72,6... | collective-permute-start | bytes 1032200 | tf_op jit(solution)/shard_map/ppermute | solution.py:661
  10.5 9.3 %collective-permute-start.4 = (f32[15,16,256]{2,1,0:T(8,128)S(1)}, f32[15,16,256]{2,1,0:T(8,128)S(1)}, u32[]{:S(2)}, u32[]{:S(2)}) collective-permute-start(f32[15,16,256]{2,1,0:T(8,128)S(1)} %get-tuple-element.48), channel_id=1, source_target_pairs={{0,8},{8,16},{16,24},{24,32},{32,40},{40,48},{48,56},{56,64},{64,7... | collective-permute-start | bytes 737288 | tf_op jit(solution)/shard_map/ppermute | solution.py:661
  16.4 9.2 %collective-permute-start.2 = (f32[58,8,256]{2,1,0:T(8,128)}, f32[58,8,256]{2,1,0:T(8,128)S(1)}, u32[]{:S(2)}, u32[]{:S(2)}) collective-permute-start(f32[58,8,256]{2,1,0:T(8,128)} %get-tuple-element.41), channel_id=1, source_target_pairs={{0,1},{1,2},{2,3},{3,4},{4,5},{5,6},{6,7},{7,0},{8,9},{9,10},{10,1... | collective-permute-start | bytes 1425416 | tf_op jit(solution)/shard_map/ppermute | solution.py:661
  19.3 8.3 %collective-permute-start.3 = (f32[58,8,256]{2,1,0:T(8,128)}, f32[58,8,256]{2,1,0:T(8,128)S(1)}, u32[]{:S(2)}, u32[]{:S(2)}) collective-permute-start(f32[58,8,256]{2,1,0:T(8,128)} %get-tuple-element.42), channel_id=1, source_target_pairs={{1,0},{2,1},{3,2},{4,3},{5,4},{6,5},{7,6},{0,7},{9,8},{10,9},{11,1... | collective-permute-start | bytes 1425416 | tf_op jit(solution)/shard_map/ppermute | solution.py:661
  22.9 11.5 %collective-permute-start.6 = (f32[45,8,256]{2,1,0:T(8,128)}, f32[45,8,256]{2,1,0:T(8,128)}, u32[]{:S(2)}, u32[]{:S(2)}) collective-permute-start(f32[45,8,256]{2,1,0:T(8,128)} %get-tuple-element.50), channel_id=1, source_target_pairs={{0,1},{1,2},{2,3},{3,4},{4,5},{5,6},{6,7},{7,0},{8,9},{9,10},{10,1... | collective-permute-start | bytes 1105928 | tf_op jit(solution)/shard_map/ppermute | solution.py:661
  25.6 8.8 %collective-permute-start.7 = (f32[45,8,256]{2,1,0:T(8,128)}, f32[45,8,256]{2,1,0:T(8,128)}, u32[]{:S(2)}, u32[]{:S(2)}) collective-permute-start(f32[45,8,256]{2,1,0:T(8,128)} %get-tuple-element.51), channel_id=1, source_target_pairs={{1,0},{2,1},{3,2},{4,3},{5,4},{6,5},{7,6},{0,7},{9,8},{10,9},{11,1... | collective-permute-start | bytes 1105928 | tf_op jit(solution)/shard_map/ppermute | solution.py:661
  73.4 11.2 %collective-permute-start.8 = (f32[18,16,256]{2,1,0:T(8,128)S(1)}, f32[18,16,256]{2,1,0:T(8,128)S(1)}, u32[]{:S(2)}, u32[]{:S(2)}) collective-permute-start(f32[18,16,256]{2,1,0:T(8,128)S(1)} %get-tuple-element.57), channel_id=1, source_target_pairs={{0,8},{8,16},{16,24},{24,32},{32,40},{40,48},{48,56},{56,64},{64,7... | collective-permute-start | bytes 884744 | tf_op jit(solution)/shard_map/ppermute | solution.py:661
  73.7 10.8 %collective-permute-start.9 = (f32[18,16,256]{2,1,0:T(8,128)S(1)}, f32[18,16,256]{2,1,0:T(8,128)S(1)}, u32[]{:S(2)}, u32[]{:S(2)}) collective-permute-start(f32[18,16,256]{2,1,0:T(8,128)S(1)} %get-tuple-element.58), channel_id=1, source_target_pairs={{8,0},{16,8},{24,16},{32,24},{40,32},{48,40},{56,48},{64,56},{72,6... | collective-permute-start | bytes 884744 | tf_op jit(solution)/shard_map/ppermute | solution.py:661
  84.7 7.9 %collective-permute-start.10 = (f32[504,256]{1,0:T(8,128)S(1)}, f32[504,256]{1,0:T(8,128)S(1)}, u32[]{:S(2)}, u32[]{:S(2)}) collective-permute-start(f32[504,256]{1,0:T(8,128)S(1)} %get-tuple-element.59), channel_id=1, source_target_pairs={{0,1},{1,2},{2,3},{3,4},{4,5},{5,6},{6,7},{7,0},{8,9},{9,10},{10,1... | collective-permute-start | bytes 1548296 | tf_op jit(solution)/shard_map/ppermute | solution.py:661
  86.6 8.8 %collective-permute-start.11 = (f32[504,256]{1,0:T(8,128)S(1)}, f32[504,256]{1,0:T(8,128)S(1)}, u32[]{:S(2)}, u32[]{:S(2)}) collective-permute-start(f32[504,256]{1,0:T(8,128)S(1)} %get-tuple-element.60), channel_id=1, source_target_pairs={{1,0},{2,1},{3,2},{4,3},{5,4},{6,5},{7,6},{0,7},{9,8},{10,9},{11,1... | collective-permute-start | bytes 1548296 | tf_op jit(solution)/shard_map/ppermute | solution.py:661

commit v4 on v3

--- a/solution.py
+++ b/solution.py
@@ -52,10 +52,10 @@
     return jnp.concatenate([jnp.where(inner, low, high), jnp.where(inner, high, 0.0)], axis=1)
 
 
-def dn_z(v):
+def dn_z(v, first=0.0):
     low, high = pltpu.roll(v[:, :128], 1, 1), pltpu.roll(v[:, 128:], 1, 1)
     inner = lax.broadcasted_iota(jnp.int32, low.shape, 1) > 0
-    return jnp.concatenate([jnp.where(inner, low, 0.0), jnp.where(inner, high, low)], axis=1)
+    return jnp.concatenate([jnp.where(inner, low, first), jnp.where(inner, high, low)], axis=1)
 
 
 def loop(low, high, compute, width=1):
@@ -180,79 +180,131 @@
         out[x + offset, 20:24] = hi
 
 
-def solve(mu):
-    g = lambda i: mu[i] - mu[i + 1]
-    g00, g01, g02, g12, g22 = g(0), g(1), g(2), g(3), g(4)
-    g11 = g02
-    inverse = lambda d, scale: jnp.where(d > PIVOT * scale, 1.0 / d, 0.0)
-    i0 = inverse(g00, 0.0 * g00)
-    l10, l20 = g01 * i0, g02 * i0
-    i1 = inverse(g11 - l10 * g01, g11)
-    e = g12 - l10 * g02
+def two_sum(a, b):
+    s = a + b
+    t = s - a
+    return s, (a - (s - t)) + (b - t)
+
+
+def halves(a):
+    c = 4097.0 * a
+    high = c - (c - a)
+    return high, a - high
+
+
+def two_product(a, b):
+    p = a * b
+    (ah, al), (bh, bl) = halves(a), halves(b)
+    return p, ((ah * bh - p) + ah * bl + al * bh) + al * bl
+
+
+def dot(pairs, start, rest):
+    for a, b in pairs:
+        p, e = two_product(a, b)
+        start, f = two_sum(start, p)
+        rest = rest + (e + f)
+    return start, rest
+
+
+def solve(m):
+    def minus(a, b):
+        d, e = two_sum(a[0], 0.0 - b[0])
+        return d, e + (a[1] - b[1])
+
+    g00, g01, g02 = m[1], m[2], m[3]
+    g11, g12, g22 = minus(m[2], m[3]), minus(m[3], m[4]), minus(m[4], m[5])
+    right = (m[0], m[1], minus(m[1], m[2]))
+    inverse = lambda d, scale: jnp.where(d > PIVOT * jnp.abs(scale), 1.0 / d, 0.0)
+    i0 = inverse(g00[0], 0.0 * g00[0])
+    l10, l20 = g01[0] * i0, g02[0] * i0
+    i1 = inverse(g11[0] - l10 * g01[0], g11[0])
+    e = g12[0] - l10 * g02[0]
     l21 = e * i1
-    i2 = inverse(g22 - l20 * g02 - l21 * e, g22)
-    c0 = mu[0]
-    c1 = mu[1] - l10 * c0
-    c2 = mu[2] - l20 * c0 - l21 * c1
-    y2 = c2 * i2
-    y1 = c1 * i1 - l21 * y2
-    y0 = c0 * i0 - l10 * y1 - l20 * y2
-    return y0, y1, y2
+    i2 = inverse(g22[0] - l20 * g02[0] - l21 * e, g22[0])
+
+    def eliminate(c0, c1, c2):
+        c1 = c1 - l10 * c0
+        c2 = c2 - l20 * c0 - l21 * c1
+        y2 = c2 * i2
+        y1 = c1 * i1 - l21 * y2
+        return c0 * i0 - l10 * y1 - l20 * y2, y1, y2
+
+    y = eliminate(*[r[0] for r in right])
+    left = []
+    for r, row in zip(right, ((g00, g01, g02), (g01, g11, g12), (g02, g12, g22))):
+        rest = r[1]
+        for a, v in zip(row, y):
+            rest = rest - a[1] * v
+        d, rest = dot([(a[0], 0.0 - v) for a, v in zip(row, y)], r[0], rest)
+        left.append(d + rest)
+    return [a + b for a, b in zip(y, eliminate(*left))]
 
 
 def coefficients(rows):
-    total = jnp.sum(rows[...], axis=0, keepdims=True)
-    at = lambda k: jnp.broadcast_to(total[:, k : k + 1], (1, 128))
+    high, low = two_sum(rows[0:64], rows[64:128])
+    while high.shape[0] > 8:
+        n = high.shape[0] // 2
+        rest = low[:n] + low[n:]
+        high, low = two_sum(high[:n], high[n:])
+        low = low + rest
+    for n in (4, 2, 1):
+        rest = low + pltpu.roll(low, n, 0)
+        high, low = two_sum(high, pltpu.roll(high, n, 0))
+        low = low + rest
+    spread = lambda v, k: jnp.broadcast_to(v[:, k : k + 1], (8, 128))
+    at = lambda k: (spread(high, k), spread(low, k))
     y = solve([at(k) for k in range(6)])
-    c = (1.0, *y)
+    y = (y[0] + y[1], y[2] - y[1], 0.0 - y[2])
+    c = (jnp.ones((8, 128), F32), *y)
+    weights = [c[a] * c[b] * (1.0 if a == b else 2.0) for a, b in PAIRS]
     mu = []
     for k in range(6):
-        m = 0.0
-        for i, (a, b) in enumerate(PAIRS):
-            w = c[a] * c[b] * (1.0 if a == b else 2.0)
-            m = m + w * at(6 + 10 * k + i)
-        mu.append(m)
+        terms = [at(6 + 10 * k + i) for i in range(len(PAIRS))]
+        rest = 0.0
+        for w, t in zip(weights, terms):
+            rest = rest + w * t[1]
+        mu.append(dot([(w, t[0]) for w, t in zip(weights, terms)], 0.0 * y[0], rest))
     v = solve(mu)
     scalar = lambda x: x[0, 0]
     return [scalar(x) for x in y], [[scalar(x * c[g]) for g in range(GENS)] for x in v]
 
 
-def around(v, x, cx, cy, cz):
+def differences(v, x, cx, cy, cz):
     c = v[x]
-    y, z = cy[x], cz[x]
+    fy, fz = cy[x] * (c - up_y(c)), cz[x] * (c - up_z(c))
     return (
-        cx[x] * v[x + 1]
-        + cx[x - 1] * v[x - 1]
-        + y * up_y(c)
-        + dn_y(y * c)
-        + z * up_z(c)
-        + dn_z(z * c)
-    )
-
-
-def pressure_chain(start, p, cx, cy, cz, inv, t, n, part):
+        cx[x] * (c - v[x + 1])
+        + cx[x - 1] * (c - v[x - 1])
+        + (fy - dn_y(fy))
+        + (fz - dn_z(fz))
+    )
+
+
+def pressure_chain(source, p, cx, cy, cz, inv, total, t, n, k, part):
     def first(x):
-        r = start(x) + around(p, x, cx, cy, cz)
+        r = source(x) - differences(p, x, cx, cy, cz)
         return [(n, (0, x), r), (t, (0, x), inv[x] * r)]
 
     loop(1, XE - 1, first, PW)
     for i in (1, 2):
 
         def follow(x):
-            r = around(t.at[i - 1], x, cx, cy, cz)
-            return [(n, (i, x), r), (t, (i, x), inv[x] * r)]
+            c = t[i - 1, x]
+            a = total[x] * c + differences(t.at[i - 1], x, cx, cy, cz)
+            d = inv[x] * a
+            return [(n, (i, x), a), (k, (i - 1, x), d), (t, (i, x), c - d)]
 
         loop(1 + i, XE - 1 - i, follow, PW)
 
     def final(x):
-        v = t[2, x]
-        e = cx[x] * t[2, x + 1] + cy[x] * up_y(v) + cz[x] * up_z(v)
+        v = k[1, x]
+        e = cx[x] * k[1, x + 1] + cy[x] * up_y(v) + cz[x] * up_z(v)
         return [(n, (3, x), 2.0 * e)]
 
     loop(LOW, LOW + NX, final, PW)
 
     def body(x, acc):
-        s = [t[i, LOW + x, 8:24] for i in range(3)]
+        s = [v[LOW + x, 8:24] for v in (t.at[0], k.at[0], k.at[1])]
         q = [n[i, LOW + x, 8:24] for i in range(4)]
         return tuple(v + s[i] * q[j] for v, (i, j) in zip(acc, LEVELS))
 
@@ -267,9 +319,9 @@
 def pressure_first_kernel(
     flags, mats, ids, p, f, low, high, yl, yh,
     code, pe, coef, t, part,
-    fe, perm, stor, stab, n,
+    fe, perm, stor, n, k,
 ):
-    cx, cy, cz, inv, diag, base, biot = (coef.at[i] for i in range(7))
+    cx, cy, cz, inv, stab, base, biot, total = (coef.at[i] for i in range(8))
     fill(code, XE, LOW, ids, low, high, (0, 0), yl, yh, 0, flags)
     fill(pe, XE, LOW, p, low, high, (6, 6), yl, yh, 20, flags)
     fill(fe.at[1 : XE - 1], XE - 2, LOW - 1, f, low, high, (12, 12), yl, yh, 40, None)
@@ -303,27 +355,27 @@
         d = stor[x] + stab[x] + flow
         return [
             (inv, x, jnp.where(inside, 1.0 / jnp.where(inside, d, 1.0), 0.0)),
-            (diag, x, stab[x] - d),
+            (total, x, stor[x] + stab[x]),
             (base, x, stor[x] * pe[x] + DT * fe[x]),
         ]
 
     loop(1, XE - 1, diagonal, 2)
-    pressure_chain(lambda x: base[x] + diag[x] * pe[x], pe, cx, cy, cz, inv, t, n, part)
+    pressure_chain(lambda x: DT * fe[x], pe, cx, cy, cz, inv, total, t, n, k, part)
 
 
 def pressure_next_kernel(
     flags, coef, p, du, uo, low, high, yl, yh,
     pe, ue, t, part,
-    de, n,
+    de, n, k,
 ):
-    cx, cy, cz, inv, diag, base, biot = (coef.at[i] for i in range(7))
+    cx, cy, cz, inv, stab, base, biot, total = (coef.at[i] for i in range(8))
     edge = lambda x, n: flags[0] if x < n else flags[1]
     zero = jnp.zeros((2, NZ), F32)
     for a in range(3):
         for x in range(19):
-            k = 6 * (19 * a + x)
+            j = 6 * (19 * a + x)
             out = de.at[a, x + 1]
-            lo, hi = yl[k : k + 6] * flags[2], yh[k : k + 6] * flags[3]
+            lo, hi = yl[j : j + 6] * flags[2], yh[j : j + 6] * flags[3]
             if 5 <= x < 14:
                 out[4:28] = du[a, x - 5]
             else:
@@ -338,8 +390,8 @@
             out[24:30] = hi
             out[30:32] = zero
     for x in range(XE):
-        k = 344 + 8 * x
-        lo, hi = yl[k : k + 8] * flags[2], yh[k : k + 8] * flags[3]
+        j = 344 + 8 * x
+        lo, hi = yl[j : j + 8] * flags[2], yh[j : j + 8] * flags[3]
         if not LOW <= x < LOW + NX:
             lo, hi = lo * edge(x, LOW), hi * edge(x, LOW)
         if 3 <= x < 17:
@@ -353,20 +405,20 @@
     def start(x):
         c2 = de[2, x]
         div = (
-            de[0, x + 1] - de[0, x]
-            + up_y(de[1, x]) - de[1, x]
-            + up_z(c2) - c2
+            (de[0, x + 1] - de[0, x])
+            + (up_y(de[1, x]) - de[1, x])
+            + (up_z(c2) - c2)
         )
-        return base[x] - biot[x] * div + diag[x] * pe[x]
-
-    pressure_chain(start, pe, cx, cy, cz, inv, t, n, part)
+        return base[x] - biot[x] * div + (stab[x] - total[x]) * pe[x]
+
+    pressure_chain(start, pe, cx, cy, cz, inv, total, t, n, k, part)
     for a in range(3):
         for m in range(ME):
             ue[a, m] = uo[a, m] + de[a, m + MO, 4:28]
 
 
 def mech_chain(u, bf, pe, t, biot, mc, kept, q, load, carry, acc, s, tg, part_p, part):
-    sx, sy, sz, diag, lame, h0, h1, h2, kk = (mc.at[i] for i in range(9))
+    sx, sy, sz, half, lame, h0, h1, h2, kk = (mc.at[i] for i in range(9))
     h = (h0, h1, h2)
 
     def loads(m):
@@ -377,20 +429,48 @@
 
     loop(0, ME - 1, loads, 2)
 
-    def ups(w, m):
-        return (w[0, m + 1], up_y(w[1, m]), up_z(w[2, m]))
-
     def precondition(r, m):
         hs = [h[a][m] for a in range(3)]
         scaled = [r[a] * hs[a] for a in range(3)]
         k = kk[m] * (scaled[0] + scaled[1] + scaled[2])
         return [scaled[a] - hs[a] * k for a in range(3)]
 
-    def pull(m):
-        p = ups(u, m)
-        return lame[m] * (p[0] + p[1] + p[2] - (u[0, m] + u[1, m] + u[2, m]))
-
-    carry[0] = load[0, 0] - pull(0)
+    def apply(w, m, more, below):
+        c = [w[a, m] for a in range(3)]
+        d = (c[0] - w[0, m + 1], c[1] - up_y(c[1]), c[2] - up_z(c[2]))
+        l = 0.0 - lame[m] * (d[0] + d[1] + d[2])
+        if more is not None:
+            l = l - more
+        x, xb, y, z, g = sx[m], sx[m - 1], sy[m], sz[m], half[m, :, :128]
+
+        def along_x(a):
+            return x * (c[a] - w[a, m + 1]) + xb * (c[a] - w[a, m - 1])
+
+        def along_y(a):
+            f = y * (c[a] - up_y(c[a]))
+            return f - dn_y(f)
+
+        def along_z(a):
+            f = z * (c[a] - up_z(c[a]))
+            return f + dn_z(0.0 - f, g * c[a][:, :128])
+
+        fx, fy, fz = x * d[0], y * d[1], z * d[2]
+        r = [
+            (fx + below - l) + along_y(0) + along_z(0),
+            (fy + dn_y(l - fy) - l) + along_x(1) + along_z(1),
+            (fz + dn_z(l - fz, g * c[2][:, :128]) - l) + along_x(2) + along_y(2),
+        ]
+        return r, l - fx
+
+    def carried(w, m, more):
+        c = [w[a, m] for a in range(3)]
+        d = (c[0] - w[0, m + 1], c[1] - up_y(c[1]), c[2] - up_z(c[2]))
+        l = 0.0 - lame[m] * (d[0] + d[1] + d[2])
+        if more is not None:
+            l = l - more
+        return l - sx[m] * d[0]
+
+    carry[0] = carried(u, 0, load[0, 0])
 
     def own(m):
         return jnp.where((m >= ML) & (m < ML + NX), m - ML, NX)
@@ -401,20 +481,12 @@
     def residual(m):
         for g in range(GENS):
             if g == 0:
-                c = load[0, m] - pull(m)
-                below = carry[0]
-                d = diag[m]
-                r = [
-                    bf[a, m] - d * u[a, m] + around(u.at[a], m, sx, sy, sz) for a in range(3)
-                ]
+                r, up = apply(u, m, load[0, m], carry[0])
+                yield carry, 0, up
+                r = [bf[a, m] - r[a] for a in range(3)]
             else:
                 c = load[g, m]
-                below = load[g, m - 1]
-                r = [0.0, 0.0, 0.0]
-            low = (below, dn_y(c), dn_z(c))
-            r = [r[a] + (low[a] - c) for a in range(3)]
-            if g == 0:
-                yield carry, 0, c
+                r = [load[g, m - 1] - c, dn_y(c) - c, dn_z(c) - c]
             z = precondition(r, m)
             for a in range(3):
                 yield q, (0, g, a, own(m)), r[a]
@@ -423,68 +495,36 @@
 
     loop(1, ME - 1, residual, 2)
 
-    def basis(i, g):
-        if i < 2:
-            return s.at[i, g], 0
-        k = (i * GENS + g) * 3
-        return kept.at[k : k + 3], ML
-
-    def parts(w, m, o):
-        c = [w[a, m - o] for a in range(3)]
-        p = (w[0, m + 1 - o], up_y(c[1]), up_z(c[2]))
-        total = p[0] + p[1] + p[2]
-        l = lame[m]
-        e = (c[0] + c[1] + c[2]) - total
-        x, y, z = sx[m], sy[m], sz[m]
-        above = x * c[0] + l * (p[0] + e)
-        r = [
-            x * p[0],
-            y * p[1] + dn_y(y * c[1] + l * (p[1] + e)),
-            z * p[2] + dn_z(z * c[2] + l * (p[2] + e)),
-        ]
-        return c, r, l * total, above
-
     for i in (1, 2):
         for g in range(GENS):
-            w, o = basis(i - 1, g)
-            carry[g] = parts(w, i, o)[3]
+            carry[g] = carried(s.at[i - 1, g], i, None)
 
         def follow(m):
             for g in range(GENS):
-                w, o = basis(i - 1, g)
-                c, r, push, above = parts(w, m, o)
-                below = carry[g]
-                yield carry, g, above
-                x, xb, y, z = sx[m], sx[m - 1], sy[m], sz[m]
-                r[0] = r[0] + push + below + (y * up_y(c[0]) + dn_y(y * c[0])) + (
-                    z * up_z(c[0]) + dn_z(z * c[0])
-                )
-                r[1] = r[1] + push + (x * w[1, m + 1 - o] + xb * w[1, m - 1 - o]) + (
-                    z * up_z(c[1]) + dn_z(z * c[1])
-                )
-                r[2] = r[2] + push + (x * w[2, m + 1 - o] + xb * w[2, m - 1 - o]) + (
-                    y * up_y(c[2]) + dn_y(y * c[2])
-                )
+                w = s.at[i - 1, g]
+                r, up = apply(w, m, None, carry[g])
+                yield carry, g, up
                 v = precondition(r, m)
                 for a in range(3):
                     yield q, (i, g, a, own(m)), r[a]
+                    yield kept, ((i * GENS + g) * 3 + a, near(m)), v[a]
                     if i == 1:
-                        yield s, (i, g, a, m), v[a]
-                    yield kept, ((i * GENS + g) * 3 + a, near(m)), v[a]
+                        yield s, (1, g, a, m), w[a, m] - v[a]
 
         loop(1 + i, ME - 1 - i, follow)
 
     def energy(m):
         l, x, y, z = lame[m], sx[m], sy[m], sz[m]
-        half = (0.5 * lame[m - 1], 0.5 * dn_y(l), 0.5 * dn_z(l))
+        low = (0.5 * lame[m - 1], 0.5 * dn_y(l), 0.5 * dn_z(l))
         for g in range(GENS):
-            w, o = basis(2, g)
+            k = (2 * GENS + g) * 3
+            w, o = kept.at[k : k + 3], ML
             total = 0.0
             for a in range(3):
                 c = w[a, m - o]
                 up = (w[a, m + 1 - o], up_y(c), up_z(c))
                 total = total + up[a]
-                yield q, (3, g, a, m - ML), x * up[0] + y * up[1] + z * up[2] + half[a] * c
+                yield q, (3, g, a, m - ML), x * up[0] + y * up[1] + z * up[2] + low[a] * c
             near_sum = w[0, m - o] + w[1, m - o] + w[2, m - o]
             yield tg, (0, g, m - ML), total
             yield tg, (1, g, m - ML), l * (near_sum - 0.5 * total)
@@ -530,7 +570,7 @@
     ue, be, mc, kept, part,
     q, load, shear, carry, acc, s, tg,
 ):
-    sx, sy, sz, diag, lame, h0, h1, h2, kk = (mc.at[i] for i in range(9))
+    sx, sy, sz, half, lame, h0, h1, h2, kk = (mc.at[i] for i in range(9))
     for a in range(3):
         fill_mech(ue.at[a], ME, ML, u.at[a], low, high, (3 * a, 4 * a), yl, yh, 8 * a, flags, 0)
         fill_mech(
@@ -564,7 +604,7 @@
         lows = (lame[m - 1], dn_y(l), dn_z(l))
         hs = [jnp.where(inside, 1.0 / jnp.where(inside, d + v, 1.0), 0.0) for v in lows]
         k = l / (1.0 + l * (hs[0] + hs[1] + hs[2]))
-        return [(diag, m, d), (h0, m, hs[0]), (h1, m, hs[1]), (h2, m, hs[2]), (kk, m, k)]
+        return [(half, m, 0.5 * g), (h0, m, hs[0]), (h1, m, hs[1]), (h2, m, hs[2]), (kk, m, k)]
 
     loop(1, ME - 1, diagonal, 2)
     mech_chain(ue, be, pe, t, coef.at[6], mc, kept, q, load, carry, acc, s, tg, part_p, part)
@@ -689,8 +729,8 @@
         pressure_first_kernel,
         "pressure_first",
         (flags, mats, own_code, own_p, own_f, low_p, high_p, yl_p, yh_p),
-        [(XE, *wide), (XE, *wide), (7, XE, *wide), (3, XE, *wide), (8, 128)],
-        [(XE, *wide)] * 4 + [(4, XE, *wide)],
+        [(XE, *wide), (XE, *wide), (8, XE, *wide), (3, XE, *wide), (8, 128)],
+        [(XE, *wide)] * 3 + [(4, XE, *wide), (2, XE, *wide)],
         [SM, SM] + [VM] * 7,
         COST,
     )
@@ -728,7 +768,7 @@
         "pressure_next",
         (flags, coef, p1, du, ue, low, high, yl, yh),
         [(XE, *wide), (3, ME, *mech), (3, XE, *wide), (8, 128)],
-        [(3, XE, *wide), (4, XE, *wide)],
+        [(3, XE, *wide), (4, XE, *wide), (2, XE, *wide)],
         [SM] + [VM] * 8,
         COST,
     )

time: 134 us -> 136 us (1.015)
  transfers between devices with their start and end apart: 12 -> 12, of which waited for: 7 -> 7; matrix products, arithmetic and copies ran while one was open for 0% -> 0% of each run, Pallas kernels for 6% -> 7%
where the time goes in v4:
time: 136 us; the launch traced here: 135 us
  Pallas kernels  51.9 us (38%)
  blocking collectives  37.5 us (28%)
  waiting for transfers between devices  24.4 us (18%)
  starting transfers between devices  20.7 us (15%)
    pallas_call x10, Pallas kernels, call(): pl.pallas_call(kernel, name=name, out_shape=[jax.ShapeDtypeStruct(o, F32)...  51.9 us
    all_to_all x2, blocking collectives, gather_rows(): return lax.all_to_all(part, ('gx', 'gy'), 0, 0, tiled=True)  37.5 us
    ppermute x6, waiting for transfers between devices, neighbours(): lax.ppermute(up, axis, ring)  17.7 us
    ppermute x6, starting transfers between devices, neighbours(): lax.ppermute(dn, axis, [(b, a) for a, b in ring])  10.7 us
    ppermute x6, starting transfers between devices, neighbours(): lax.ppermute(up, axis, ring)  10 us
    ppermute x6, waiting for transfers between devices, neighbours(): lax.ppermute(dn, axis, [(b, a) for a, b in ring])  6.77 us
  transfers between devices with their start and end apart: 12, of which 7 were waited for; matrix products, arithmetic and copies ran while one was open for 0% of the time, Pallas kernels for 7%

profile of v4, /device:TPU:1, one launch (start us, length us, event | category | flops | bytes accessed | tf_op | source)
XLA Modules:
  0.0 135.4 jit_solution(4365134147167225633)
XLA Ops:
  0.7 1.6 %pack_x.1 = (f32[17,16,256]{2,1,0:T(8,128)S(1)}, f32[17,16,256]{2,1,0:T(8,128)S(1)}, f32[15,16,256]{2,1,0:T(8,128)S(1)}, f32[21,16,256]{2,1,0:T(8,128)S(1)}, f32...) custom-call(s32[8,16,256]{2,1,0:T(8,128)} %ids.1, f32[8,16,256]{2,1,0:T(8,128)} %p.1, ...), custom_call_target="tpu_custom_call" | custom-call | tf_op jit(solution)/shard_map/pack_x/pallas_call | solution.py:687
  2.3 2.1 %collective-permute-start = (f32[17,16,256]{2,1,0:T(8,128)S(1)}, f32[17,16,256]{2,1,0:T(8,128)S(1)}, u32[]{:S(2)}, u32[]{:S(2)}) collective-permute-start(f32[17,16,256]{2,1,0:T(8,128)S(1)} %get-tuple-element.39), channel_id=1, source_target_pairs={{0,8},{8,16},{16,24},{24,32},{32,40},{40,48},{48,56},{56,64},{64,7... | collective-permute-start | bytes 835592 | tf_op jit(solution)/shard_map/ppermute | solution.py:701
  4.4 4.8 %collective-permute-start.1 = (f32[17,16,256]{2,1,0:T(8,128)S(1)}, f32[17,16,256]{2,1,0:T(8,128)S(1)}, u32[]{:S(2)}, u32[]{:S(2)}) collective-permute-start(f32[17,16,256]{2,1,0:T(8,128)S(1)} %get-tuple-element.40), channel_id=1, source_target_pairs={{8,0},{16,8},{24,16},{32,24},{40,32},{48,40},{56,48},{64,56},{72,6... | collective-permute-start | bytes 835592 | tf_op jit(solution)/shard_map/ppermute | solution.py:701
  9.2 1.4 %collective-permute-start.5 = (f32[21,16,256]{2,1,0:T(8,128)S(1)}, f32[21,16,256]{2,1,0:T(8,128)S(1)}, u32[]{:S(2)}, u32[]{:S(2)}) collective-permute-start(f32[21,16,256]{2,1,0:T(8,128)S(1)} %get-tuple-element.49), channel_id=1, source_target_pairs={{8,0},{16,8},{24,16},{32,24},{40,32},{48,40},{56,48},{64,56},{72,6... | collective-permute-start | bytes 1032200 | tf_op jit(solution)/shard_map/ppermute | solution.py:701
  10.6 0.1 collective-permute-start.4
  10.6 4.8 %collective-permute-done.low = f32[17,16,256]{2,1,0:T(8,128)S(1)} collective-permute-done((f32[17,16,256]{2,1,0:T(8,128)S(1)}, f32[17,16,256]{2,1,0:T(8,128)S(1)}, u32[]{:S(2)}, u32[]{:S(2)}) %collective-permute-start) | collective-permute-done | bytes 278560 | tf_op jit(solution)/shard_map/ppermute | solution.py:701
  15.5 1.0 pack_yp.1
  16.5 2.9 %collective-permute-start.2 = (f32[58,8,256]{2,1,0:T(8,128)}, f32[58,8,256]{2,1,0:T(8,128)S(1)}, u32[]{:S(2)}, u32[]{:S(2)}) collective-permute-start(f32[58,8,256]{2,1,0:T(8,128)} %get-tuple-element.41), channel_id=1, source_target_pairs={{0,1},{1,2},{2,3},{3,4},{4,5},{5,6},{6,7},{7,0},{8,9},{9,10},{10,1... | collective-permute-start | bytes 1425416 | tf_op jit(solution)/shard_map/ppermute | solution.py:701
  19.4 0.5 collective-permute-done.4.low
  19.9 2.0 %collective-permute-done.5.high = f32[21,16,256]{2,1,0:T(8,128)S(1)} collective-permute-done((f32[21,16,256]{2,1,0:T(8,128)S(1)}, f32[21,16,256]{2,1,0:T(8,128)S(1)}, u32[]{:S(2)}, u32[]{:S(2)}) %collective-permute-start.5) | collective-permute-done | bytes 344096 | tf_op jit(solution)/shard_map/ppermute | solution.py:701
  21.9 1.0 pack_ym.1
  22.9 2.7 %collective-permute-start.6 = (f32[45,8,256]{2,1,0:T(8,128)}, f32[45,8,256]{2,1,0:T(8,128)}, u32[]{:S(2)}, u32[]{:S(2)}) collective-permute-start(f32[45,8,256]{2,1,0:T(8,128)} %get-tuple-element.50), channel_id=1, source_target_pairs={{0,1},{1,2},{2,3},{3,4},{4,5},{5,6},{6,7},{7,0},{8,9},{9,10},{10,1... | collective-permute-start | bytes 1105928 | tf_op jit(solution)/shard_map/ppermute | solution.py:701
  25.6 0.1 add_convert_fusion.flags
  25.7 0.0 collective-permute-done.2.yl
  25.7 2.0 %collective-permute-done.3.yh = f32[58,8,256]{2,1,0:T(8,128)S(1)} collective-permute-done((f32[58,8,256]{2,1,0:T(8,128)}, f32[58,8,256]{2,1,0:T(8,128)S(1)}, u32[]{:S(2)}, u32[]{:S(2)}) %collective-permute-start.3) | collective-permute-done | bytes 475168 | tf_op jit(solution)/shard_map/ppermute | solution.py:701
  27.7 7.2 %pressure_first.1 = (f32[20,32,256]{2,1,0:T(8,128)S(1)}, f32[20,32,256]{2,1,0:T(8,128)S(1)}, f32[8,20,32,256]{3,2,1,0:T(8,128)S(1)}, f32[3,20,32,256]{3,2,1,0:T(8,128)S(1)}, f32[8,128]{1,0:T(8,128)S(1)}) custom-call(f32[4]{0:T(128)S(1)} %add_convert_fusion.flags, f32[5,8]{1,0:T(8,128)S(1)} %copy-done.2, f32[8,16,256]{2,1,0:T(8,128)S(1)} %get-tuple-element.36.ids, ...), custom_call_target="tpu_custom_call" | custom-call | flops 200000000 | tf_op jit(solution)/shard_map/pressure_first/pallas_call | solution.py:687
  34.9 0.0 collective-permute-done.6.yl
  34.9 18.6 %mech_first.1 = (f32[3,15,24,256]{3,2,1,0:T(8,128)S(1)}, f32[3,15,24,256]{3,2,1,0:T(8,128)S(1)}, f32[9,15,24,256]{3,2,1,0:T(8,128)S(1)}, f32[36,10,24,256]{3,2,1,0:T(8,128)S(1)}, f32[128,128]{1,0:T(8,128)S(1)}) custom-call(f32[4]{0:T(128)S(1)} %add_convert_fusion.flags, f32[5,8]{1,0:T(8,128)S(1)} %copy-done.2, f32[8,128]{1,0:T(8,128)S(1)} %get-tuple-element.44.part_p, ...), custom_call_target="tpu_custom_call" | custom-call | flops 200000000 | tf_op jit(solution)/shard_map/mech_first/pallas_call | solution.py:687
  53.5 19.0 %all_to_all.22 = f32[128,1,128]{2,1,0:T(1,128)S(1)} all-to-all(f32[128,1,128]{2,1,0:T(1,128)S(1)} %bitcast.14), channel_id=1, replica_groups=mesh['gx'=16,'gy'=8] {'gx','gy'}, dimensions={0} | all-to-all | bytes 131072 | tf_op jit(solution)/shard_map/all_to_all | solution.py:705
  72.5 1.5 %change.1 = (f32[3,9,24,256]{3,2,1,0:T(8,128)S(1)}, f32[14,32,256]{2,1,0:T(8,128)S(1)}, f32[3,8,16,256]{3,2,1,0:T(8,128)S(1)}, f32[18,16,256]{2,1,0:T(8,128)S(1)}, f32[18,16,256]{2,1,0:T(8,128)S(1)}) custom-call(f32[128,128]{1,0:T(8,128)S(1)} %bitcast.12, f32[3,20,32,256]{3,2,1,0:T(8,128)S(1)} %get-tuple-element.47.t, ...), custom_call_target="tpu_custom_call" | custom-call | tf_op jit(solution)/shard_map/change/pallas_call | solution.py:687
  74.1 0.4 collective-permute-start.8
  74.4 4.5 %collective-permute-start.9 = (f32[18,16,256]{2,1,0:T(8,128)S(1)}, f32[18,16,256]{2,1,0:T(8,128)S(1)}, u32[]{:S(2)}, u32[]{:S(2)}) collective-permute-start(f32[18,16,256]{2,1,0:T(8,128)S(1)} %get-tuple-element.58), channel_id=1, source_target_pairs={{8,0},{16,8},{24,16},{32,24},{40,32},{48,40},{56,48},{64,56},{72,6... | collective-permute-start | bytes 884744 | tf_op jit(solution)/shard_map/ppermute | solution.py:701
  78.9 6.3 %collective-permute-done.8.low = f32[18,16,256]{2,1,0:T(8,128)S(1)} collective-permute-done((f32[18,16,256]{2,1,0:T(8,128)S(1)}, f32[18,16,256]{2,1,0:T(8,128)S(1)}, u32[]{:S(2)}, u32[]{:S(2)}) %collective-permute-start.8) | collective-permute-done | bytes 294944 | tf_op jit(solution)/shard_map/ppermute | solution.py:701
  85.2 0.2 pack_change.1
  85.4 1.9 %collective-permute-start.10 = (f32[504,256]{1,0:T(8,128)S(1)}, f32[504,256]{1,0:T(8,128)S(1)}, u32[]{:S(2)}, u32[]{:S(2)}) collective-permute-start(f32[504,256]{1,0:T(8,128)S(1)} %get-tuple-element.59), channel_id=1, source_target_pairs={{0,1},{1,2},{2,3},{3,4},{4,5},{5,6},{6,7},{7,0},{8,9},{9,10},{10,1... | collective-permute-start | bytes 1548296 | tf_op jit(solution)/shard_map/ppermute | solution.py:701
  87.3 0.0 collective-permute-start.11
  87.3 6.0 %collective-permute-done.10.yl = f32[504,256]{1,0:T(8,128)S(1)} collective-permute-done((f32[504,256]{1,0:T(8,128)S(1)}, f32[504,256]{1,0:T(8,128)S(1)}, u32[]{:S(2)}, u32[]{:S(2)}) %collective-permute-start.10) | collective-permute-done | bytes 516128 | tf_op jit(solution)/shard_map/ppermute | solution.py:701
  93.3 2.8 %collective-permute-done.11.yh = f32[504,256]{1,0:T(8,128)S(1)} collective-permute-done((f32[504,256]{1,0:T(8,128)S(1)}, f32[504,256]{1,0:T(8,128)S(1)}, u32[]{:S(2)}, u32[]{:S(2)}) %collective-permute-start.11) | collective-permute-done | bytes 516128 | tf_op jit(solution)/shard_map/ppermute | solution.py:701
  96.1 4.2 %pressure_next.1 = (f32[20,32,256]{2,1,0:T(8,128)S(1)}, f32[3,15,24,256]{3,2,1,0:T(8,128)S(1)}, f32[3,20,32,256]{3,2,1,0:T(8,128)S(1)}, f32[8,128]{1,0:T(8,128)S(1)}) custom-call(f32[4]{0:T(128)S(1)} %add_convert_fusion.flags, f32[8,20,32,256]{3,2,1,0:T(8,128)S(1)} %get-tuple-element.43.coef, f32[14,32,256]{2,1,0:T(8,128)S(1)} %get-tuple-element.54.p, ...), custom_call_target="tpu_custom_call" | custom-call | flops 200000000 | tf_op jit(solution)/shard_map/pressure_next/pallas_call | solution.py:687
  100.3 14.9 %mech_next.1 = (f32[36,10,24,256]{3,2,1,0:T(8,128)S(1)}, f32[128,128]{1,0:T(8,128)S(1)}) custom-call(f32[8,128]{1,0:T(8,128)S(1)} %get-tuple-element.61.part_p, f32[20,32,256]{2,1,0:T(8,128)S(1)} %get-tuple-element.62.pe.p, f32[8,20,32,256]{3,2,1,0:T(8,128)S(1)} %get-tuple-element.43.coef, f32[3,20,32,256]{3,2,1,0:T(8,128)S(1)} %get-tuple-element.63.t, ...), custom_call_target="tpu_custom_call" | custom-call | flops 200000000 | tf_op jit(solution)/shard_map/mech_next/pallas_call | solution.py:687
  115.2 18.4 %all_to_all.23 = f32[128,1,128]{2,1,0:T(1,128)S(1)} all-to-all(f32[128,1,128]{2,1,0:T(1,128)S(1)} %bitcast.15), channel_id=1, replica_groups=mesh['gx'=16,'gy'=8] {'gx','gy'}, dimensions={0} | all-to-all | bytes 131072 | tf_op jit(solution)/shard_map/all_to_all | solution.py:705
  133.6 1.7 %finish.1 = (f32[3,8,16,256]{3,2,1,0:T(8,128)}, f32[8,16,256]{2,1,0:T(8,128)}) custom-call(f32[128,128]{1,0:T(8,128)S(1)} %bitcast.13, f32[3,20,32,256]{3,2,1,0:T(8,128)S(1)} %get-tuple-element.63.t, f32[20,32,256]{2,1,0:T(8,128)S(1)} %get-tuple-element.62.pe.p, f32[36,10,24,256]{3,2,1,0:T(8,128)S(1)} %get-tuple-element.68.kept, ...), custom_call_target="tpu_custom_call" | custom-call | tf_op jit(solution)/shard_map/finish/pallas_call | solution.py:687
  (11 shorter events, 0.0 us)
Async XLA Ops:
  0.6 21.3 %copy-start = (f32[3,8,16,256]{3,2,1,0:T(8,128)S(1)}, f32[3,8,16,256]{3,2,1,0:T(8,128)}, u32[]{:S(2)}) copy-start(f32[3,8,16,256]{3,2,1,0:T(8,128)} %u.7) | copy-start | bytes 1179652
  0.6 21.3 %copy-start.1 = (f32[3,8,16,256]{3,2,1,0:T(8,128)S(1)}, f32[3,8,16,256]{3,2,1,0:T(8,128)}, u32[]{:S(2)}) copy-start(f32[3,8,16,256]{3,2,1,0:T(8,128)} %b.5) | copy-start | bytes 1179652
  0.7 27.0 %copy-start.2 = (f32[5,8]{1,0:T(8,128)S(1)}, f32[5,8]{1,0:T(8,128)}, u32[]{:S(2)}) copy-start(f32[5,8]{1,0:T(8,128)} %mats.3) | copy-start | bytes 484
  2.3 13.2 %collective-permute-start = (f32[17,16,256]{2,1,0:T(8,128)S(1)}, f32[17,16,256]{2,1,0:T(8,128)S(1)}, u32[]{:S(2)}, u32[]{:S(2)}) collective-permute-start(f32[17,16,256]{2,1,0:T(8,128)S(1)} %get-tuple-element.39), channel_id=1, source_target_pairs={{0,8},{8,16},{16,24},{24,32},{32,40},{40,48},{48,56},{56,64},{64,7... | collective-permute-start | bytes 835592 | tf_op jit(solution)/shard_map/ppermute | solution.py:701
  4.4 11.1 %collective-permute-start.1 = (f32[17,16,256]{2,1,0:T(8,128)S(1)}, f32[17,16,256]{2,1,0:T(8,128)S(1)}, u32[]{:S(2)}, u32[]{:S(2)}) collective-permute-start(f32[17,16,256]{2,1,0:T(8,128)S(1)} %get-tuple-element.40), channel_id=1, source_target_pairs={{8,0},{16,8},{24,16},{32,24},{40,32},{48,40},{56,48},{64,56},{72,6... | collective-permute-start | bytes 835592 | tf_op jit(solution)/shard_map/ppermute | solution.py:701
  9.2 12.7 %collective-permute-start.5 = (f32[21,16,256]{2,1,0:T(8,128)S(1)}, f32[21,16,256]{2,1,0:T(8,128)S(1)}, u32[]{:S(2)}, u32[]{:S(2)}) collective-permute-start(f32[21,16,256]{2,1,0:T(8,128)S(1)} %get-tuple-element.49), channel_id=1, source_target_pairs={{8,0},{16,8},{24,16},{32,24},{40,32},{48,40},{56,48},{64,56},{72,6... | collective-permute-start | bytes 1032200 | tf_op jit(solution)/shard_map/ppermute | solution.py:701
  10.6 9.3 %collective-permute-start.4 = (f32[15,16,256]{2,1,0:T(8,128)S(1)}, f32[15,16,256]{2,1,0:T(8,128)S(1)}, u32[]{:S(2)}, u32[]{:S(2)}) collective-permute-start(f32[15,16,256]{2,1,0:T(8,128)S(1)} %get-tuple-element.48), channel_id=1, source_target_pairs={{0,8},{8,16},{16,24},{24,32},{32,40},{40,48},{48,56},{56,64},{64,7... | collective-permute-start | bytes 737288 | tf_op jit(solution)/shard_map/ppermute | solution.py:701
  16.5 9.2 %collective-permute-start.2 = (f32[58,8,256]{2,1,0:T(8,128)}, f32[58,8,256]{2,1,0:T(8,128)S(1)}, u32[]{:S(2)}, u32[]{:S(2)}) collective-permute-start(f32[58,8,256]{2,1,0:T(8,128)} %get-tuple-element.41), channel_id=1, source_target_pairs={{0,1},{1,2},{2,3},{3,4},{4,5},{5,6},{6,7},{7,0},{8,9},{9,10},{10,1... | collective-permute-start | bytes 1425416 | tf_op jit(solution)/shard_map/ppermute | solution.py:701
  19.4 8.3 %collective-permute-start.3 = (f32[58,8,256]{2,1,0:T(8,128)}, f32[58,8,256]{2,1,0:T(8,128)S(1)}, u32[]{:S(2)}, u32[]{:S(2)}) collective-permute-start(f32[58,8,256]{2,1,0:T(8,128)} %get-tuple-element.42), channel_id=1, source_target_pairs={{1,0},{2,1},{3,2},{4,3},{5,4},{6,5},{7,6},{0,7},{9,8},{10,9},{11,1... | collective-permute-start | bytes 1425416 | tf_op jit(solution)/shard_map/ppermute | solution.py:701
  22.9 12.0 %collective-permute-start.6 = (f32[45,8,256]{2,1,0:T(8,128)}, f32[45,8,256]{2,1,0:T(8,128)}, u32[]{:S(2)}, u32[]{:S(2)}) collective-permute-start(f32[45,8,256]{2,1,0:T(8,128)} %get-tuple-element.50), channel_id=1, source_target_pairs={{0,1},{1,2},{2,3},{3,4},{4,5},{5,6},{6,7},{7,0},{8,9},{9,10},{10,1... | collective-permute-start | bytes 1105928 | tf_op jit(solution)/shard_map/ppermute | solution.py:701
  25.6 9.3 %collective-permute-start.7 = (f32[45,8,256]{2,1,0:T(8,128)}, f32[45,8,256]{2,1,0:T(8,128)}, u32[]{:S(2)}, u32[]{:S(2)}) collective-permute-start(f32[45,8,256]{2,1,0:T(8,128)} %get-tuple-element.51), channel_id=1, source_target_pairs={{1,0},{2,1},{3,2},{4,3},{5,4},{6,5},{7,6},{0,7},{9,8},{10,9},{11,1... | collective-permute-start | bytes 1105928 | tf_op jit(solution)/shard_map/ppermute | solution.py:701
  74.1 11.2 %collective-permute-start.8 = (f32[18,16,256]{2,1,0:T(8,128)S(1)}, f32[18,16,256]{2,1,0:T(8,128)S(1)}, u32[]{:S(2)}, u32[]{:S(2)}) collective-permute-start(f32[18,16,256]{2,1,0:T(8,128)S(1)} %get-tuple-element.57), channel_id=1, source_target_pairs={{0,8},{8,16},{16,24},{24,32},{32,40},{40,48},{48,56},{56,64},{64,7... | collective-permute-start | bytes 884744 | tf_op jit(solution)/shard_map/ppermute | solution.py:701
  74.4 10.8 %collective-permute-start.9 = (f32[18,16,256]{2,1,0:T(8,128)S(1)}, f32[18,16,256]{2,1,0:T(8,128)S(1)}, u32[]{:S(2)}, u32[]{:S(2)}) collective-permute-start(f32[18,16,256]{2,1,0:T(8,128)S(1)} %get-tuple-element.58), channel_id=1, source_target_pairs={{8,0},{16,8},{24,16},{32,24},{40,32},{48,40},{56,48},{64,56},{72,6... | collective-permute-start | bytes 884744 | tf_op jit(solution)/shard_map/ppermute | solution.py:701
  85.4 7.9 %collective-permute-start.10 = (f32[504,256]{1,0:T(8,128)S(1)}, f32[504,256]{1,0:T(8,128)S(1)}, u32[]{:S(2)}, u32[]{:S(2)}) collective-permute-start(f32[504,256]{1,0:T(8,128)S(1)} %get-tuple-element.59), channel_id=1, source_target_pairs={{0,1},{1,2},{2,3},{3,4},{4,5},{5,6},{6,7},{7,0},{8,9},{9,10},{10,1... | collective-permute-start | bytes 1548296 | tf_op jit(solution)/shard_map/ppermute | solution.py:701
  87.3 8.8 %collective-permute-start.11 = (f32[504,256]{1,0:T(8,128)S(1)}, f32[504,256]{1,0:T(8,128)S(1)}, u32[]{:S(2)}, u32[]{:S(2)}) collective-permute-start(f32[504,256]{1,0:T(8,128)S(1)} %get-tuple-element.60), channel_id=1, source_target_pairs={{1,0},{2,1},{3,2},{4,3},{5,4},{6,5},{7,6},{0,7},{9,8},{10,9},{11,1... | collective-permute-start | bytes 1548296 | tf_op jit(solution)/shard_map/ppermute | solution.py:701

commit v5 on v4

--- a/solution.py
+++ b/solution.py
@@ -123,31 +123,30 @@
 
 
 def pack_y_pressure_kernel(ids, p, f, low, high, up, dn):
+    def put(k, n, source):
+        ref, i = source
+        up[k : k + n] = ref[i, NY - n : NY]
+        dn[k : k + n] = ref[i, 0:n]
+
     for x in range(XE):
-        ref, i = pick(x, low, ids, high, (0, 0), LOW)
-        up[x] = ref[i, 8:16]
-        dn[x] = ref[i, 0:8]
-        ref, i = pick(x, low, p, high, (6, 6), LOW)
-        up[20 + x] = ref[i, 8:16]
-        dn[20 + x] = ref[i, 0:8]
+        put(6 * x, 6, pick(x, low, ids, high, (0, 0), LOW))
+        put(120 + 6 * x, 6, pick(x, low, p, high, (6, 6), LOW))
     for x in range(XE - 2):
-        ref, i = pick(x, low, f, high, (12, 12), LOW - 1)
-        up[40 + x] = ref[i, 8:16]
-        dn[40 + x] = ref[i, 0:8]
+        put(240 + 5 * x, 5, pick(x, low, f, high, (12, 12), LOW - 1))
 
 
 def pack_y_mech_kernel(u, b, low, high, up, dn):
+    def put(k, n, source):
+        ref, i = source
+        up[k : k + n] = ref[i, NY - n : NY]
+        dn[k : k + n] = ref[i, 0:n]
+
     for a in range(3):
         for m in range(ME):
-            ref, i = pick(m, low, u.at[a], high, (3 * a, 4 * a), ML)
-            k, r = 8 * a + m // 2, 4 * (m % 2)
-            up[k, r : r + 4] = ref[i, 12:16]
-            dn[k, r : r + 4] = ref[i, 0:4]
+            put(4 * (ME * a + m), 4, pick(m, low, u.at[a], high, (3 * a, 4 * a), ML))
         for m in range(ME - 2):
-            ref, i = pick(m, low, b.at[a], high, (9 + 2 * a, 12 + 3 * a), ML - 1)
-            k, r = 24 + 7 * a + m // 2, 4 * (m % 2)
-            up[k, r : r + 4] = ref[i, 12:16]
-            dn[k, r : r + 4] = ref[i, 0:4]
+            source = pick(m, low, b.at[a], high, (9 + 2 * a, 12 + 3 * a), ML - 1)
+            put(180 + 3 * (13 * a + m), 3, source)
 
 
 def masked(x, n_low, flags, v, lo, hi):
@@ -160,24 +159,32 @@
     return v * edge, lo * edge, hi * edge
 
 
-def fill(out, n, n_low, own, low, high, first, yl, yh, k, flags):
+def fill(out, n, n_low, own, low, high, first, yl, yh, k, flags, rows):
+    zero = jnp.zeros((8 - rows, NZ), F32)
     for x in range(n):
         ref, i = pick(x, low, own, high, first, n_low)
-        v, lo, hi = masked(x, n_low, flags, ref[i], yl[k + x], yh[k + x])
+        j = k + rows * x
+        v, lo, hi = masked(x, n_low, flags, ref[i], yl[j : j + rows], yh[j : j + rows])
+        out[x, 0 : 8 - rows] = zero
+        out[x, 8 - rows : 8] = lo
         out[x, 8:24] = v
-        out[x, 0:8] = lo
-        out[x, 24:32] = hi
-
-
-def fill_mech(out, n, n_low, own, low, high, first, yl, yh, k, flags, offset):
+        out[x, 24 : 24 + rows] = hi
+        out[x, 24 + rows : 32] = zero
+
+
+def fill_mech(out, n, n_low, own, low, high, first, yl, yh, k, flags, offset, rows):
     for x in range(n):
         ref, i = pick(x, low, own, high, first, n_low)
-        r = 4 * (x % 2)
-        lo, hi = yl[k + x // 2, r : r + 4], yh[k + x // 2, r : r + 4]
+        j = k + rows * x
+        lo, hi = yl[j : j + rows], yh[j : j + rows]
         v, lo, hi = masked(x, n_low, flags, ref[i], lo, hi)
-        out[x + offset, 0:4] = lo
-        out[x + offset, 4:20] = v
-        out[x + offset, 20:24] = hi
+        y = x + offset
+        if rows < 4:
+            out[y, 0 : 4 - rows] = jnp.zeros((4 - rows, NZ), F32)
+            out[y, 20 + rows : 24] = jnp.zeros((4 - rows, NZ), F32)
+        out[y, 4 - rows : 4] = lo
+        out[y, 4:20] = v
+        out[y, 20 : 20 + rows] = hi
 
 
 def two_sum(a, b):
@@ -322,9 +329,9 @@
     fe, perm, stor, n, k,
 ):
     cx, cy, cz, inv, stab, base, biot, total = (coef.at[i] for i in range(8))
-    fill(code, XE, LOW, ids, low, high, (0, 0), yl, yh, 0, flags)
-    fill(pe, XE, LOW, p, low, high, (6, 6), yl, yh, 20, flags)
-    fill(fe.at[1 : XE - 1], XE - 2, LOW - 1, f, low, high, (12, 12), yl, yh, 40, None)
+    fill(code, XE, LOW, ids, low, high, (0, 0), yl, yh, 0, flags, 6)
+    fill(pe, XE, LOW, p, low, high, (6, 6), yl, yh, 120, flags, 6)
+    fill(fe.at[1 : XE - 1], XE - 2, LOW - 1, f, low, high, (12, 12), yl, yh, 240, None, 5)
 
     def tables(x):
         l, s, k, st, bi = lookup(code[x], mats, range(5))
@@ -390,8 +397,8 @@
             out[24:30] = hi
             out[30:32] = zero
     for x in range(XE):
-        j = 344 + 8 * x
-        lo, hi = yl[j : j + 8] * flags[2], yh[j : j + 8] * flags[3]
+        j = 342 + 6 * x
+        lo, hi = yl[j : j + 6] * flags[2], yh[j : j + 6] * flags[3]
         if not LOW <= x < LOW + NX:
             lo, hi = lo * edge(x, LOW), hi * edge(x, LOW)
         if 3 <= x < 17:
@@ -399,8 +406,10 @@
         else:
             ref = low.at[15 + x] if x < 3 else high.at[15 + x - 17]
             pe[x, 8:24] = ref[...] * edge(x, LOW)
-        pe[x, 0:8] = lo
-        pe[x, 24:32] = hi
+        pe[x, 0:2] = zero
+        pe[x, 2:8] = lo
+        pe[x, 24:30] = hi
+        pe[x, 30:32] = zero
 
     def start(x):
         c2 = de[2, x]
@@ -572,9 +581,9 @@
 ):
     sx, sy, sz, half, lame, h0, h1, h2, kk = (mc.at[i] for i in range(9))
     for a in range(3):
-        fill_mech(ue.at[a], ME, ML, u.at[a], low, high, (3 * a, 4 * a), yl, yh, 8 * a, flags, 0)
+        fill_mech(ue.at[a], ME, ML, u.at[a], low, high, (3 * a, 4 * a), yl, yh, 60 * a, flags, 0, 4)
         fill_mech(
-            be.at[a], ME - 2, ML - 1, b.at[a], low, high, (9 + 2 * a, 12 + 3 * a), yl, yh, 24 + 7 * a, None, 1
+            be.at[a], ME - 2, ML - 1, b.at[a], low, high, (9 + 2 * a, 12 + 3 * a), yl, yh, 180 + 39 * a, None, 1, 3
         )
 
     def tables(m):
@@ -668,9 +677,9 @@
             ref, r = p.at[x - 3], 8
         else:
             ref, r = high.at[15 + x - 17], 0
-        k = 344 + 8 * x
-        up[k : k + 8] = ref[r + 8 : r + 16]
-        dn[k : k + 8] = ref[r : r + 8]
+        k = 342 + 6 * x
+        up[k : k + 6] = ref[r + 10 : r + 16]
+        dn[k : k + 6] = ref[r : r + 6]
 
 
 def finish_kernel(rows, t, p, kept, u, unew, pnew):
@@ -720,10 +729,10 @@
     low_p, high_p = neighbours("gx", gx_size, up_p, dn_p)
     low_m, high_m = neighbours("gx", gx_size, up_m, dn_m)
     up, dn = call(
-        pack_y_pressure_kernel, "pack_yp", (own_code, own_p, own_f, low_p, high_p), [(58, 8, NZ), (58, 8, NZ)], limit=4
+        pack_y_pressure_kernel, "pack_yp", (own_code, own_p, own_f, low_p, high_p), [(336, NZ), (336, NZ)], limit=4
     )
     yl_p, yh_p = neighbours("gy", gy_size, up, dn)
-    up, dn = call(pack_y_mech_kernel, "pack_ym", (u, b, low_m, high_m), [(45, 8, NZ), (45, 8, NZ)], limit=4)
+    up, dn = call(pack_y_mech_kernel, "pack_ym", (u, b, low_m, high_m), [(304, NZ), (304, NZ)], limit=4)
     yl_m, yh_m = neighbours("gy", gy_size, up, dn)
     code, pe, coef, t, part_p = call(
         pressure_first_kernel,
@@ -732,7 +741,7 @@
         [(XE, *wide), (XE, *wide), (8, XE, *wide), (3, XE, *wide), (8, 128)],
         [(XE, *wide)] * 3 + [(4, XE, *wide), (2, XE, *wide)],
         [SM, SM] + [VM] * 7,
-        COST,
+        2_000_000_000,
     )
     mech_scratch = [
         (4, GENS, 3, NX + 1, *mech),
@@ -761,7 +770,7 @@
         [(3, NX + 1, *mech), (PK, *wide), (3, NX, NY, NZ), (18, NY, NZ), (18, NY, NZ)],
     )
     low, high = neighbours("gx", gx_size, up, dn)
-    up, dn = call(pack_change_kernel, "pack_change", (du, p1, low, high), [(504, NZ), (504, NZ)])
+    up, dn = call(pack_change_kernel, "pack_change", (du, p1, low, high), [(464, NZ), (464, NZ)])
     yl, yh = neighbours("gy", gy_size, up, dn)
     pe, ue, t, part_p = call(
         pressure_next_kernel,

time: 136 us -> 133 us (0.978)
  waiting for transfers between devices: 24.4 us -> 22.7 us
where the time goes in v5:
time: 133 us
  Pallas kernels  51.8 us (39%)
  blocking collectives  37.1 us (28%)
  waiting for transfers between devices  22.7 us (17%)
  starting transfers between devices  20.7 us (16%)
    pallas_call x10, Pallas kernels, call(): pl.pallas_call(kernel, name=name, out_shape=[jax.ShapeDtypeStruct(o, F32)...  51.8 us
    all_to_all x2, blocking collectives, gather_rows(): return lax.all_to_all(part, ('gx', 'gy'), 0, 0, tiled=True)  37.1 us
    ppermute x6, waiting for transfers between devices, neighbours(): lax.ppermute(up, axis, ring)  17.3 us
    ppermute x6, starting transfers between devices, neighbours(): lax.ppermute(dn, axis, [(b, a) for a, b in ring])  10.7 us
    ppermute x6, starting transfers between devices, neighbours(): lax.ppermute(up, axis, ring)  10 us
    ppermute x6, waiting for transfers between devices, neighbours(): lax.ppermute(dn, axis, [(b, a) for a, b in ring])  5.43 us
  transfers between devices with their start and end apart: 12, of which 7 were waited for; matrix products, arithmetic and copies ran while one was open for 0% of the time, Pallas kernels for 7%

profile of v5, /device:TPU:1, one launch (start us, length us, event | category | flops | bytes accessed | tf_op | source)
XLA Modules:
  0.0 133.2 jit_solution(782003674961419062)
XLA Ops:
  0.7 1.5 %pack_x.1 = (f32[17,16,256]{2,1,0:T(8,128)S(1)}, f32[17,16,256]{2,1,0:T(8,128)S(1)}, f32[15,16,256]{2,1,0:T(8,128)S(1)}, f32[21,16,256]{2,1,0:T(8,128)S(1)}, f32...) custom-call(s32[8,16,256]{2,1,0:T(8,128)} %ids.1, f32[8,16,256]{2,1,0:T(8,128)} %p.1, ...), custom_call_target="tpu_custom_call" | custom-call | tf_op jit(solution)/shard_map/pack_x/pallas_call | solution.py:696
  2.2 2.1 %collective-permute-start = (f32[17,16,256]{2,1,0:T(8,128)S(1)}, f32[17,16,256]{2,1,0:T(8,128)S(1)}, u32[]{:S(2)}, u32[]{:S(2)}) collective-permute-start(f32[17,16,256]{2,1,0:T(8,128)S(1)} %get-tuple-element.39), channel_id=1, source_target_pairs={{0,8},{8,16},{16,24},{24,32},{32,40},{40,48},{48,56},{56,64},{64,7... | collective-permute-start | bytes 835592 | tf_op jit(solution)/shard_map/ppermute | solution.py:710
  4.3 4.8 %collective-permute-start.1 = (f32[17,16,256]{2,1,0:T(8,128)S(1)}, f32[17,16,256]{2,1,0:T(8,128)S(1)}, u32[]{:S(2)}, u32[]{:S(2)}) collective-permute-start(f32[17,16,256]{2,1,0:T(8,128)S(1)} %get-tuple-element.40), channel_id=1, source_target_pairs={{8,0},{16,8},{24,16},{32,24},{40,32},{48,40},{56,48},{64,56},{72,6... | collective-permute-start | bytes 835592 | tf_op jit(solution)/shard_map/ppermute | solution.py:710
  9.1 1.4 %collective-permute-start.5 = (f32[21,16,256]{2,1,0:T(8,128)S(1)}, f32[21,16,256]{2,1,0:T(8,128)S(1)}, u32[]{:S(2)}, u32[]{:S(2)}) collective-permute-start(f32[21,16,256]{2,1,0:T(8,128)S(1)} %get-tuple-element.49), channel_id=1, source_target_pairs={{8,0},{16,8},{24,16},{32,24},{40,32},{48,40},{56,48},{64,56},{72,6... | collective-permute-start | bytes 1032200 | tf_op jit(solution)/shard_map/ppermute | solution.py:710
  10.5 0.1 collective-permute-start.4
  10.6 4.8 %collective-permute-done.low = f32[17,16,256]{2,1,0:T(8,128)S(1)} collective-permute-done((f32[17,16,256]{2,1,0:T(8,128)S(1)}, f32[17,16,256]{2,1,0:T(8,128)S(1)}, u32[]{:S(2)}, u32[]{:S(2)}) %collective-permute-start) | collective-permute-done | bytes 278560 | tf_op jit(solution)/shard_map/ppermute | solution.py:710
  15.4 0.0 collective-permute-done.1.high
  15.4 1.0 pack_yp.1
  16.4 2.9 %collective-permute-start.2 = (f32[336,256]{1,0:T(8,128)}, f32[336,256]{1,0:T(8,128)S(1)}, u32[]{:S(2)}, u32[]{:S(2)}) collective-permute-start(f32[336,256]{1,0:T(8,128)} %get-tuple-element.41), channel_id=1, source_target_pairs={{0,1},{1,2},{2,3},{3,4},{4,5},{5,6},{6,7},{7,0},{8,9},{9,10},{10,1... | collective-permute-start | bytes 1032200 | tf_op jit(solution)/shard_map/ppermute | solution.py:710
  19.3 0.0 collective-permute-start.3
  19.3 0.6 collective-permute-done.4.low
  19.8 2.0 %collective-permute-done.5.high = f32[21,16,256]{2,1,0:T(8,128)S(1)} collective-permute-done((f32[21,16,256]{2,1,0:T(8,128)S(1)}, f32[21,16,256]{2,1,0:T(8,128)S(1)}, u32[]{:S(2)}, u32[]{:S(2)}) %collective-permute-start.5) | collective-permute-done | bytes 344096 | tf_op jit(solution)/shard_map/ppermute | solution.py:710
  21.9 1.0 pack_ym.1
  22.8 2.7 %collective-permute-start.6 = (f32[304,256]{1,0:T(8,128)}, f32[304,256]{1,0:T(8,128)S(1)}, u32[]{:S(2)}, u32[]{:S(2)}) collective-permute-start(f32[304,256]{1,0:T(8,128)} %get-tuple-element.50), channel_id=1, source_target_pairs={{0,1},{1,2},{2,3},{3,4},{4,5},{5,6},{6,7},{7,0},{8,9},{9,10},{10,1... | collective-permute-start | bytes 933896 | tf_op jit(solution)/shard_map/ppermute | solution.py:710
  25.6 0.1 add_convert_fusion.flags
  25.6 0.6 collective-permute-done.3.yh
  26.3 7.7 %pressure_first.1 = (f32[20,32,256]{2,1,0:T(8,128)S(1)}, f32[20,32,256]{2,1,0:T(8,128)S(1)}, f32[8,20,32,256]{3,2,1,0:T(8,128)S(1)}, f32[3,20,32,256]{3,2,1,0:T(8,128)S(1)}, f32[8,128]{1,0:T(8,128)S(1)}) custom-call(f32[4]{0:T(128)S(1)} %add_convert_fusion.flags, f32[5,8]{1,0:T(8,128)S(1)} %copy-done.2, f32[8,16,256]{2,1,0:T(8,128)S(1)} %get-tuple-element.36.ids, ...), custom_call_target="tpu_custom_call" | custom-call | flops 2000000000 | tf_op jit(solution)/shard_map/pressure_first/pallas_call | solution.py:696
  34.0 0.0 collective-permute-done.7.yh
  34.0 18.1 %mech_first.1 = (f32[3,15,24,256]{3,2,1,0:T(8,128)S(1)}, f32[3,15,24,256]{3,2,1,0:T(8,128)S(1)}, f32[9,15,24,256]{3,2,1,0:T(8,128)S(1)}, f32[36,10,24,256]{3,2,1,0:T(8,128)S(1)}, f32[128,128]{1,0:T(8,128)S(1)}) custom-call(f32[4]{0:T(128)S(1)} %add_convert_fusion.flags, f32[5,8]{1,0:T(8,128)S(1)} %copy-done.2, f32[8,128]{1,0:T(8,128)S(1)} %get-tuple-element.44.part_p, ...), custom_call_target="tpu_custom_call" | custom-call | flops 200000000 | tf_op jit(solution)/shard_map/mech_first/pallas_call | solution.py:696
  52.1 18.7 %all_to_all.22 = f32[128,1,128]{2,1,0:T(1,128)S(1)} all-to-all(f32[128,1,128]{2,1,0:T(1,128)S(1)} %bitcast.14), channel_id=1, replica_groups=mesh['gx'=16,'gy'=8] {'gx','gy'}, dimensions={0} | all-to-all | bytes 131072 | tf_op jit(solution)/shard_map/all_to_all | solution.py:714
  70.8 1.5 %change.1 = (f32[3,9,24,256]{3,2,1,0:T(8,128)S(1)}, f32[14,32,256]{2,1,0:T(8,128)S(1)}, f32[3,8,16,256]{3,2,1,0:T(8,128)S(1)}, f32[18,16,256]{2,1,0:T(8,128)S(1)}, f32[18,16,256]{2,1,0:T(8,128)S(1)}) custom-call(f32[128,128]{1,0:T(8,128)S(1)} %bitcast.12, f32[3,20,32,256]{3,2,1,0:T(8,128)S(1)} %get-tuple-element.47.t, ...), custom_call_target="tpu_custom_call" | custom-call | tf_op jit(solution)/shard_map/change/pallas_call | solution.py:696
  72.3 0.4 collective-permute-start.8
  72.7 4.5 %collective-permute-start.9 = (f32[18,16,256]{2,1,0:T(8,128)S(1)}, f32[18,16,256]{2,1,0:T(8,128)S(1)}, u32[]{:S(2)}, u32[]{:S(2)}) collective-permute-start(f32[18,16,256]{2,1,0:T(8,128)S(1)} %get-tuple-element.58), channel_id=1, source_target_pairs={{8,0},{16,8},{24,16},{32,24},{40,32},{48,40},{56,48},{64,56},{72,6... | collective-permute-start | bytes 884744 | tf_op jit(solution)/shard_map/ppermute | solution.py:710
  77.2 6.3 %collective-permute-done.8.low = f32[18,16,256]{2,1,0:T(8,128)S(1)} collective-permute-done((f32[18,16,256]{2,1,0:T(8,128)S(1)}, f32[18,16,256]{2,1,0:T(8,128)S(1)}, u32[]{:S(2)}, u32[]{:S(2)}) %collective-permute-start.8) | collective-permute-done | bytes 294944 | tf_op jit(solution)/shard_map/ppermute | solution.py:710
  83.5 0.2 pack_change.1
  83.7 1.9 %collective-permute-start.10 = (f32[464,256]{1,0:T(8,128)S(1)}, f32[464,256]{1,0:T(8,128)S(1)}, u32[]{:S(2)}, u32[]{:S(2)}) collective-permute-start(f32[464,256]{1,0:T(8,128)S(1)} %get-tuple-element.59), channel_id=1, source_target_pairs={{0,1},{1,2},{2,3},{3,4},{4,5},{5,6},{6,7},{7,0},{8,9},{9,10},{10,1... | collective-permute-start | bytes 1425416 | tf_op jit(solution)/shard_map/ppermute | solution.py:710
  85.6 5.6 %collective-permute-done.10.yl = f32[464,256]{1,0:T(8,128)S(1)} collective-permute-done((f32[464,256]{1,0:T(8,128)S(1)}, f32[464,256]{1,0:T(8,128)S(1)}, u32[]{:S(2)}, u32[]{:S(2)}) %collective-permute-start.10) | collective-permute-done | bytes 475168 | tf_op jit(solution)/shard_map/ppermute | solution.py:710
  91.2 2.8 %collective-permute-done.11.yh = f32[464,256]{1,0:T(8,128)S(1)} collective-permute-done((f32[464,256]{1,0:T(8,128)S(1)}, f32[464,256]{1,0:T(8,128)S(1)}, u32[]{:S(2)}, u32[]{:S(2)}) %collective-permute-start.11) | collective-permute-done | bytes 475168 | tf_op jit(solution)/shard_map/ppermute | solution.py:710
  93.9 4.2 %pressure_next.1 = (f32[20,32,256]{2,1,0:T(8,128)S(1)}, f32[3,15,24,256]{3,2,1,0:T(8,128)S(1)}, f32[3,20,32,256]{3,2,1,0:T(8,128)S(1)}, f32[8,128]{1,0:T(8,128)S(1)}) custom-call(f32[4]{0:T(128)S(1)} %add_convert_fusion.flags, f32[8,20,32,256]{3,2,1,0:T(8,128)S(1)} %get-tuple-element.43.coef, f32[14,32,256]{2,1,0:T(8,128)S(1)} %get-tuple-element.54.p, ...), custom_call_target="tpu_custom_call" | custom-call | flops 200000000 | tf_op jit(solution)/shard_map/pressure_next/pallas_call | solution.py:696
  98.1 14.9 %mech_next.1 = (f32[36,10,24,256]{3,2,1,0:T(8,128)S(1)}, f32[128,128]{1,0:T(8,128)S(1)}) custom-call(f32[8,128]{1,0:T(8,128)S(1)} %get-tuple-element.61.part_p, f32[20,32,256]{2,1,0:T(8,128)S(1)} %get-tuple-element.62.pe.p, f32[8,20,32,256]{3,2,1,0:T(8,128)S(1)} %get-tuple-element.43.coef, f32[3,20,32,256]{3,2,1,0:T(8,128)S(1)} %get-tuple-element.63.t, ...), custom_call_target="tpu_custom_call" | custom-call | flops 200000000 | tf_op jit(solution)/shard_map/mech_next/pallas_call | solution.py:696
  113.1 18.4 %all_to_all.23 = f32[128,1,128]{2,1,0:T(1,128)S(1)} all-to-all(f32[128,1,128]{2,1,0:T(1,128)S(1)} %bitcast.15), channel_id=1, replica_groups=mesh['gx'=16,'gy'=8] {'gx','gy'}, dimensions={0} | all-to-all | bytes 131072 | tf_op jit(solution)/shard_map/all_to_all | solution.py:714
  131.5 1.7 %finish.1 = (f32[3,8,16,256]{3,2,1,0:T(8,128)}, f32[8,16,256]{2,1,0:T(8,128)}) custom-call(f32[128,128]{1,0:T(8,128)S(1)} %bitcast.13, f32[3,20,32,256]{3,2,1,0:T(8,128)S(1)} %get-tuple-element.63.t, f32[20,32,256]{2,1,0:T(8,128)S(1)} %get-tuple-element.62.pe.p, f32[36,10,24,256]{3,2,1,0:T(8,128)S(1)} %get-tuple-element.68.kept, ...), custom_call_target="tpu_custom_call" | custom-call | tf_op jit(solution)/shard_map/finish/pallas_call | solution.py:696
  (11 shorter events, 0.0 us)
Async XLA Ops:
  0.6 21.2 %copy-start = (f32[3,8,16,256]{3,2,1,0:T(8,128)S(1)}, f32[3,8,16,256]{3,2,1,0:T(8,128)}, u32[]{:S(2)}) copy-start(f32[3,8,16,256]{3,2,1,0:T(8,128)} %u.7) | copy-start | bytes 1179652
  0.6 21.2 %copy-start.1 = (f32[3,8,16,256]{3,2,1,0:T(8,128)S(1)}, f32[3,8,16,256]{3,2,1,0:T(8,128)}, u32[]{:S(2)}) copy-start(f32[3,8,16,256]{3,2,1,0:T(8,128)} %b.5) | copy-start | bytes 1179652
  0.7 25.6 %copy-start.2 = (f32[5,8]{1,0:T(8,128)S(1)}, f32[5,8]{1,0:T(8,128)}, u32[]{:S(2)}) copy-start(f32[5,8]{1,0:T(8,128)} %mats.3) | copy-start | bytes 484
  2.2 13.2 %collective-permute-start = (f32[17,16,256]{2,1,0:T(8,128)S(1)}, f32[17,16,256]{2,1,0:T(8,128)S(1)}, u32[]{:S(2)}, u32[]{:S(2)}) collective-permute-start(f32[17,16,256]{2,1,0:T(8,128)S(1)} %get-tuple-element.39), channel_id=1, source_target_pairs={{0,8},{8,16},{16,24},{24,32},{32,40},{40,48},{48,56},{56,64},{64,7... | collective-permute-start | bytes 835592 | tf_op jit(solution)/shard_map/ppermute | solution.py:710
  4.3 11.1 %collective-permute-start.1 = (f32[17,16,256]{2,1,0:T(8,128)S(1)}, f32[17,16,256]{2,1,0:T(8,128)S(1)}, u32[]{:S(2)}, u32[]{:S(2)}) collective-permute-start(f32[17,16,256]{2,1,0:T(8,128)S(1)} %get-tuple-element.40), channel_id=1, source_target_pairs={{8,0},{16,8},{24,16},{32,24},{40,32},{48,40},{56,48},{64,56},{72,6... | collective-permute-start | bytes 835592 | tf_op jit(solution)/shard_map/ppermute | solution.py:710
  9.1 12.7 %collective-permute-start.5 = (f32[21,16,256]{2,1,0:T(8,128)S(1)}, f32[21,16,256]{2,1,0:T(8,128)S(1)}, u32[]{:S(2)}, u32[]{:S(2)}) collective-permute-start(f32[21,16,256]{2,1,0:T(8,128)S(1)} %get-tuple-element.49), channel_id=1, source_target_pairs={{8,0},{16,8},{24,16},{32,24},{40,32},{48,40},{56,48},{64,56},{72,6... | collective-permute-start | bytes 1032200 | tf_op jit(solution)/shard_map/ppermute | solution.py:710
  10.5 9.3 %collective-permute-start.4 = (f32[15,16,256]{2,1,0:T(8,128)S(1)}, f32[15,16,256]{2,1,0:T(8,128)S(1)}, u32[]{:S(2)}, u32[]{:S(2)}) collective-permute-start(f32[15,16,256]{2,1,0:T(8,128)S(1)} %get-tuple-element.48), channel_id=1, source_target_pairs={{0,8},{8,16},{16,24},{24,32},{32,40},{40,48},{48,56},{56,64},{64,7... | collective-permute-start | bytes 737288 | tf_op jit(solution)/shard_map/ppermute | solution.py:710
  16.4 9.3 %collective-permute-start.2 = (f32[336,256]{1,0:T(8,128)}, f32[336,256]{1,0:T(8,128)S(1)}, u32[]{:S(2)}, u32[]{:S(2)}) collective-permute-start(f32[336,256]{1,0:T(8,128)} %get-tuple-element.41), channel_id=1, source_target_pairs={{0,1},{1,2},{2,3},{3,4},{4,5},{5,6},{6,7},{7,0},{8,9},{9,10},{10,1... | collective-permute-start | bytes 1032200 | tf_op jit(solution)/shard_map/ppermute | solution.py:710
  19.3 7.0 %collective-permute-start.3 = (f32[336,256]{1,0:T(8,128)}, f32[336,256]{1,0:T(8,128)}, u32[]{:S(2)}, u32[]{:S(2)}) collective-permute-start(f32[336,256]{1,0:T(8,128)} %get-tuple-element.42), channel_id=1, source_target_pairs={{1,0},{2,1},{3,2},{4,3},{5,4},{6,5},{7,6},{0,7},{9,8},{10,9},{11,1... | collective-permute-start | bytes 1032200 | tf_op jit(solution)/shard_map/ppermute | solution.py:710
  22.8 11.1 %collective-permute-start.6 = (f32[304,256]{1,0:T(8,128)}, f32[304,256]{1,0:T(8,128)S(1)}, u32[]{:S(2)}, u32[]{:S(2)}) collective-permute-start(f32[304,256]{1,0:T(8,128)} %get-tuple-element.50), channel_id=1, source_target_pairs={{0,1},{1,2},{2,3},{3,4},{4,5},{5,6},{6,7},{7,0},{8,9},{9,10},{10,1... | collective-permute-start | bytes 933896 | tf_op jit(solution)/shard_map/ppermute | solution.py:710
  25.6 8.4 %collective-permute-start.7 = (f32[304,256]{1,0:T(8,128)}, f32[304,256]{1,0:T(8,128)S(1)}, u32[]{:S(2)}, u32[]{:S(2)}) collective-permute-start(f32[304,256]{1,0:T(8,128)} %get-tuple-element.51), channel_id=1, source_target_pairs={{1,0},{2,1},{3,2},{4,3},{5,4},{6,5},{7,6},{0,7},{9,8},{10,9},{11,1... | collective-permute-start | bytes 933896 | tf_op jit(solution)/shard_map/ppermute | solution.py:710
  72.3 11.2 %collective-permute-start.8 = (f32[18,16,256]{2,1,0:T(8,128)S(1)}, f32[18,16,256]{2,1,0:T(8,128)S(1)}, u32[]{:S(2)}, u32[]{:S(2)}) collective-permute-start(f32[18,16,256]{2,1,0:T(8,128)S(1)} %get-tuple-element.57), channel_id=1, source_target_pairs={{0,8},{8,16},{16,24},{24,32},{32,40},{40,48},{48,56},{56,64},{64,7... | collective-permute-start | bytes 884744 | tf_op jit(solution)/shard_map/ppermute | solution.py:710
  72.7 10.8 %collective-permute-start.9 = (f32[18,16,256]{2,1,0:T(8,128)S(1)}, f32[18,16,256]{2,1,0:T(8,128)S(1)}, u32[]{:S(2)}, u32[]{:S(2)}) collective-permute-start(f32[18,16,256]{2,1,0:T(8,128)S(1)} %get-tuple-element.58), channel_id=1, source_target_pairs={{8,0},{16,8},{24,16},{32,24},{40,32},{48,40},{56,48},{64,56},{72,6... | collective-permute-start | bytes 884744 | tf_op jit(solution)/shard_map/ppermute | solution.py:710
  83.7 7.5 %collective-permute-start.10 = (f32[464,256]{1,0:T(8,128)S(1)}, f32[464,256]{1,0:T(8,128)S(1)}, u32[]{:S(2)}, u32[]{:S(2)}) collective-permute-start(f32[464,256]{1,0:T(8,128)S(1)} %get-tuple-element.59), channel_id=1, source_target_pairs={{0,1},{1,2},{2,3},{3,4},{4,5},{5,6},{6,7},{7,0},{8,9},{9,10},{10,1... | collective-permute-start | bytes 1425416 | tf_op jit(solution)/shard_map/ppermute | solution.py:710
  85.6 8.4 %collective-permute-start.11 = (f32[464,256]{1,0:T(8,128)S(1)}, f32[464,256]{1,0:T(8,128)S(1)}, u32[]{:S(2)}, u32[]{:S(2)}) collective-permute-start(f32[464,256]{1,0:T(8,128)S(1)} %get-tuple-element.60), channel_id=1, source_target_pairs={{1,0},{2,1},{3,2},{4,3},{5,4},{6,5},{7,6},{0,7},{9,8},{10,9},{11,1... | collective-permute-start | bytes 1425416 | tf_op jit(solution)/shard_map/ppermute | solution.py:710

commit v6 on v5

--- a/solution.py
+++ b/solution.py
@@ -83,34 +83,46 @@
     return found
 
 
-def pack_x_kernel(ids, p, f, u, b, up_p, dn_p, up_m, dn_m, code, pv, fv, raw, sems):
+def fetcher(sems):
     copies = []
 
     def take(src, dst):
         copies.append(pltpu.make_async_copy(src, dst, sems.at[len(copies)]))
         copies[-1].start()
 
+    return copies, take
+
+
+def pack_x_pressure_kernel(ids, p, f, up, dn, code, pv, fv, raw, sems):
+    copies, take = fetcher(sems)
     take(ids, raw)
     take(p, pv)
     take(f, fv)
-    take(p.at[2:8], up_p.at[6:12])
-    take(p.at[0:6], dn_p.at[6:12])
-    take(f.at[3:8], up_p.at[12:17])
-    take(f.at[0:5], dn_p.at[12:17])
-    for a in range(3):
-        take(u.at[a, 5:8], up_m.at[3 * a : 3 * a + 3])
-        take(u.at[a, 0:4], dn_m.at[4 * a : 4 * a + 4])
-        take(b.at[a, 6:8], up_m.at[9 + 2 * a : 11 + 2 * a])
-        take(b.at[a, 0:3], dn_m.at[12 + 3 * a : 15 + 3 * a])
+    take(p.at[2:8], up.at[6:12])
+    take(p.at[0:6], dn.at[6:12])
+    take(f.at[3:8], up.at[12:17])
+    take(f.at[0:5], dn.at[12:17])
     copies[0].wait()
     for x in range(NX):
         c = (raw[x] + 1).astype(F32)
         code[x] = c
         if x >= 2:
-            up_p[x - 2] = c
+            up[x - 2] = c
         if x < 6:
-            dn_p[x] = c
+            dn[x] = c
     for copy in copies[1:]:
+        copy.wait()
+
+
+def pack_x_mech_kernel(u, b, after, up, dn, sems):
+    del after
+    copies, take = fetcher(sems)
+    for a in range(3):
+        take(u.at[a, 5:8], up.at[3 * a : 3 * a + 3])
+        take(u.at[a, 0:4], dn.at[4 * a : 4 * a + 4])
+        take(b.at[a, 6:8], up.at[9 + 2 * a : 11 + 2 * a])
+        take(b.at[a, 0:3], dn.at[12 + 3 * a : 15 + 3 * a])
+    for copy in copies:
         copy.wait()
 
 
@@ -718,13 +730,22 @@
     gx, gy = lax.axis_index("gx"), lax.axis_index("gy")
     flags = jnp.stack([gx > 0, gx < gx_size - 1, gy > 0, gy < gy_size - 1]).astype(F32)
     wide, mech = (YE, NZ), (YM, NZ)
-    up_p, dn_p, up_m, dn_m, own_code, own_p, own_f = call(
-        pack_x_kernel,
-        "pack_x",
-        [pltpu.with_memory_space_constraint(v, pltpu.HBM) for v in (ids, p, f, u, b)],
-        [(17, NY, NZ), (17, NY, NZ), (15, NY, NZ), (21, NY, NZ)] + [(NX, NY, NZ)] * 3,
-        [pltpu.VMEM((NX, NY, NZ), jnp.int32), pltpu.SemaphoreType.DMA((19,))],
-        [HB] * 5,
+    in_hbm = lambda v: pltpu.with_memory_space_constraint(v, pltpu.HBM)
+    up_p, dn_p, own_code, own_p, own_f = call(
+        pack_x_pressure_kernel,
+        "pack_xp",
+        [in_hbm(v) for v in (ids, p, f)],
+        [(17, NY, NZ)] * 2 + [(NX, NY, NZ)] * 3,
+        [pltpu.VMEM((NX, NY, NZ), jnp.int32), pltpu.SemaphoreType.DMA((7,))],
+        [HB] * 3,
+    )
+    up_m, dn_m = call(
+        pack_x_mech_kernel,
+        "pack_xm",
+        (in_hbm(u), in_hbm(b), own_code),
+        [(15, NY, NZ), (21, NY, NZ)],
+        [pltpu.SemaphoreType.DMA((12,))],
+        [HB, HB, pl.BlockSpec(memory_space=pl.ANY)],
     )
     low_p, high_p = neighbours("gx", gx_size, up_p, dn_p)
     low_m, high_m = neighbours("gx", gx_size, up_m, dn_m)

time: 133 us -> 133 us (level)
    pallas_call x10 -> x11, Pallas kernels: 51.8 us -> 52.8 us  [call(): pl.pallas_call(kernel, name=name, out_shape=[jax.ShapeDtypeStruct(o, F32)...]
  transfers between devices with their start and end apart: 12 -> 12, of which waited for: 7 -> 7; matrix products, arithmetic and copies ran while one was open for 0% -> 0% of each run, Pallas kernels for 7% -> 8%
where the time goes in v6:
time: 133 us
  Pallas kernels  52.8 us (40%)
  blocking collectives  37.1 us (28%)
  waiting for transfers between devices  21.4 us (16%)
  starting transfers between devices  20.9 us (16%)
    pallas_call x11, Pallas kernels, call(): pl.pallas_call(kernel, name=name, out_shape=[jax.ShapeDtypeStruct(o, F32)...  52.8 us
    all_to_all x2, blocking collectives, gather_rows(): return lax.all_to_all(part, ('gx', 'gy'), 0, 0, tiled=True)  37.1 us
    ppermute x6, waiting for transfers between devices, neighbours(): lax.ppermute(up, axis, ring)  17.3 us
    ppermute x6, starting transfers between devices, neighbours(): lax.ppermute(dn, axis, [(b, a) for a, b in ring])  10.8 us
    ppermute x6, starting transfers between devices, neighbours(): lax.ppermute(up, axis, ring)  10.1 us
    ppermute x6, waiting for transfers between devices, neighbours(): lax.ppermute(dn, axis, [(b, a) for a, b in ring])  4.1 us
  transfers between devices with their start and end apart: 12, of which 7 were waited for; matrix products, arithmetic and copies ran while one was open for 0% of the time, Pallas kernels for 8%

profile of v6, /device:TPU:1, one launch (start us, length us, event | category | flops | bytes accessed | tf_op | source)
XLA Modules:
  0.0 133.0 jit_solution(5965628205064924068)
XLA Ops:
  0.6 0.0 copy-start
  0.6 0.0 copy-start.1
  0.7 1.3 pack_xp.1
  2.0 2.1 %collective-permute-start = (f32[17,16,256]{2,1,0:T(8,128)S(1)}, f32[17,16,256]{2,1,0:T(8,128)S(1)}, u32[]{:S(2)}, u32[]{:S(2)}) collective-permute-start(f32[17,16,256]{2,1,0:T(8,128)S(1)} %get-tuple-element.39), channel_id=1, source_target_pairs={{0,8},{8,16},{16,24},{24,32},{32,40},{40,48},{48,56},{56,64},{64,7... | collective-permute-start | bytes 835592 | tf_op jit(solution)/shard_map/ppermute | solution.py:722
  4.1 4.8 %collective-permute-start.1 = (f32[17,16,256]{2,1,0:T(8,128)S(1)}, f32[17,16,256]{2,1,0:T(8,128)S(1)}, u32[]{:S(2)}, u32[]{:S(2)}) collective-permute-start(f32[17,16,256]{2,1,0:T(8,128)S(1)} %get-tuple-element.40), channel_id=1, source_target_pairs={{8,0},{16,8},{24,16},{32,24},{40,32},{48,40},{56,48},{64,56},{72,6... | collective-permute-start | bytes 835592 | tf_op jit(solution)/shard_map/ppermute | solution.py:722
  8.9 1.2 pack_xm.1
  10.1 1.5 %collective-permute-start.5 = (f32[21,16,256]{2,1,0:T(8,128)S(1)}, f32[21,16,256]{2,1,0:T(8,128)S(1)}, u32[]{:S(2)}, u32[]{:S(2)}) collective-permute-start(f32[21,16,256]{2,1,0:T(8,128)S(1)} %get-tuple-element.49), channel_id=1, source_target_pairs={{8,0},{16,8},{24,16},{32,24},{40,32},{48,40},{56,48},{64,56},{72,6... | collective-permute-start | bytes 1032200 | tf_op jit(solution)/shard_map/ppermute | solution.py:722
  11.5 0.1 collective-permute-start.4
  11.6 3.6 %collective-permute-done.low = f32[17,16,256]{2,1,0:T(8,128)S(1)} collective-permute-done((f32[17,16,256]{2,1,0:T(8,128)S(1)}, f32[17,16,256]{2,1,0:T(8,128)S(1)}, u32[]{:S(2)}, u32[]{:S(2)}) %collective-permute-start) | collective-permute-done | bytes 278560 | tf_op jit(solution)/shard_map/ppermute | solution.py:722
  15.2 1.0 pack_yp.1
  16.2 2.9 %collective-permute-start.2 = (f32[336,256]{1,0:T(8,128)}, f32[336,256]{1,0:T(8,128)S(1)}, u32[]{:S(2)}, u32[]{:S(2)}) collective-permute-start(f32[336,256]{1,0:T(8,128)} %get-tuple-element.41), channel_id=1, source_target_pairs={{0,1},{1,2},{2,3},{3,4},{4,5},{5,6},{6,7},{7,0},{8,9},{9,10},{10,1... | collective-permute-start | bytes 1032200 | tf_op jit(solution)/shard_map/ppermute | solution.py:722
  19.1 1.8 %collective-permute-done.4.low = f32[15,16,256]{2,1,0:T(8,128)S(1)} collective-permute-done((f32[15,16,256]{2,1,0:T(8,128)S(1)}, f32[15,16,256]{2,1,0:T(8,128)S(1)}, u32[]{:S(2)}, u32[]{:S(2)}) %collective-permute-start.4) | collective-permute-done | bytes 245792 | tf_op jit(solution)/shard_map/ppermute | solution.py:722
  20.9 0.8 collective-permute-done.5.high
  21.6 1.0 pack_ym.1
  22.6 2.8 %collective-permute-start.6 = (f32[304,256]{1,0:T(8,128)}, f32[304,256]{1,0:T(8,128)S(1)}, u32[]{:S(2)}, u32[]{:S(2)}) collective-permute-start(f32[304,256]{1,0:T(8,128)} %get-tuple-element.50), channel_id=1, source_target_pairs={{0,1},{1,2},{2,3},{3,4},{4,5},{5,6},{6,7},{7,0},{8,9},{9,10},{10,1... | collective-permute-start | bytes 933896 | tf_op jit(solution)/shard_map/ppermute | solution.py:722
  25.4 0.1 add_convert_fusion.flags
  25.5 0.5 collective-permute-done.3.yh
  26.1 7.7 %pressure_first.1 = (f32[20,32,256]{2,1,0:T(8,128)S(1)}, f32[20,32,256]{2,1,0:T(8,128)S(1)}, f32[8,20,32,256]{3,2,1,0:T(8,128)S(1)}, f32[3,20,32,256]{3,2,1,0:T(8,128)S(1)}, f32[8,128]{1,0:T(8,128)S(1)}) custom-call(f32[4]{0:T(128)S(1)} %add_convert_fusion.flags, f32[5,8]{1,0:T(8,128)S(1)} %copy-done.2, f32[8,16,256]{2,1,0:T(8,128)S(1)} %get-tuple-element.36.ids.after, ...), custom_call_target="tpu_custom_call" | custom-call | flops 2000000000 | tf_op jit(solution)/shard_map/pressure_first/pallas_call | solution.py:708
  33.8 18.1 %mech_first.1 = (f32[3,15,24,256]{3,2,1,0:T(8,128)S(1)}, f32[3,15,24,256]{3,2,1,0:T(8,128)S(1)}, f32[9,15,24,256]{3,2,1,0:T(8,128)S(1)}, f32[36,10,24,256]{3,2,1,0:T(8,128)S(1)}, f32[128,128]{1,0:T(8,128)S(1)}) custom-call(f32[4]{0:T(128)S(1)} %add_convert_fusion.flags, f32[5,8]{1,0:T(8,128)S(1)} %copy-done.2, f32[8,128]{1,0:T(8,128)S(1)} %get-tuple-element.44.part_p, ...), custom_call_target="tpu_custom_call" | custom-call | flops 200000000 | tf_op jit(solution)/shard_map/mech_first/pallas_call | solution.py:708
  51.9 18.7 %all_to_all.22 = f32[128,1,128]{2,1,0:T(1,128)S(1)} all-to-all(f32[128,1,128]{2,1,0:T(1,128)S(1)} %bitcast.14), channel_id=1, replica_groups=mesh['gx'=16,'gy'=8] {'gx','gy'}, dimensions={0} | all-to-all | bytes 131072 | tf_op jit(solution)/shard_map/all_to_all | solution.py:726
  70.6 1.5 %change.1 = (f32[3,9,24,256]{3,2,1,0:T(8,128)S(1)}, f32[14,32,256]{2,1,0:T(8,128)S(1)}, f32[3,8,16,256]{3,2,1,0:T(8,128)S(1)}, f32[18,16,256]{2,1,0:T(8,128)S(1)}, f32[18,16,256]{2,1,0:T(8,128)S(1)}) custom-call(f32[128,128]{1,0:T(8,128)S(1)} %bitcast.12, f32[3,20,32,256]{3,2,1,0:T(8,128)S(1)} %get-tuple-element.47.t, ...), custom_call_target="tpu_custom_call" | custom-call | tf_op jit(solution)/shard_map/change/pallas_call | solution.py:708
  72.1 0.4 collective-permute-start.8
  72.5 4.5 %collective-permute-start.9 = (f32[18,16,256]{2,1,0:T(8,128)S(1)}, f32[18,16,256]{2,1,0:T(8,128)S(1)}, u32[]{:S(2)}, u32[]{:S(2)}) collective-permute-start(f32[18,16,256]{2,1,0:T(8,128)S(1)} %get-tuple-element.58), channel_id=1, source_target_pairs={{8,0},{16,8},{24,16},{32,24},{40,32},{48,40},{56,48},{64,56},{72,6... | collective-permute-start | bytes 884744 | tf_op jit(solution)/shard_map/ppermute | solution.py:722
  76.9 6.3 %collective-permute-done.8.low = f32[18,16,256]{2,1,0:T(8,128)S(1)} collective-permute-done((f32[18,16,256]{2,1,0:T(8,128)S(1)}, f32[18,16,256]{2,1,0:T(8,128)S(1)}, u32[]{:S(2)}, u32[]{:S(2)}) %collective-permute-start.8) | collective-permute-done | bytes 294944 | tf_op jit(solution)/shard_map/ppermute | solution.py:722
  83.3 0.2 pack_change.1
  83.5 1.9 %collective-permute-start.10 = (f32[464,256]{1,0:T(8,128)S(1)}, f32[464,256]{1,0:T(8,128)S(1)}, u32[]{:S(2)}, u32[]{:S(2)}) collective-permute-start(f32[464,256]{1,0:T(8,128)S(1)} %get-tuple-element.59), channel_id=1, source_target_pairs={{0,1},{1,2},{2,3},{3,4},{4,5},{5,6},{6,7},{7,0},{8,9},{9,10},{10,1... | collective-permute-start | bytes 1425416 | tf_op jit(solution)/shard_map/ppermute | solution.py:722
  85.4 5.6 %collective-permute-done.10.yl = f32[464,256]{1,0:T(8,128)S(1)} collective-permute-done((f32[464,256]{1,0:T(8,128)S(1)}, f32[464,256]{1,0:T(8,128)S(1)}, u32[]{:S(2)}, u32[]{:S(2)}) %collective-permute-start.10) | collective-permute-done | bytes 475168 | tf_op jit(solution)/shard_map/ppermute | solution.py:722
  90.9 2.8 %collective-permute-done.11.yh = f32[464,256]{1,0:T(8,128)S(1)} collective-permute-done((f32[464,256]{1,0:T(8,128)S(1)}, f32[464,256]{1,0:T(8,128)S(1)}, u32[]{:S(2)}, u32[]{:S(2)}) %collective-permute-start.11) | collective-permute-done | bytes 475168 | tf_op jit(solution)/shard_map/ppermute | solution.py:722
  93.7 4.2 %pressure_next.1 = (f32[20,32,256]{2,1,0:T(8,128)S(1)}, f32[3,15,24,256]{3,2,1,0:T(8,128)S(1)}, f32[3,20,32,256]{3,2,1,0:T(8,128)S(1)}, f32[8,128]{1,0:T(8,128)S(1)}) custom-call(f32[4]{0:T(128)S(1)} %add_convert_fusion.flags, f32[8,20,32,256]{3,2,1,0:T(8,128)S(1)} %get-tuple-element.43.coef, f32[14,32,256]{2,1,0:T(8,128)S(1)} %get-tuple-element.54.p, ...), custom_call_target="tpu_custom_call" | custom-call | flops 200000000 | tf_op jit(solution)/shard_map/pressure_next/pallas_call | solution.py:708
  97.9 14.9 %mech_next.1 = (f32[36,10,24,256]{3,2,1,0:T(8,128)S(1)}, f32[128,128]{1,0:T(8,128)S(1)}) custom-call(f32[8,128]{1,0:T(8,128)S(1)} %get-tuple-element.61.part_p, f32[20,32,256]{2,1,0:T(8,128)S(1)} %get-tuple-element.62.pe.p, f32[8,20,32,256]{3,2,1,0:T(8,128)S(1)} %get-tuple-element.43.coef, f32[3,20,32,256]{3,2,1,0:T(8,128)S(1)} %get-tuple-element.63.t, ...), custom_call_target="tpu_custom_call" | custom-call | flops 200000000 | tf_op jit(solution)/shard_map/mech_next/pallas_call | solution.py:708
  112.8 18.4 %all_to_all.23 = f32[128,1,128]{2,1,0:T(1,128)S(1)} all-to-all(f32[128,1,128]{2,1,0:T(1,128)S(1)} %bitcast.15), channel_id=1, replica_groups=mesh['gx'=16,'gy'=8] {'gx','gy'}, dimensions={0} | all-to-all | bytes 131072 | tf_op jit(solution)/shard_map/all_to_all | solution.py:726
  131.3 1.7 %finish.1 = (f32[3,8,16,256]{3,2,1,0:T(8,128)}, f32[8,16,256]{2,1,0:T(8,128)}) custom-call(f32[128,128]{1,0:T(8,128)S(1)} %bitcast.13, f32[3,20,32,256]{3,2,1,0:T(8,128)S(1)} %get-tuple-element.63.t, f32[20,32,256]{2,1,0:T(8,128)S(1)} %get-tuple-element.62.pe.p, f32[36,10,24,256]{3,2,1,0:T(8,128)S(1)} %get-tuple-element.68.kept, ...), custom_call_target="tpu_custom_call" | custom-call | tf_op jit(solution)/shard_map/finish/pallas_call | solution.py:708
  (12 shorter events, 0.0 us)
Async XLA Ops:
  0.6 21.0 %copy-start = (f32[3,8,16,256]{3,2,1,0:T(8,128)S(1)}, f32[3,8,16,256]{3,2,1,0:T(8,128)}, u32[]{:S(2)}) copy-start(f32[3,8,16,256]{3,2,1,0:T(8,128)} %u.7) | copy-start | bytes 1179652
  0.6 21.0 %copy-start.1 = (f32[3,8,16,256]{3,2,1,0:T(8,128)S(1)}, f32[3,8,16,256]{3,2,1,0:T(8,128)}, u32[]{:S(2)}) copy-start(f32[3,8,16,256]{3,2,1,0:T(8,128)} %b.5) | copy-start | bytes 1179652
  0.7 25.4 %copy-start.2 = (f32[5,8]{1,0:T(8,128)S(1)}, f32[5,8]{1,0:T(8,128)}, u32[]{:S(2)}) copy-start(f32[5,8]{1,0:T(8,128)} %mats.3) | copy-start | bytes 484
  2.0 13.2 %collective-permute-start = (f32[17,16,256]{2,1,0:T(8,128)S(1)}, f32[17,16,256]{2,1,0:T(8,128)S(1)}, u32[]{:S(2)}, u32[]{:S(2)}) collective-permute-start(f32[17,16,256]{2,1,0:T(8,128)S(1)} %get-tuple-element.39), channel_id=1, source_target_pairs={{0,8},{8,16},{16,24},{24,32},{32,40},{40,48},{48,56},{56,64},{64,7... | collective-permute-start | bytes 835592 | tf_op jit(solution)/shard_map/ppermute | solution.py:722
  4.1 11.1 %collective-permute-start.1 = (f32[17,16,256]{2,1,0:T(8,128)S(1)}, f32[17,16,256]{2,1,0:T(8,128)S(1)}, u32[]{:S(2)}, u32[]{:S(2)}) collective-permute-start(f32[17,16,256]{2,1,0:T(8,128)S(1)} %get-tuple-element.40), channel_id=1, source_target_pairs={{8,0},{16,8},{24,16},{32,24},{40,32},{48,40},{56,48},{64,56},{72,6... | collective-permute-start | bytes 835592 | tf_op jit(solution)/shard_map/ppermute | solution.py:722
  10.1 11.5 %collective-permute-start.5 = (f32[21,16,256]{2,1,0:T(8,128)S(1)}, f32[21,16,256]{2,1,0:T(8,128)S(1)}, u32[]{:S(2)}, u32[]{:S(2)}) collective-permute-start(f32[21,16,256]{2,1,0:T(8,128)S(1)} %get-tuple-element.49), channel_id=1, source_target_pairs={{8,0},{16,8},{24,16},{32,24},{40,32},{48,40},{56,48},{64,56},{72,6... | collective-permute-start | bytes 1032200 | tf_op jit(solution)/shard_map/ppermute | solution.py:722
  11.5 9.3 %collective-permute-start.4 = (f32[15,16,256]{2,1,0:T(8,128)S(1)}, f32[15,16,256]{2,1,0:T(8,128)S(1)}, u32[]{:S(2)}, u32[]{:S(2)}) collective-permute-start(f32[15,16,256]{2,1,0:T(8,128)S(1)} %get-tuple-element.48), channel_id=1, source_target_pairs={{0,8},{8,16},{16,24},{24,32},{32,40},{40,48},{48,56},{56,64},{64,7... | collective-permute-start | bytes 737288 | tf_op jit(solution)/shard_map/ppermute | solution.py:722
  16.2 9.3 %collective-permute-start.2 = (f32[336,256]{1,0:T(8,128)}, f32[336,256]{1,0:T(8,128)S(1)}, u32[]{:S(2)}, u32[]{:S(2)}) collective-permute-start(f32[336,256]{1,0:T(8,128)} %get-tuple-element.41), channel_id=1, source_target_pairs={{0,1},{1,2},{2,3},{3,4},{4,5},{5,6},{6,7},{7,0},{8,9},{9,10},{10,1... | collective-permute-start | bytes 1032200 | tf_op jit(solution)/shard_map/ppermute | solution.py:722
  19.1 7.0 %collective-permute-start.3 = (f32[336,256]{1,0:T(8,128)}, f32[336,256]{1,0:T(8,128)}, u32[]{:S(2)}, u32[]{:S(2)}) collective-permute-start(f32[336,256]{1,0:T(8,128)} %get-tuple-element.42), channel_id=1, source_target_pairs={{1,0},{2,1},{3,2},{4,3},{5,4},{6,5},{7,6},{0,7},{9,8},{10,9},{11,1... | collective-permute-start | bytes 1032200 | tf_op jit(solution)/shard_map/ppermute | solution.py:722
  22.6 11.1 %collective-permute-start.6 = (f32[304,256]{1,0:T(8,128)}, f32[304,256]{1,0:T(8,128)S(1)}, u32[]{:S(2)}, u32[]{:S(2)}) collective-permute-start(f32[304,256]{1,0:T(8,128)} %get-tuple-element.50), channel_id=1, source_target_pairs={{0,1},{1,2},{2,3},{3,4},{4,5},{5,6},{6,7},{7,0},{8,9},{9,10},{10,1... | collective-permute-start | bytes 933896 | tf_op jit(solution)/shard_map/ppermute | solution.py:722
  25.4 8.4 %collective-permute-start.7 = (f32[304,256]{1,0:T(8,128)}, f32[304,256]{1,0:T(8,128)S(1)}, u32[]{:S(2)}, u32[]{:S(2)}) collective-permute-start(f32[304,256]{1,0:T(8,128)} %get-tuple-element.51), channel_id=1, source_target_pairs={{1,0},{2,1},{3,2},{4,3},{5,4},{6,5},{7,6},{0,7},{9,8},{10,9},{11,1... | collective-permute-start | bytes 933896 | tf_op jit(solution)/shard_map/ppermute | solution.py:722
  72.1 11.2 %collective-permute-start.8 = (f32[18,16,256]{2,1,0:T(8,128)S(1)}, f32[18,16,256]{2,1,0:T(8,128)S(1)}, u32[]{:S(2)}, u32[]{:S(2)}) collective-permute-start(f32[18,16,256]{2,1,0:T(8,128)S(1)} %get-tuple-element.57), channel_id=1, source_target_pairs={{0,8},{8,16},{16,24},{24,32},{32,40},{40,48},{48,56},{56,64},{64,7... | collective-permute-start | bytes 884744 | tf_op jit(solution)/shard_map/ppermute | solution.py:722
  72.5 10.8 %collective-permute-start.9 = (f32[18,16,256]{2,1,0:T(8,128)S(1)}, f32[18,16,256]{2,1,0:T(8,128)S(1)}, u32[]{:S(2)}, u32[]{:S(2)}) collective-permute-start(f32[18,16,256]{2,1,0:T(8,128)S(1)} %get-tuple-element.58), channel_id=1, source_target_pairs={{8,0},{16,8},{24,16},{32,24},{40,32},{48,40},{56,48},{64,56},{72,6... | collective-permute-start | bytes 884744 | tf_op jit(solution)/shard_map/ppermute | solution.py:722
  83.5 7.5 %collective-permute-start.10 = (f32[464,256]{1,0:T(8,128)S(1)}, f32[464,256]{1,0:T(8,128)S(1)}, u32[]{:S(2)}, u32[]{:S(2)}) collective-permute-start(f32[464,256]{1,0:T(8,128)S(1)} %get-tuple-element.59), channel_id=1, source_target_pairs={{0,1},{1,2},{2,3},{3,4},{4,5},{5,6},{6,7},{7,0},{8,9},{9,10},{10,1... | collective-permute-start | bytes 1425416 | tf_op jit(solution)/shard_map/ppermute | solution.py:722
  85.3 8.4 %collective-permute-start.11 = (f32[464,256]{1,0:T(8,128)S(1)}, f32[464,256]{1,0:T(8,128)S(1)}, u32[]{:S(2)}, u32[]{:S(2)}) collective-permute-start(f32[464,256]{1,0:T(8,128)S(1)} %get-tuple-element.60), channel_id=1, source_target_pairs={{1,0},{2,1},{3,2},{4,3},{5,4},{6,5},{7,6},{0,7},{9,8},{10,9},{11,1... | collective-permute-start | bytes 1425416 | tf_op jit(solution)/shard_map/ppermute | solution.py:722
